TPU v7x, 512 devices: a whole 4x8x8 slice. The times are simulated.
512 devices in a mesh: dp: 64 (over y, z), aug: 8 (over x, core).
Axes of the slice: x: 4, y: 8, z: 8, core: 2. Of those that a mesh axis runs over, the one named last changes fastest.
Arguments:
- images: bfloat16 [8, 64, 197, 768], P('aug', 'dp'), may hold values from -6 to 6
- out_grads: bfloat16 [8, 64, 197, 768], P('aug', 'dp'), may hold values from -8 to 8
- up_weight_t: bfloat16 [3072, 768], P(('dp', 'aug')), may hold values from -0.21875 to 0.21875
- down_weight_t: bfloat16 [3072, 768], P(('dp', 'aug')), may hold values from -0.21875 to 0.21875
- left_up: bfloat16 [3072, 128], P(('dp', 'aug')), may hold values from -0.109375 to 0.109375
- right_up: bfloat16 [768, 128], replicated, may hold values from -0.21875 to 0.21875
- left_down: bfloat16 [768, 128], replicated, may hold values from -0.21875 to 0.21875
- right_down: bfloat16 [3072, 128], P(('dp', 'aug')), may hold values from -0.109375 to 0.109375
- noise: float32 [2, 128, 128], P(None, 'aug'), may hold values from -6 to 6
Outputs:
- update: float32 [2, 128, 128], P(None, 'aug')
- clip_scales: float32 [64], P('dp')
All inputs are finite; a program needn't handle non-finite values.
Results may differ from a plain program's by a relative error of at most 0.0032.
Values may be sent and summed in bfloat16 or wider, within the bound.
No kernel may reach another device: no remote copies, remote signals or barrier semaphores. Data moves between devices by JAX's collectives and lax.ppermute only.
A program may use at most 64 MiB of HBM per device.

v0:
```python
import math

import jax
import jax.numpy as jnp
from jax import lax
from jax.sharding import Mesh
from jax.sharding import PartitionSpec as P

DP = ("dp_0", "dp_1")
DP_AUG = ("dp_0", "dp_1", "aug")


gelu_coef = 0.7978845608028654
clip_frac = 0.3
noise_mult = 0.05


def side_by_side(arrays, axis, dim, along):
    ends, at = ([], 0)
    for a in arrays[:-1]:
        at += a.shape[along]
        ends.append(at)
    both = jnp.concatenate(arrays, axis=along)
    return tuple(jnp.split(lax.all_gather(both, axis, axis=dim, tiled=True), ends, axis=along))


def copy_for_each(shard, axis):
    size = lax.axis_size(axis)
    return lax.all_to_all(
        jnp.broadcast_to(shard[None], (size, *shard.shape)), axis, 0, 0, tiled=True
    )


def of_everyone(shard, axis):
    return copy_for_each(shard, axis).sum(axis=0)


def by_axis(shard, axes):
    for axis in axes:
        shard = lax.psum(shard, axis)
    return shard


def gelu_pair(hidden):
    inner = gelu_coef * (hidden + 0.044715 * hidden * hidden * hidden)
    tangent = jnp.tanh(inner)
    value = 0.5 * hidden * (1.0 + tangent)
    slope = 0.5 * (1.0 + tangent) + 0.5 * hidden * (1.0 - tangent * tangent) * gelu_coef * (
        1.0 + 3.0 * 0.044715 * hidden * hidden
    )
    return (value, slope)


def contract_last(left, right):
    return lax.dot_general(
        left, right, (((1,), (1,)), ((), ())), preferred_element_type=jnp.float32
    )


def local(
    images, out_grads, up_weight_t, down_weight_t, left_up, right_up, left_down, right_down, noise
):
    local_augs = images.shape[0]
    local_images = images.shape[1]
    tokens = images.shape[2]
    width = images.shape[3]
    rank = right_up.shape[1]
    token_rows = images.reshape(-1, width)
    grad_rows = out_grads.reshape(-1, width)
    grouped = side_by_side((up_weight_t, down_weight_t, left_up, right_down), "aug", 0, 1)
    up_piece, down_piece, left_piece, right_piece = side_by_side(
        (grouped[0], grouped[1], grouped[2], grouped[3]), DP, 0, 1
    )
    hidden = contract_last(token_rows, up_piece)
    activation, slope = gelu_pair(hidden)
    back = contract_last(grad_rows, down_piece)
    hidden_grad = (back * slope).astype(jnp.bfloat16)
    first = jnp.dot(hidden_grad, left_piece, preferred_element_type=jnp.float32)
    second = jnp.dot(
        activation.astype(jnp.bfloat16), right_piece, preferred_element_type=jnp.float32
    )
    up_total = first
    down_total = second
    v_up = up_total.astype(jnp.bfloat16)
    u_down = down_total.astype(jnp.bfloat16)
    u_up = jnp.dot(token_rows, right_up, preferred_element_type=jnp.float32).astype(jnp.bfloat16)
    v_down = jnp.dot(grad_rows, left_down, preferred_element_type=jnp.float32).astype(jnp.bfloat16)
    shape = (local_augs, local_images, tokens, rank)
    first = jnp.einsum(
        "aitr,aits->irs",
        v_up.reshape(shape),
        u_up.reshape(shape),
        preferred_element_type=jnp.float32,
    )
    second = jnp.einsum(
        "aitr,aits->irs",
        v_down.reshape(shape),
        u_down.reshape(shape),
        preferred_element_type=jnp.float32,
    )
    local_terms = jnp.stack([first, second], axis=1)
    all_augs = local_augs * lax.axis_size("aug")
    share_rows = rank // lax.axis_size("aug")
    lower_row = lax.axis_index("aug") * share_rows
    summed_terms = of_everyone(local_terms, "aug")
    aug_mean = summed_terms / all_augs
    squares = jnp.sum(aug_mean * aug_mean, axis=(1, 2, 3))
    my_rows = lax.dynamic_slice_in_dim(aug_mean, lower_row, share_rows, 2)
    norms = jnp.sqrt(squares + 1e-06)
    clip_norm = clip_frac * rank * math.sqrt(tokens / all_augs)
    clip_scales = jnp.minimum(1.0, clip_norm / norms)
    clipped_rows = jnp.sum(clip_scales[:, None, None, None] * my_rows, axis=0)
    summed_rows = by_axis(clipped_rows, DP)
    all_images = local_images * lax.axis_size(DP)
    update = (summed_rows + noise_mult * clip_norm * noise) / jnp.sqrt(jnp.float32(all_images))
    return (update, clip_scales)


def solution(mesh):
    torus = Mesh(mesh.devices.reshape(8, 8, mesh.shape["aug"]), ("dp_0", "dp_1", "aug"))
    placed = (
        P("aug", DP, None, None),
        P("aug", DP, None, None),
        P(DP_AUG, None),
        P(DP_AUG, None),
        P(DP_AUG, None),
        P(),
        P(),
        P(DP_AUG, None),
        P(None, "aug", None),
    )
    return jax.shard_map(
        local, mesh=torus, in_specs=placed, out_specs=(P(None, "aug", None), P(DP)), check_vma=False
    )
```

profile of v0, /device:TPU:2, one launch (start us, length us, event | category | flops | bytes accessed | tf_op | source)
XLA Modules:
  0.0 238.5 jit_solution(18309758157067267480)
XLA Ops:
  7.2 0.0 copy-start
  7.2 0.0 all-gather.3.cloned.1.call-start
  7.2 0.8 maximum_bitcast_fusion.1
  8.0 15.5 %all-gather = bf16[8,6,1792]{2,1,0:T(8,128)(2,1)S(1)} all-gather(bf16[1,6,1792]{2,1,0:T(8,128)(2,1)S(1)} %maximum_bitcast_fusion.1), channel_id=1, replica_groups=mesh['dp_0'=8,'dp_1'=8,'aug'=8] {'aug'}, dimensions={0}, use_global_device_ids=true | all-gather | bytes 193536 | tf_op jit(solution)/shard_map/all_gather | solution.py:24
  23.5 0.7 reshape.63
  24.3 0.0 all-gather.3.cloned.1.call-update
  24.3 0.0 copy-start.1
  24.3 113.4 %all-gather.3.cloned.1.call-done = bf16[3072,1792]{1,0:T(8,128)(2,1)} async-done(((bf16[48,1792]{1,0:T(8,128)(2,1)}), bf16[3072,1792]{1,0:T(8,128)(2,1)}) %all-gather.3.cloned.1.call-update) | async-done | bytes 11010064 | tf_op jit(solution)/shard_map/all_gather | solution.py:24
  137.7 0.0 copy-done
  137.7 4.0 %fusion.7 = f32[197,3072]{1,0:T(8,128)S(1)} fusion(bf16[3072,1792]{1,0:T(8,128)(2,1)} %all-gather.3.cloned.1.call-done, bf16[1,1,197,768]{3,2,1,0:T(8,128)(2,1)S(1)} %copy-done), kind=kOutput, calls=%fused_computation.5 | convolution fusion | flops 929562624 | bytes 7441920 | tf_op jit(solution)/shard_map/dot_general | solution.py:55
  141.7 0.0 copy-done.1
  141.7 0.0 copy-start.2
  141.7 5.3 %fusion.30 = bf16[197,128]{1,0:T(8,128)(2,1)S(1)} fusion(bf16[3072,1792]{1,0:T(8,128)(2,1)} %all-gather.3.cloned.1.call-done, f32[197,3072]{1,0:T(8,128)S(1)} %fusion.7, bf16[1,1,197,768]{3,2,1,0:T(8,128)(2,1)S(1)} %copy-done.1), kind=kOutput, calls=%fused_computation.23 | convolution fusion | flops 1096013440 | bytes 8278784 | tf_op jit(solution)/shard_map/dot_general | solution.py:78
  147.0 0.0 copy-done.2
  147.0 0.4 convolution_bitcast_fusion.1
  147.4 0.0 copy-start.3
  147.4 2.2 fusion.33
  149.6 0.0 copy-done.3
  149.6 0.5 convolution_bitcast_fusion
  150.1 0.0 copy-start.4
  150.1 1.1 broadcast_in_dim.10
  151.2 4.8 %all-to-all-start = ((f32[8,1,2,128,128]{4,3,2,1,0:T(8,128)}), f32[8,1,2,128,128]{4,3,2,1,0:T(8,128)S(1)}, u32[]{:S(2)}, u32[]{:S(2)}) async-start(f32[8,1,2,128,128]{4,3,2,1,0:T(8,128)} %broadcast_in_dim.10), calls=%async_computation | async-start | bytes 2097152 | tf_op jit(solution)/shard_map/all_to_all | solution.py:29
  156.0 14.5 %all-to-all-done = f32[8,1,2,128,128]{4,3,2,1,0:T(8,128)S(1)} async-done(((f32[8,1,2,128,128]{4,3,2,1,0:T(8,128)}), f32[8,1,2,128,128]{4,3,2,1,0:T(8,128)S(1)}, u32[]{:S(2)}, u32[]{:S(2)}) %all-to-all-start) | async-done | bytes 1048608 | tf_op jit(solution)/shard_map/all_to_all | solution.py:29
  170.5 0.1 reduce_sum.16
  170.5 0.6 multiply_reduce_fusion
  171.9 29.7 %psum.14 = f32[2,16,128]{2,1,0:T(8,128)S(1)} all-reduce(f32[2,16,128]{2,1,0:T(8,128)S(1)} %dynamic-slice_multiply_fusion), channel_id=1, replica_groups=mesh['dp_0'=8,'dp_1'=8,'aug'=8] {'dp_0'}, use_global_device_ids=true, to_apply=%region_2.0 | all-reduce | flops 4096 | bytes 32768 | tf_op jit(solution)/shard_map/psum | solution.py:40
  201.6 28.3 %psum.15 = f32[2,16,128]{2,1,0:T(8,128)S(1)} all-reduce(f32[2,16,128]{2,1,0:T(8,128)S(1)} %psum.14), channel_id=1, replica_groups=mesh['dp_0'=8,'dp_1'=8,'aug'=8] {'dp_1'}, use_global_device_ids=true, to_apply=%region_3.0 | all-reduce | flops 4096 | bytes 32768 | tf_op jit(solution)/shard_map/psum | solution.py:40
  229.9 0.0 copy-done.4
  229.9 0.6 add_multiply_fusion
  (2 shorter events, 0.0 us)
Async XLA Ops:
  7.2 130.6 %copy-start = (bf16[1,1,197,768]{3,2,1,0:T(8,128)(2,1)S(1)}, bf16[1,1,197,768]{3,2,1,0:T(8,128)(2,1)}, u32[]{:S(2)}) copy-start(bf16[1,1,197,768]{3,2,1,0:T(8,128)(2,1)} %param.9) | copy-start | bytes 907780
  7.2 130.6 %all-gather.3.cloned.1.call-start = ((), (), s32[]{:S(2)}) async-start(), calls=%async_computation.1 | async-start | bytes 11182080 | tf_op jit(solution)/shard_map/all_gather | solution.py:24
  24.3 117.4 %copy-start.1 = (bf16[1,1,197,768]{3,2,1,0:T(8,128)(2,1)S(1)}, bf16[1,1,197,768]{3,2,1,0:T(8,128)(2,1)}, u32[]{:S(2)}) copy-start(bf16[1,1,197,768]{3,2,1,0:T(8,128)(2,1)} %param.10) | copy-start | bytes 907780
  141.7 5.3 %copy-start.2 = (bf16[768,128]{1,0:T(8,128)(2,1)S(1)}, bf16[768,128]{1,0:T(8,128)(2,1)}, u32[]{:S(2)}) copy-start(bf16[768,128]{1,0:T(8,128)(2,1)} %param.14) | copy-start | bytes 589828
  147.4 2.2 copy-start.3
  150.1 79.8 %copy-start.4 = (f32[2,16,128]{2,1,0:T(8,128)S(1)}, f32[2,16,128]{2,1,0:T(8,128)}, u32[]{:S(2)}) copy-start(f32[2,16,128]{2,1,0:T(8,128)} %param.17) | copy-start | bytes 49156
  151.2 19.3 %all-to-all-start = ((f32[8,1,2,128,128]{4,3,2,1,0:T(8,128)}), f32[8,1,2,128,128]{4,3,2,1,0:T(8,128)S(1)}, u32[]{:S(2)}, u32[]{:S(2)}) async-start(f32[8,1,2,128,128]{4,3,2,1,0:T(8,128)} %broadcast_in_dim.10), calls=%async_computation | async-start | bytes 2097152 | tf_op jit(solution)/shard_map/all_to_all | solution.py:29
Sparse Core Ops, SparseCore 0:
  24.4 113.2 all-gather.2
where the time goes:
time: 239 us
  waiting for transfers between devices  128 us (54%)
  blocking collectives  73.6 us (31%)
  between operations  16 us (7%)
  matrix products  12.2 us (5%)
  starting transfers between devices  4.83 us (2%)
    all_gather x1, waiting for transfers between devices, side_by_side(): lax.all_gather(both, axis, axis=dim, tiled=True)  113 us
    psum x2, blocking collectives, by_axis(): shard = lax.psum(shard, axis)  58.1 us
    all_gather x1, blocking collectives, side_by_side(): lax.all_gather(both, axis, axis=dim, tiled=True)  15.5 us
    all_to_all x1, waiting for transfers between devices, copy_for_each(): lax.all_to_all(jnp.broadcast_to(shard[None], (size, *shard.shape)), axis,...  14.5 us
    dot_general x1, matrix products, local(): first = jnp.dot(hidden_grad, left_piece, preferred_element_type=jnp.float32)  5.26 us
    all_to_all x1, starting transfers between devices, copy_for_each(): lax.all_to_all(jnp.broadcast_to(shard[None], (size, *shard.shape)), axis,...  4.79 us
  transfers between devices with their start and end apart: 2, of which 2 were waited for; matrix products, arithmetic and copies ran while one was open for 0% of the time, Pallas kernels for 0%

commit v1 on v0

v1 whole, which is shorter than its diff:
```python
import math

import jax
import jax.numpy as jnp
from jax import lax
from jax.sharding import Mesh
from jax.sharding import PartitionSpec as P

DP = ("dp_0", "dp_1")
AUG = ("x", "core")
bf16 = jnp.bfloat16
f32 = jnp.float32


gelu_coef = 0.7978845608028654
clip_frac = 0.3
noise_mult = 0.05


def copy_for_each(shard, axis):
    size = lax.axis_size(axis)
    return lax.all_to_all(
        jnp.broadcast_to(shard[None], (size, *shard.shape)), axis, 0, 0, tiled=True
    )


def of_everyone(shard, axis):
    return copy_for_each(shard, axis).astype(f32).sum(axis=0)


def gelu_pair(hidden):
    inner = gelu_coef * (hidden + 0.044715 * hidden * hidden * hidden)
    tangent = jnp.tanh(inner)
    value = 0.5 * hidden * (1.0 + tangent)
    slope = 0.5 * (1.0 + tangent) + 0.5 * hidden * (1.0 - tangent * tangent) * gelu_coef * (
        1.0 + 3.0 * 0.044715 * hidden * hidden
    )
    return (value, slope)


def contract(left, right, dims):
    return lax.dot_general(left, right, ((dims[0], dims[1]), ((), ())), preferred_element_type=f32)


def pack_weights(up, down, left, right):
    rows, width = up.shape
    flat = jnp.concatenate([left.reshape(1, width), right.reshape(1, width)], axis=1)
    both = jnp.concatenate([up, down], axis=1)
    fill = jnp.zeros((8 - rows - 1, 2 * width), bf16)
    return jnp.concatenate([both, flat, fill], axis=0)


def unpack_weights(gathered, rows, rank):
    senders, padded, twice = gathered.shape
    width = twice // 2
    picked = (rows + 1) * senders
    at = lax.broadcasted_iota(jnp.int32, (picked, senders * padded), 0)
    of = lax.broadcasted_iota(jnp.int32, (picked, senders * padded), 1)
    select = (of == (at % senders) * padded + at // senders).astype(bf16)
    both = contract(select, gathered.reshape(senders * padded, twice), ((1,), (0,))).astype(bf16)
    hidden_units = rows * senders
    up, down = both[:hidden_units, :width], both[:hidden_units, width:]
    flat = both[hidden_units:]
    left = jnp.concatenate([flat[:, r * rank : (r + 1) * rank] for r in range(rows)], axis=0)
    right = jnp.concatenate(
        [flat[:, width + r * rank : width + (r + 1) * rank] for r in range(rows)], axis=0
    )
    return up, down, left, right


def neighbour(array, shift):
    return lax.ppermute(array, "x", [(i, (i + shift) % 4) for i in range(4)])


def pad_rows(tokens):
    count, width = tokens.shape[-2:]
    return jnp.pad(tokens.reshape(count, width), ((0, -count % 8), (0, 0)))


def local(
    images, out_grads, up_weight_t, down_weight_t, left_up, right_up, left_down, right_down, noise
):
    tokens = images.shape[2]
    rank = right_up.shape[1]
    rows = up_weight_t.shape[0]
    packed = pack_weights(up_weight_t, down_weight_t, left_up, right_down)
    gathered = copy_for_each(packed, DP)
    mine = jnp.stack([pad_rows(images), pad_rows(out_grads)])
    below = neighbour(mine, 1)
    above = neighbour(mine, -1)
    far_tokens = neighbour(below[0], 1)
    far_grads = neighbour(above[1], -1)
    token_rows = jnp.concatenate([mine[0], below[0], above[0], far_tokens], axis=0)
    grad_rows = jnp.concatenate([mine[1], below[1], above[1], far_grads], axis=0)
    u_up = contract(token_rows, right_up, ((1,), (0,))).astype(bf16)
    v_down = contract(grad_rows, left_down, ((1,), (0,))).astype(bf16)
    partners = lax.ppermute(gathered, "core", [(0, 1), (1, 0)])
    v_up, u_down = 0.0, 0.0
    for part in (gathered, partners):
        up, down, left, right = unpack_weights(part, rows, rank)
        hidden = contract(token_rows, up, ((1,), (1,)))
        activation, slope = gelu_pair(hidden)
        back = contract(grad_rows, down, ((1,), (1,)))
        hidden_grad = (back * slope).astype(bf16)
        v_up += contract(hidden_grad, left, ((1,), (0,)))
        u_down += contract(activation.astype(bf16), right, ((1,), (0,)))
    first = contract(v_up.astype(bf16), u_up, ((0,), (0,)))
    second = contract(v_down, u_down.astype(bf16), ((0,), (0,)))
    terms = jnp.stack([first, second], axis=0).astype(bf16)
    all_augs = lax.axis_size(AUG)
    share_rows = rank // all_augs
    lower_row = lax.axis_index(AUG) * share_rows
    aug_mean = of_everyone(terms, AUG) / all_augs
    squares = jnp.sum(aug_mean * aug_mean)
    my_rows = lax.dynamic_slice_in_dim(aug_mean, lower_row, share_rows, 1)
    norm = jnp.sqrt(squares + 1e-06)
    clip_norm = clip_frac * rank * math.sqrt(tokens / all_augs)
    clip_scale = jnp.minimum(1.0, clip_norm / norm)
    summed_rows = of_everyone(of_everyone(clip_scale * my_rows, "dp_0"), "dp_1")
    all_images = lax.axis_size(DP)
    update = (summed_rows + noise_mult * clip_norm * noise) / jnp.sqrt(jnp.float32(all_images))
    return (update, clip_scale.reshape(1))


def solution(mesh):
    torus = Mesh(mesh.devices.reshape(8, 8, 4, 2), ("dp_0", "dp_1", "x", "core"))
    everyone = ("dp_0", "dp_1", "x", "core")
    placed = (
        P(AUG, DP, None, None),
        P(AUG, DP, None, None),
        P(everyone, None),
        P(everyone, None),
        P(everyone, None),
        P(),
        P(),
        P(everyone, None),
        P(None, AUG, None),
    )
    return jax.shard_map(
        local, mesh=torus, in_specs=placed, out_specs=(P(None, AUG, None), P(DP)), check_vma=False
    )
```

time: 239 us -> 129 us (0.54)
  waiting for transfers between devices: 128 us -> 35.8 us
  blocking collectives: 73.6 us -> 27.2 us
  starting transfers between devices: 4.83 us -> 34.8 us
  between operations: 16 us -> 2.89 us
  matrix products: 12.2 us -> 21.6 us
    all_gather x1 -> x0, waiting for transfers between devices: 113 us -> none  [side_by_side(): lax.all_gather(both, axis, axis=dim, tiled=True)]
    psum x2 -> x0, blocking collectives: 58.1 us -> none  [by_axis(): shard = lax.psum(shard, axis)]
    all_to_all x0 -> x2, blocking collectives: none -> 27.2 us  [copy_for_each(): lax.all_to_all(jnp.broadcast_to(shard[None], (size, *shard.shape)), axis,...]
    all_to_all x1 -> x2, starting transfers between devices: 4.79 us -> 21.5 us  [copy_for_each(): lax.all_to_all(jnp.broadcast_to(shard[None], (size, *shard.shape)), axis,...]
    ppermute x0 -> x5, waiting for transfers between devices: none -> 15.7 us  [the longest x4 15.6 us: neighbour(): return lax.ppermute(array, 'x', [(i, (i + shift) % 4) for i in range(4)])]
    all_gather x1 -> x0, blocking collectives: 15.5 us -> none  [side_by_side(): lax.all_gather(both, axis, axis=dim, tiled=True)]
    ppermute x0 -> x5, starting transfers between devices: none -> 13.2 us  [the longest x4 11.3 us: neighbour(): return lax.ppermute(array, 'x', [(i, (i + shift) % 4) for i in range(4)])]
    dot_general x5 -> x10, matrix products: 12.2 us -> 21.6 us  [contract(): lax.dot_general(left, right, ((dims[0], dims[1]), ((), ())), preferred_el...]
  transfers between devices with their start and end apart: 2 -> 7, of which waited for: 2 -> 6; matrix products, arithmetic and copies ran while one was open for 0% -> 5% of each run, Pallas kernels for 0% -> 0%
where the time goes in v1:
time: 129 us; the launch traced here: 128 us
  waiting for transfers between devices  35.8 us (28%)
  starting transfers between devices  34.8 us (27%)
  blocking collectives  27.2 us (21%)
  matrix products  21.6 us (17%)
  local copies, waits for them, and re-layouts  3.41 us (3%)
  between operations  2.89 us (2%)
  other arithmetic  2.24 us (2%)
    all_to_all x2, blocking collectives, copy_for_each(): lax.all_to_all(jnp.broadcast_to(shard[None], (size, *shard.shape)), axis,...  27.2 us
    dot_general x10, matrix products, contract(): lax.dot_general(left, right, ((dims[0], dims[1]), ((), ())), preferred_el...  21.6 us
    all_to_all x2, starting transfers between devices, copy_for_each(): lax.all_to_all(jnp.broadcast_to(shard[None], (size, *shard.shape)), axis,...  21.5 us
    all_to_all x2, waiting for transfers between devices, copy_for_each(): lax.all_to_all(jnp.broadcast_to(shard[None], (size, *shard.shape)), axis,...  20.1 us
    ppermute x4, waiting for transfers between devices, neighbour(): return lax.ppermute(array, 'x', [(i, (i + shift) % 4) for i in range(4)])  15.6 us
    ppermute x4, starting transfers between devices, neighbour(): return lax.ppermute(array, 'x', [(i, (i + shift) % 4) for i in range(4)])  11.3 us
  transfers between devices with their start and end apart: 7, of which 6 were waited for; matrix products, arithmetic and copies ran while one was open for 5% of the time, Pallas kernels for 0%

profile of v1, /device:TPU:2, one launch (start us, length us, event | category | flops | bytes accessed | tf_op | source)
XLA Modules:
  0.0 128.0 jit_solution(1989729809425994589)
XLA Ops:
  0.6 0.7 copy_bitcast_fusion
  1.5 0.8 maximum_maximum_fusion
  2.3 1.3 broadcast_in_dim.11
  3.5 16.7 %all-to-all-start = ((bf16[64,8,1536]{2,1,0:T(8,128)(2,1)}), bf16[64,8,1536]{2,1,0:T(8,128)(2,1)S(1)}, u32[]{:S(2)}, u32[]{:S(2)}) async-start(bf16[64,8,1536]{2,1,0:T(8,128)(2,1)} %broadcast_in_dim.11), calls=%async_computation | async-start | bytes 3145728 | tf_op jit(solution)/shard_map/all_to_all | solution.py:22
  20.3 0.1 fusion.98
  20.5 2.4 %collective-permute-start.1 = (bf16[2,200,768]{2,1,0:T(8,128)(2,1)S(1)}, bf16[2,200,768]{2,1,0:T(8,128)(2,1)S(1)}, u32[]{:S(2)}, u32[]{:S(2)}) collective-permute-start(bf16[2,200,768]{2,1,0:T(8,128)(2,1)S(1)} %pad_maximum_fusion.2), channel_id=1, source_target_pairs={{0,6},{2,0},{4,2},{6,4},{1,7},{3,1},{5,3},{7,5},{8,14},{10,8},{12,... | collective-permute-start | bytes 1843208 | tf_op jit(solution)/shard_map/ppermute | solution.py:72
  22.9 3.4 %collective-permute-start = (bf16[2,200,768]{2,1,0:T(8,128)(2,1)S(1)}, bf16[2,200,768]{2,1,0:T(8,128)(2,1)S(1)}, u32[]{:S(2)}, u32[]{:S(2)}) collective-permute-start(bf16[2,200,768]{2,1,0:T(8,128)(2,1)S(1)} %pad_maximum_fusion.2), channel_id=1, source_target_pairs={{0,2},{2,4},{4,6},{6,0},{1,3},{3,5},{5,7},{7,1},{8,10},{10,12},{12... | collective-permute-start | bytes 1843208 | tf_op jit(solution)/shard_map/ppermute | solution.py:72
  26.4 11.3 %collective-permute-done.1 = bf16[2,200,768]{2,1,0:T(8,128)(2,1)S(1)} collective-permute-done((bf16[2,200,768]{2,1,0:T(8,128)(2,1)S(1)}, bf16[2,200,768]{2,1,0:T(8,128)(2,1)S(1)}, u32[]{:S(2)}, u32[]{:S(2)}) %collective-permute-start.1) | collective-permute-done | bytes 614432 | tf_op jit(solution)/shard_map/ppermute | solution.py:72
  37.7 2.7 %collective-permute-start.2 = (bf16[200,768]{1,0:T(8,128)(2,1)S(1)}, bf16[200,768]{1,0:T(8,128)(2,1)}, u32[]{:S(2)}, u32[]{:S(2)}) collective-permute-start(bf16[200,768]{1,0:T(8,128)(2,1)S(1)} %get-tuple-element.27), channel_id=1, source_target_pairs={{0,6},{2,0},{4,2},{6,4},{1,7},{3,1},{5,3},{7,5},{8,14},{10,8},{12,... | collective-permute-start | bytes 921608 | tf_op jit(solution)/shard_map/ppermute | solution.py:72
  40.5 0.4 collective-permute-done
  40.9 2.8 %collective-permute-start.3 = (bf16[200,768]{1,0:T(8,128)(2,1)S(1)}, bf16[200,768]{1,0:T(8,128)(2,1)}, u32[]{:S(2)}, u32[]{:S(2)}) collective-permute-start(bf16[200,768]{1,0:T(8,128)(2,1)S(1)} %get-tuple-element.28), channel_id=1, source_target_pairs={{0,2},{2,4},{4,6},{6,0},{1,3},{3,5},{5,7},{7,1},{8,10},{10,12},{12... | collective-permute-start | bytes 921608 | tf_op jit(solution)/shard_map/ppermute | solution.py:72
  43.7 3.9 %collective-permute-done.2 = bf16[200,768]{1,0:T(8,128)(2,1)} collective-permute-done((bf16[200,768]{1,0:T(8,128)(2,1)S(1)}, bf16[200,768]{1,0:T(8,128)(2,1)}, u32[]{:S(2)}, u32[]{:S(2)}) %collective-permute-start.2) | collective-permute-done | bytes 307232 | tf_op jit(solution)/shard_map/ppermute | solution.py:72
  47.6 2.1 %convolution_convert_fusion.2 = bf16[800,128]{1,0:T(8,128)(2,1)} fusion(bf16[768,128]{1,0:T(8,128)(2,1)S(1)} %copy-done, bf16[200,768]{1,0:T(8,128)(2,1)} %collective-permute-done.2, bf16[200,768]{1,0:T(8,128)(2,1)S(1)} %get-tuple-element.27, bf16[200,768]{1,0:T(8,128)(2,1)S(1)} %get-tuple-element.29, bf16[200,768]{1,0:T(8,128)(2,1)S(1)} %get-tuple-element.37), kind=kOutput, calls=%fused_computation.41 | convolution fusion | flops 162304000 | bytes 1630208 | tf_op jit(solution)/shard_map/dot_general | solution.py:42
  49.7 11.2 %all-to-all-done = bf16[64,8,1536]{2,1,0:T(8,128)(2,1)S(1)} async-done(((bf16[64,8,1536]{2,1,0:T(8,128)(2,1)}), bf16[64,8,1536]{2,1,0:T(8,128)(2,1)S(1)}, u32[]{:S(2)}, u32[]{:S(2)}) %all-to-all-start) | async-done | bytes 1572896 | tf_op jit(solution)/shard_map/all_to_all | solution.py:22
  61.0 1.4 %convolution_convert_fusion.1 = bf16[448,1536]{1,0:T(8,128)(2,1)S(1)} fusion(bf16[64,8,1536]{2,1,0:T(8,128)(2,1)S(1)} %all-to-all-done, s32[448]{0:T(512)S(1)} %get-tuple-element.40, s32[448]{0:T(512)S(1)} %get-tuple-element.43, s32[448]{0:T(512)S(1)} %get-tuple-element.41, s32[448]{0:T(512)S(1)} %get-tuple-element.42, ...), kind=kOutput, calls=%fused_computation.1 | convolution fusion | flops 706478080 | bytes 2957184 | tf_op jit(solution)/shard_map/dot_general | solution.py:42
  62.4 1.9 %collective-permute-start.4 = (bf16[64,8,1536]{2,1,0:T(8,128)(2,1)S(1)}, bf16[64,8,1536]{2,1,0:T(8,128)(2,1)S(1)}, u32[]{:S(2)}, u32[]{:S(2)}) collective-permute-start(bf16[64,8,1536]{2,1,0:T(8,128)(2,1)S(1)} %all-to-all-done), channel_id=1, source_target_pairs={{0,1},{1,0},{2,3},{3,2},{4,5},{5,4},{6,7},{7,6},{8,9},{9,8},{10,11... | collective-permute-start | bytes 4718600 | tf_op jit(solution)/shard_map/ppermute | solution.py:97
  64.5 1.8 %fusion.66 = f32[800,384]{1,0:T(8,128)S(1)} fusion(bf16[448,1536]{1,0:T(8,128)(2,1)S(1)} %convolution_convert_fusion.1, bf16[200,768]{1,0:T(8,128)(2,1)} %collective-permute-done.3, bf16[200,768]{1,0:T(8,128)(2,1)S(1)} %get-tuple-element.26, bf16[200,768]{1,0:T(8,128)(2,1)S(1)} %get-tuple-element.28, bf16[200,768]{1,0:T(8,128)(2,1)S(1)} %get-tuple-element.30), kind=kOutput, calls=%fused_computation.75 | convolution fusion | flops 476774400 | bytes 3047424 | tf_op jit(solution)/shard_map/dot_general | solution.py:42
  66.3 1.3 %fusion.61 = f32[800,128]{1,0:T(8,128)} fusion(bf16[384,128]{1,0:T(8,128)(2,1)S(1)} %get-tuple-element.3, f32[800,384]{1,0:T(8,128)S(1)} %fusion.66), kind=kOutput, calls=%fused_computation.71 | convolution fusion | flops 81408000 | bytes 1736704 | tf_op jit(solution)/shard_map/dot_general | solution.py:42
  67.6 0.1 collective-permute-done.4
  67.8 1.4 %convolution_convert_fusion = bf16[448,1536]{1,0:T(8,128)(2,1)S(1)} fusion(bf16[64,8,1536]{2,1,0:T(8,128)(2,1)S(1)} %collective-permute-done.4, s32[448]{0:T(512)S(1)} %get-tuple-element.40, s32[448]{0:T(512)S(1)} %copy-done.12, s32[448]{0:T(512)S(1)} %get-tuple-element.41, s32[448]{0:T(512)S(1)} %copy-done.10, pred[448]{0:T(512)(128)(4,1)S(1)} %copy-done.15, ...), kind=kOutput, calls=%fused_computation | convolution fusion | flops 706478080 | bytes 2957184 | tf_op jit(solution)/shard_map/dot_general | solution.py:42
  69.3 2.9 %fusion.62 = f32[800,384]{1,0:T(8,128)} fusion(bf16[448,1536]{1,0:T(8,128)(2,1)S(1)} %convolution_convert_fusion, bf16[200,768]{1,0:T(8,128)(2,1)} %collective-permute-done.3, bf16[200,768]{1,0:T(8,128)(2,1)S(1)} %get-tuple-element.26, bf16[200,768]{1,0:T(8,128)(2,1)S(1)} %get-tuple-element.28, bf16[200,768]{1,0:T(8,128)(2,1)S(1)} %get-tuple-element.30), kind=kOutput, calls=%fused_computation.72 | convolution fusion | flops 476774400 | bytes 3047424 | tf_op jit(solution)/shard_map/dot_general | solution.py:42
  72.2 2.2 %fusion.42 = bf16[1,128,128]{2,1,0:T(8,128)(2,1)S(1)} fusion(bf16[800,128]{1,0:T(8,128)(2,1)} %convolution_convert_fusion.2, f32[800,128]{1,0:T(8,128)} %fusion.61, bf16[384,128]{1,0:T(8,128)(2,1)} %copy-done.8, f32[800,384]{1,0:T(8,128)} %fusion.62), kind=kOutput, calls=%fused_computation.53 | convolution fusion | flops 107843584 | bytes 1974272 | tf_op jit(solution)/shard_map/dot_general | solution.py:42
  74.4 3.6 %fusion.4 = f32[800,128]{1,0:T(8,128)} fusion(bf16[384,128]{1,0:T(8,128)(2,1)} %copy-done.7, f32[800,384]{1,0:T(8,128)} %fusion.62, bf16[448,1536]{1,0:T(8,128)(2,1)S(1)} %convolution_convert_fusion, bf16[200,768]{1,0:T(8,128)(2,1)} %collective-permute-done.2, bf16[200,768]{1,0:T(8,128)(2,1)S(1)} %get-tuple-element.27, bf16[200,768]{1,0:T(8,128)(2,1)S(1)} %copy-done.4, ...), kind=kOutput, calls=%fused_computation.12 | convolution fusion | flops 561254400 | bytes 3555328 | tf_op jit(solution)/shard_map/dot_general | solution.py:42
  78.0 3.2 %fusion.29 = bf16[800,128]{1,0:T(8,128)(2,1)S(1)} fusion(f32[800,128]{1,0:T(8,128)} %fusion.4, bf16[384,128]{1,0:T(8,128)(2,1)S(1)} %get-tuple-element.2, f32[800,384]{1,0:T(8,128)} %copy-done.18, bf16[448,1536]{1,0:T(8,128)(2,1)} %copy-done.5, bf16[200,768]{1,0:T(8,128)(2,1)} %collective-permute-done.2, bf16[200,768]{1,0:T(8,128)(2,1)S(1)} %get-tuple-element.27, ...), kind=kOutput, calls=%fused_computation.40 | convolution fusion | flops 561459200 | bytes 3760128 | tf_op jit(solution)/shard_map/dot_general | solution.py:42
  81.2 1.7 %fusion.41 = bf16[1,128,128]{2,1,0:T(8,128)(2,1)S(1)} fusion(bf16[800,128]{1,0:T(8,128)(2,1)S(1)} %fusion.29, bf16[768,128]{1,0:T(8,128)(2,1)S(1)} %copy-done.13, bf16[200,768]{1,0:T(8,128)(2,1)} %collective-permute-done.3, bf16[200,768]{1,0:T(8,128)(2,1)S(1)} %get-tuple-element.26, bf16[200,768]{1,0:T(8,128)(2,1)S(1)} %get-tuple-element.28, ...), kind=kOutput, calls=%fused_computation.52 | convolution fusion | flops 188534784 | bytes 1662976 | tf_op jit(solution)/shard_map/dot_general | solution.py:42
  82.9 0.9 broadcast_in_dim.12
  83.8 4.8 %all-to-all-start.1 = ((bf16[8,2,128,128]{3,2,1,0:T(8,128)(2,1)}), bf16[8,2,128,128]{3,2,1,0:T(8,128)(2,1)S(1)}, u32[]{:S(2)}, u32[]{:S(2)}) async-start(bf16[8,2,128,128]{3,2,1,0:T(8,128)(2,1)} %broadcast_in_dim.12), calls=%async_computation.1 | async-start | bytes 1048576 | tf_op jit(solution)/shard_map/all_to_all | solution.py:22
  88.7 8.9 %all-to-all-done.1 = bf16[8,2,128,128]{3,2,1,0:T(8,128)(2,1)S(1)} async-done(((bf16[8,2,128,128]{3,2,1,0:T(8,128)(2,1)}), bf16[8,2,128,128]{3,2,1,0:T(8,128)(2,1)S(1)}, u32[]{:S(2)}, u32[]{:S(2)}) %all-to-all-start.1) | async-done | bytes 524320 | tf_op jit(solution)/shard_map/all_to_all | solution.py:22
  97.6 0.6 multiply_reduce_fusion
  98.9 14.1 %all_to_all.20 = f32[8,2,16,128]{3,2,1,0:T(8,128)S(1)} all-to-all(f32[8,2,16,128]{3,2,1,0:T(8,128)S(1)} %broadcast_in_dim.13), channel_id=1, replica_groups=mesh['dp_0'=8,'dp_1'=8,'x'=4,'core'=2] {'dp_0'}, dimensions={0} | all-to-all | bytes 262144 | tf_op jit(solution)/shard_map/all_to_all | solution.py:22
  113.1 13.1 %all_to_all.21 = f32[8,2,16,128]{3,2,1,0:T(8,128)S(1)} all-to-all(f32[8,2,16,128]{3,2,1,0:T(8,128)S(1)} %broadcast_in_dim.14), channel_id=1, replica_groups=mesh['dp_0'=8,'dp_1'=8,'x'=4,'core'=2] {'dp_1'}, dimensions={0} | all-to-all | bytes 262144 | tf_op jit(solution)/shard_map/all_to_all | solution.py:22
  126.2 0.6 add_multiply_fusion
  (65 shorter events, 0.6 us)
Async XLA Ops:
  0.6 47.0 %copy-start = (bf16[768,128]{1,0:T(8,128)(2,1)S(1)}, bf16[768,128]{1,0:T(8,128)(2,1)}, u32[]{:S(2)}) copy-start(bf16[768,128]{1,0:T(8,128)(2,1)} %param.15) | copy-start | bytes 589828
  3.5 16.7 %copy-start.1 = (bf16[1,1,197,768]{3,2,1,0:T(8,128)(2,1)S(1)}, bf16[1,1,197,768]{3,2,1,0:T(8,128)(2,1)}, u32[]{:S(2)}) copy-start(bf16[1,1,197,768]{3,2,1,0:T(8,128)(2,1)} %param.9) | copy-start | bytes 907780
  3.5 16.7 %copy-start.2 = (bf16[1,1,197,768]{3,2,1,0:T(8,128)(2,1)S(1)}, bf16[1,1,197,768]{3,2,1,0:T(8,128)(2,1)}, u32[]{:S(2)}) copy-start(bf16[1,1,197,768]{3,2,1,0:T(8,128)(2,1)} %param.10) | copy-start | bytes 907780
  3.5 57.4 %all-to-all-start = ((bf16[64,8,1536]{2,1,0:T(8,128)(2,1)}), bf16[64,8,1536]{2,1,0:T(8,128)(2,1)S(1)}, u32[]{:S(2)}, u32[]{:S(2)}) async-start(bf16[64,8,1536]{2,1,0:T(8,128)(2,1)} %broadcast_in_dim.11), calls=%async_computation | async-start | bytes 3145728 | tf_op jit(solution)/shard_map/all_to_all | solution.py:22
  20.5 17.2 %collective-permute-start.1 = (bf16[2,200,768]{2,1,0:T(8,128)(2,1)S(1)}, bf16[2,200,768]{2,1,0:T(8,128)(2,1)S(1)}, u32[]{:S(2)}, u32[]{:S(2)}) collective-permute-start(bf16[2,200,768]{2,1,0:T(8,128)(2,1)S(1)} %pad_maximum_fusion.2), channel_id=1, source_target_pairs={{0,6},{2,0},{4,2},{6,4},{1,7},{3,1},{5,3},{7,5},{8,14},{10,8},{12,... | collective-permute-start | bytes 1843208 | tf_op jit(solution)/shard_map/ppermute | solution.py:72
  22.9 18.0 %collective-permute-start = (bf16[2,200,768]{2,1,0:T(8,128)(2,1)S(1)}, bf16[2,200,768]{2,1,0:T(8,128)(2,1)S(1)}, u32[]{:S(2)}, u32[]{:S(2)}) collective-permute-start(bf16[2,200,768]{2,1,0:T(8,128)(2,1)S(1)} %pad_maximum_fusion.2), channel_id=1, source_target_pairs={{0,2},{2,4},{4,6},{6,0},{1,3},{3,5},{5,7},{7,1},{8,10},{10,12},{12... | collective-permute-start | bytes 1843208 | tf_op jit(solution)/shard_map/ppermute | solution.py:72
  26.3 34.6 %copy-start.9 = (s32[448]{0:T(512)}, s32[448]{0:T(512)S(1)}, u32[]{:S(2)}) copy-start(s32[448]{0:T(512)S(1)} %get-tuple-element.42) | copy-start | bytes 5380
  26.4 34.6 %copy-start.11 = (s32[448]{0:T(512)}, s32[448]{0:T(512)S(1)}, u32[]{:S(2)}) copy-start(s32[448]{0:T(512)S(1)} %get-tuple-element.43) | copy-start | bytes 5380
  37.7 9.9 %collective-permute-start.2 = (bf16[200,768]{1,0:T(8,128)(2,1)S(1)}, bf16[200,768]{1,0:T(8,128)(2,1)}, u32[]{:S(2)}, u32[]{:S(2)}) collective-permute-start(bf16[200,768]{1,0:T(8,128)(2,1)S(1)} %get-tuple-element.27), channel_id=1, source_target_pairs={{0,6},{2,0},{4,2},{6,4},{1,7},{3,1},{5,3},{7,5},{8,14},{10,8},{12,... | collective-permute-start | bytes 921608 | tf_op jit(solution)/shard_map/ppermute | solution.py:72
  40.5 20.5 %copy-start.14 = (pred[448]{0:T(512)(128)(4,1)}, pred[448]{0:T(512)(128)(4,1)S(1)}, u32[]{:S(2)}) copy-start(pred[448]{0:T(512)(128)(4,1)S(1)} %get-tuple-element.44) | copy-start | bytes 1348
  40.5 20.5 %copy-start.16 = (pred[448]{0:T(512)(128)(4,1)}, pred[448]{0:T(512)(128)(4,1)S(1)}, u32[]{:S(2)}) copy-start(pred[448]{0:T(512)(128)(4,1)S(1)} %get-tuple-element.45) | copy-start | bytes 1348
  40.9 6.7 %copy-start.3 = (bf16[200,768]{1,0:T(8,128)(2,1)}, bf16[200,768]{1,0:T(8,128)(2,1)S(1)}, u32[]{:S(2)}) copy-start(bf16[200,768]{1,0:T(8,128)(2,1)S(1)} %get-tuple-element.29) | copy-start | bytes 921604
  40.9 23.5 %collective-permute-start.3 = (bf16[200,768]{1,0:T(8,128)(2,1)S(1)}, bf16[200,768]{1,0:T(8,128)(2,1)}, u32[]{:S(2)}, u32[]{:S(2)}) collective-permute-start(bf16[200,768]{1,0:T(8,128)(2,1)S(1)} %get-tuple-element.28), channel_id=1, source_target_pairs={{0,2},{2,4},{4,6},{6,0},{1,3},{3,5},{5,7},{7,1},{8,10},{10,12},{12... | collective-permute-start | bytes 921608 | tf_op jit(solution)/shard_map/ppermute | solution.py:72
  62.4 3.8 %copy-start.5 = (bf16[448,1536]{1,0:T(8,128)(2,1)}, bf16[448,1536]{1,0:T(8,128)(2,1)S(1)}, u32[]{:S(2)}) copy-start(bf16[448,1536]{1,0:T(8,128)(2,1)S(1)} %convolution_convert_fusion.1) | copy-start | bytes 4128772
  62.4 5.3 %collective-permute-start.4 = (bf16[64,8,1536]{2,1,0:T(8,128)(2,1)S(1)}, bf16[64,8,1536]{2,1,0:T(8,128)(2,1)S(1)}, u32[]{:S(2)}, u32[]{:S(2)}) collective-permute-start(bf16[64,8,1536]{2,1,0:T(8,128)(2,1)S(1)} %all-to-all-done), channel_id=1, source_target_pairs={{0,1},{1,0},{2,3},{3,2},{4,5},{5,4},{6,7},{7,6},{8,9},{9,8},{10,11... | collective-permute-start | bytes 4718600 | tf_op jit(solution)/shard_map/ppermute | solution.py:97
  66.3 1.4 %copy-start.18 = (f32[800,384]{1,0:T(8,128)}, f32[800,384]{1,0:T(8,128)S(1)}, u32[]{:S(2)}) copy-start(f32[800,384]{1,0:T(8,128)S(1)} %fusion.66) | copy-start | bytes 3686404
  66.3 1.5 %copy-start.10 = (s32[448]{0:T(512)S(1)}, s32[448]{0:T(512)}, u32[]{:S(2)}) copy-start(s32[448]{0:T(512)} %copy-done.9) | copy-start | bytes 5380
  66.3 1.5 %copy-start.12 = (s32[448]{0:T(512)S(1)}, s32[448]{0:T(512)}, u32[]{:S(2)}) copy-start(s32[448]{0:T(512)} %copy-done.11) | copy-start | bytes 5380
  66.3 1.5 %copy-start.15 = (pred[448]{0:T(512)(128)(4,1)S(1)}, pred[448]{0:T(512)(128)(4,1)}, u32[]{:S(2)}) copy-start(pred[448]{0:T(512)(128)(4,1)} %copy-done.14) | copy-start | bytes 1348
  66.3 1.5 %copy-start.17 = (pred[448]{0:T(512)(128)(4,1)S(1)}, pred[448]{0:T(512)(128)(4,1)}, u32[]{:S(2)}) copy-start(pred[448]{0:T(512)(128)(4,1)} %copy-done.16) | copy-start | bytes 1348
  69.3 2.9 %copy-start.7 = (bf16[384,128]{1,0:T(8,128)(2,1)}, bf16[384,128]{1,0:T(8,128)(2,1)S(1)}, u32[]{:S(2)}) copy-start(bf16[384,128]{1,0:T(8,128)(2,1)S(1)} %get-tuple-element.14) | copy-start | bytes 294916
  69.3 2.9 %copy-start.8 = (bf16[384,128]{1,0:T(8,128)(2,1)}, bf16[384,128]{1,0:T(8,128)(2,1)S(1)}, u32[]{:S(2)}) copy-start(bf16[384,128]{1,0:T(8,128)(2,1)S(1)} %get-tuple-element.15) | copy-start | bytes 294916
  72.2 2.2 %copy-start.4 = (bf16[200,768]{1,0:T(8,128)(2,1)S(1)}, bf16[200,768]{1,0:T(8,128)(2,1)}, u32[]{:S(2)}) copy-start(bf16[200,768]{1,0:T(8,128)(2,1)} %copy-done.3) | copy-start | bytes 921604
  78.0 3.2 %copy-start.13 = (bf16[768,128]{1,0:T(8,128)(2,1)S(1)}, bf16[768,128]{1,0:T(8,128)(2,1)}, u32[]{:S(2)}) copy-start(bf16[768,128]{1,0:T(8,128)(2,1)} %param.14) | copy-start | bytes 589828
  83.8 13.7 %all-to-all-start.1 = ((bf16[8,2,128,128]{3,2,1,0:T(8,128)(2,1)}), bf16[8,2,128,128]{3,2,1,0:T(8,128)(2,1)S(1)}, u32[]{:S(2)}, u32[]{:S(2)}) async-start(bf16[8,2,128,128]{3,2,1,0:T(8,128)(2,1)} %broadcast_in_dim.12), calls=%async_computation.1 | async-start | bytes 1048576 | tf_op jit(solution)/shard_map/all_to_all | solution.py:22
  88.7 37.6 %copy-start.6 = (f32[2,16,128]{2,1,0:T(8,128)S(1)}, f32[2,16,128]{2,1,0:T(8,128)}, u32[]{:S(2)}) copy-start(f32[2,16,128]{2,1,0:T(8,128)} %param.17) | copy-start | bytes 49156

commit v2 on v1

v2 whole, which is shorter than its diff:
```python
import functools
import math

import jax
import jax.numpy as jnp
from jax import lax
from jax.experimental import pallas as pl
from jax.experimental.pallas import tpu as pltpu
from jax.sharding import Mesh
from jax.sharding import PartitionSpec as P


DP = ("dp_0", "dp_1")
AUG = ("x", "core")
bf16 = jnp.bfloat16
f32 = jnp.float32


gelu_coef = 0.7978845608028654
clip_frac = 0.3
noise_mult = 0.05
kernel_vmem = 24 * 2**20


def copy_for_each(shard, axis):
    size = lax.axis_size(axis)
    return lax.all_to_all(
        jnp.broadcast_to(shard[None], (size, *shard.shape)), axis, 0, 0, tiled=True
    )


def of_everyone(shard, axis):
    return copy_for_each(shard, axis).astype(f32).sum(axis=0)


def gelu_pair(hidden):
    square = hidden * hidden
    inner = hidden * (gelu_coef + (gelu_coef * 0.044715) * square)
    upper = 0.5 + 0.5 * jnp.tanh(inner)
    value = hidden * upper
    bend = 2.0 * gelu_coef + (6.0 * 0.044715 * gelu_coef) * square
    slope = upper + value * (1.0 - upper) * bend
    return (value, slope)


def contract(left, right, dims):
    return lax.dot_general(left, right, ((dims[0], dims[1]), ((), ())), preferred_element_type=f32)


def pack_weights(_, shards, fetches, results):
    up, down, left, right = shards
    (copies,) = results
    for fetch in fetches:
        fetch.wait()
    count, rows, lane = copies.shape[0], up.shape[0], left.shape[1]
    tiles = up.shape[1] // lane
    for wide, narrow, first in ((up, left, 0), (down, right, tiles)):
        for t in range(tiles):
            tile = jnp.concatenate(
                [
                    wide[:, t * lane : (t + 1) * lane].astype(f32),
                    narrow[t : t + 1, :].astype(f32),
                    jnp.zeros((8 - rows - 1, lane), f32),
                ],
                axis=0,
            ).astype(bf16)
            at = (first + t) * 8
            copies[:, at : at + 8, :] = jnp.broadcast_to(tile[None], (count, 8, lane))


def unpack_weights(gathered, senders, rank):
    height, twice = gathered.shape
    padded, width = height // senders, twice // 2
    rows = width // rank
    picked = (rows + 1) * senders
    at = lax.broadcasted_iota(jnp.int32, (picked, height), 0)
    of = lax.broadcasted_iota(jnp.int32, (picked, height), 1)
    select = (of == (at % senders) * padded + at // senders).astype(f32).astype(bf16)
    both = contract(select, gathered, ((1,), (0,))).astype(bf16)
    units = rows * senders
    up, down = both[:units, :width], both[:units, width:]
    flat = both[units:]
    left = jnp.concatenate([flat[:, r * rank : (r + 1) * rank] for r in range(rows)], axis=0)
    right = jnp.concatenate(
        [flat[:, width + r * rank : width + (r + 1) * rank] for r in range(rows)], axis=0
    )
    return up, down, left, right


def through_units(token_rows, grad_rows, weights):
    up, down, left, right = weights
    hidden = contract(token_rows, up, ((1,), (1,)))
    back = contract(grad_rows, down, ((1,), (1,)))
    activation, slope = gelu_pair(hidden)
    v_up = contract((back * slope).astype(bf16), left, ((1,), (0,)))
    u_down = contract(activation.astype(bf16), right, ((1,), (0,)))
    return v_up, u_down


def project(near, late, fetches, results):
    far, right_up, left_down = late
    u_up, v_down = results
    for fetch in fetches:
        fetch.wait()
    for k, group in enumerate((*near, far)):
        u_up[k] = contract(group[0], right_up[...], ((1,), (0,))).astype(bf16)
        v_down[k] = contract(group[1], left_down[...], ((1,), (0,))).astype(bf16)


def first_half(senders, rank, near, late, fetches, results):
    v_up, u_down = results
    unpacked = unpack_weights(near[0][...], senders, rank)
    for k, group in enumerate((*near[1:], late[0])):
        if k == len(near) - 1:
            fetches[0].wait()
        v_up[k], u_down[k] = through_units(group[0], group[1], unpacked)


def second_half(senders, rank, near, late, fetches, results):
    far, u_up, v_down, v_up, u_down = late
    (terms,) = results
    unpacked = unpack_weights(near[0][...], senders, rank)
    for fetch in fetches:
        fetch.wait()
    first, second = 0.0, 0.0
    for k, group in enumerate((*near[1:], far)):
        v_up_rest, u_down_rest = through_units(group[0], group[1], unpacked)
        v_up_all = (v_up[k] + v_up_rest).astype(bf16)
        u_down_all = (u_down[k] + u_down_rest).astype(bf16)
        first += contract(v_up_all, u_up[k], ((0,), (0,)))
        second += contract(v_down[k], u_down_all, ((0,), (0,)))
    both = jnp.stack([first, second]).astype(bf16)
    terms[...] = jnp.broadcast_to(both[None], terms.shape)


def held(arrays, space):
    return [pltpu.with_memory_space_constraint(a, space) for a in arrays]


def kernel(body, results, near, late=(), flops=0):
    def run(*refs):
        at, parts = 0, []
        for size in (len(near), len(late), len(results), len(late)):
            parts.append(refs[at : at + size])
            at += size
        near_refs, sources, result_refs, late_refs = parts
        fetches = [
            pltpu.make_async_copy(source, target, refs[at].at[i])
            for i, (source, target) in enumerate(zip(sources, late_refs))
        ]
        for fetch in fetches:
            fetch.start()
        body(near_refs, late_refs, fetches, result_refs)

    spec = pl.BlockSpec(memory_space=pltpu.VMEM)
    scratch = [pltpu.VMEM(a.shape, a.dtype) for a in late]
    call = pl.pallas_call(
        run,
        out_shape=tuple(pltpu.HBM(shape, dtype) for shape, dtype in results),
        in_specs=[spec] * len(near) + [pl.BlockSpec(memory_space=pltpu.HBM)] * len(late),
        out_specs=(spec,) * len(results),
        scratch_shapes=scratch + [pltpu.SemaphoreType.DMA((max(1, len(late)),))],
        compiler_params=pltpu.CompilerParams(vmem_limit_bytes=kernel_vmem),
        cost_estimate=pl.CostEstimate(flops=flops, bytes_accessed=10**6, transcendentals=0),
    )
    return call(*held(near, pltpu.VMEM), *held(late, pltpu.HBM))


def neighbour(array, shift):
    return lax.ppermute(array, "x", [(i, (i + shift) % 4) for i in range(4)])


def pad_rows(tokens):
    count, width = tokens.shape[-2:]
    return jnp.pad(tokens.reshape(count, width), ((0, -count % 8), (0, 0)))


def local(
    images, out_grads, up_weight_t, down_weight_t, left_up, right_up, left_down, right_down, noise
):
    tokens = images.shape[2]
    rank = right_up.shape[1]
    senders = lax.axis_size(DP)
    blocks = 2 * up_weight_t.shape[1] // rank
    shards = (up_weight_t, down_weight_t, left_up, right_down)
    (copies,) = kernel(pack_weights, [((senders, blocks * 8, rank), bf16)], (), shards)
    gathered = lax.all_to_all(copies, DP, 0, 0, tiled=True)
    gathered = gathered.reshape(senders, blocks, 8, rank).transpose(0, 2, 1, 3)
    gathered = gathered.reshape(senders * 8, blocks * rank)
    mine = jnp.stack([pad_rows(images), pad_rows(out_grads)])
    below = neighbour(mine, 1)
    above = neighbour(mine, -1)
    far = neighbour(mine, 2)
    partners = lax.ppermute(gathered, "core", [(0, 1), (1, 0)])
    groups = (mine, below, above)
    size = (len(groups) + 1, mine.shape[1], rank)
    kept = kernel(project, [(size, bf16)] * 2, groups, (far, right_up, left_down), flops=3 * 10**8)
    half = functools.partial(first_half, senders, rank)
    sums = kernel(half, [(size, f32)] * 2, (gathered, *groups), (far,), flops=2 * 10**9)
    all_augs = lax.axis_size(AUG)
    half = functools.partial(second_half, senders, rank)
    size = (all_augs, 2, rank, rank)
    (terms,) = kernel(
        half, [(size, bf16)], (partners, *groups), (far, *kept, *sums), flops=2 * 10**9
    )
    share_rows = rank // all_augs
    lower_row = lax.axis_index(AUG) * share_rows
    aug_mean = lax.all_to_all(terms, AUG, 0, 0, tiled=True).astype(f32).sum(axis=0) / all_augs
    squares = jnp.sum(aug_mean * aug_mean)
    my_rows = lax.dynamic_slice_in_dim(aug_mean, lower_row, share_rows, 1)
    norm = jnp.sqrt(squares + 1e-06)
    clip_norm = clip_frac * rank * math.sqrt(tokens / all_augs)
    clip_scale = jnp.minimum(1.0, clip_norm / norm)
    summed_rows = of_everyone(of_everyone(clip_scale * my_rows, "dp_0"), "dp_1")
    all_images = lax.axis_size(DP)
    update = (summed_rows + noise_mult * clip_norm * noise) / jnp.sqrt(jnp.float32(all_images))
    return (update, clip_scale.reshape(1))


def solution(mesh):
    torus = Mesh(mesh.devices.reshape(8, 8, 4, 2), ("dp_0", "dp_1", "x", "core"))
    everyone = ("dp_0", "dp_1", "x", "core")
    placed = (
        P(AUG, DP, None, None),
        P(AUG, DP, None, None),
        P(everyone, None),
        P(everyone, None),
        P(everyone, None),
        P(),
        P(),
        P(everyone, None),
        P(None, AUG, None),
    )
    return jax.shard_map(
        local, mesh=torus, in_specs=placed, out_specs=(P(None, AUG, None), P(DP)), check_vma=False
    )
```

time: 129 us -> 156 us (1.21)
  blocking collectives: 27.2 us -> 84.6 us
  matrix products: 21.6 us -> 0 us
  starting transfers between devices: 34.8 us -> 15.9 us
  Pallas kernels: 0 us -> 15.8 us
  local copies, waits for them, and re-layouts: 3.41 us -> 0.93 us
  waiting for transfers between devices: 35.8 us -> 34 us
    all_to_all x0 -> x1, blocking collectives: none -> 57.4 us  [local(): gathered = lax.all_to_all(copies, DP, 0, 0, tiled=True)]
    dot_general x10 -> x0, matrix products: 21.6 us -> none  [contract(): lax.dot_general(left, right, ((dims[0], dims[1]), ((), ())), preferred_el...]
    all_to_all x2 -> x1, starting transfers between devices: 21.5 us -> 4.14 us  [local(): lax.all_to_all(terms, AUG, 0, 0, tiled=True).astype(f32).sum(axis=0)]
    pallas_call x0 -> x4, Pallas kernels: none -> 15.8 us  [kernel(): return call(*held(near, pltpu.VMEM), *held(late, pltpu.HBM))]
    all_to_all x2 -> x1, waiting for transfers between devices: 20.1 us -> 8.86 us  [local(): lax.all_to_all(terms, AUG, 0, 0, tiled=True).astype(f32).sum(axis=0)]
    ppermute x4 -> x3, waiting for transfers between devices: 15.6 us -> 25.2 us  [neighbour(): return lax.ppermute(array, 'x', [(i, (i + shift) % 4) for i in range(4)])]
    broadcast_in_dim x4 -> x2, local copies, waits for them, and re-layouts: 2.19 us -> 0.02 us  [copy_for_each(): jnp.broadcast_to(shard[None], (size, *shard.shape))]
    ppermute x4 -> x3, starting transfers between devices: 11.3 us -> 9.88 us  [neighbour(): return lax.ppermute(array, 'x', [(i, (i + shift) % 4) for i in range(4)])]
  transfers between devices with their start and end apart: 7 -> 5, of which waited for: 6 -> 4; matrix products, arithmetic and copies ran while one was open for 5% -> 0% of each run, Pallas kernels for 0% -> 5%
where the time goes in v2:
time: 156 us; the launch traced here: 155 us
  blocking collectives  84.6 us (54%)
  waiting for transfers between devices  34 us (22%)
  starting transfers between devices  15.9 us (10%)
  Pallas kernels  15.8 us (10%)
  between operations  2.61 us (2%)
    all_to_all x1, blocking collectives, local(): gathered = lax.all_to_all(copies, DP, 0, 0, tiled=True)  57.4 us
    all_to_all x2, blocking collectives, copy_for_each(): lax.all_to_all(jnp.broadcast_to(shard[None], (size, *shard.shape)), axis,...  27.2 us
    ppermute x3, waiting for transfers between devices, neighbour(): return lax.ppermute(array, 'x', [(i, (i + shift) % 4) for i in range(4)])  25.2 us
    pallas_call x4, Pallas kernels, kernel(): return call(*held(near, pltpu.VMEM), *held(late, pltpu.HBM))  15.8 us
    ppermute x3, starting transfers between devices, neighbour(): return lax.ppermute(array, 'x', [(i, (i + shift) % 4) for i in range(4)])  9.88 us
    all_to_all x1, waiting for transfers between devices, local(): lax.all_to_all(terms, AUG, 0, 0, tiled=True).astype(f32).sum(axis=0)  8.86 us
    all_to_all x1, starting transfers between devices, local(): lax.all_to_all(terms, AUG, 0, 0, tiled=True).astype(f32).sum(axis=0)  4.14 us
  transfers between devices with their start and end apart: 5, of which 4 were waited for; matrix products, arithmetic and copies ran while one was open for 0% of the time, Pallas kernels for 5%

profile of v2, /device:TPU:2, one launch (start us, length us, event | category | flops | bytes accessed | tf_op | source)
XLA Modules:
  0.0 155.4 jit_solution(6381689779079676331)
XLA Ops:
  0.6 2.1 %shard_map.104 = bf16[64,96,128]{2,1,0:T(8,128)(2,1)} custom-call(bf16[6,768]{1,0:T(8,128)(2,1)} %refs_0_.1, bf16[6,768]{1,0:T(8,128)(2,1)} %refs_1_.1, bf16[6,128]{1,0:T(8,128)(2,1)} %refs_2_.1, bf16[6,128]{1,0:T(8,128)(2,1)} %refs_3_.1), custom_call_target="tpu_custom_call" | custom-call | bytes 1000000 | tf_op jit(solution)/shard_map/pallas_call | solution.py:166
  2.8 0.0 copy-start.1
  2.8 0.0 copy-start.2
  2.8 57.4 %all_to_all.20 = bf16[64,96,128]{2,1,0:T(8,128)(2,1)S(1)} all-to-all(bf16[64,96,128]{2,1,0:T(8,128)(2,1)} %shard_map.104), channel_id=1, replica_groups=mesh['dp_0'=8,'dp_1'=8,'x'=4,'core'=2] {'dp_0','dp_1'}, dimensions={0} | all-to-all | bytes 3145728 | tf_op jit(solution)/shard_map/all_to_all | solution.py:187
  60.2 1.9 %collective-permute-start = (bf16[512,1536]{1,0:T(8,128)(2,1)S(1)}, bf16[512,1536]{1,0:T(8,128)(2,1)S(1)}, u32[]{:S(2)}, u32[]{:S(2)}) collective-permute-start(bf16[512,1536]{1,0:T(8,128)(2,1)S(1)} %bitcast.12), channel_id=1, source_target_pairs={{0,1},{1,0},{2,3},{3,2},{4,5},{5,4},{6,7},{7,6},{8,9},{9,8},{10,11... | collective-permute-start | bytes 4718600 | tf_op jit(solution)/shard_map/ppermute | solution.py:194
  62.1 0.0 copy-done.1
  62.2 0.0 copy-done.2
  62.2 0.1 pad_bitcast_fusion
  62.2 0.1 pad_maximum_fusion.refs_0_.refs_1_
  62.3 3.4 %collective-permute-start.1 = (bf16[2,200,768]{2,1,0:T(8,128)(2,1)S(1)}, bf16[2,200,768]{2,1,0:T(8,128)(2,1)S(1)}, u32[]{:S(2)}, u32[]{:S(2)}) collective-permute-start(bf16[2,200,768]{2,1,0:T(8,128)(2,1)S(1)} %pad_maximum_fusion.refs_0_.refs_1_), channel_id=1, source_target_pairs={{0,2},{2,4},{4,6},{6,0},{1,3},{3,5},{5,7},{7,1},{8,10},{10,12},{12... | collective-permute-start | bytes 1843208 | tf_op jit(solution)/shard_map/ppermute | solution.py:170
  65.7 2.4 %collective-permute-start.2 = (bf16[2,200,768]{2,1,0:T(8,128)(2,1)S(1)}, bf16[2,200,768]{2,1,0:T(8,128)(2,1)S(1)}, u32[]{:S(2)}, u32[]{:S(2)}) collective-permute-start(bf16[2,200,768]{2,1,0:T(8,128)(2,1)S(1)} %pad_maximum_fusion.refs_0_.refs_1_), channel_id=1, source_target_pairs={{0,6},{2,0},{4,2},{6,4},{1,7},{3,1},{5,3},{7,5},{8,14},{10,8},{12,... | collective-permute-start | bytes 1843208 | tf_op jit(solution)/shard_map/ppermute | solution.py:170
  68.2 4.0 %collective-permute-start.3 = (bf16[2,200,768]{2,1,0:T(8,128)(2,1)S(1)}, bf16[2,200,768]{2,1,0:T(8,128)(2,1)S(1)}, u32[]{:S(2)}, u32[]{:S(2)}) collective-permute-start(bf16[2,200,768]{2,1,0:T(8,128)(2,1)S(1)} %pad_maximum_fusion.refs_0_.refs_1_), channel_id=1, source_target_pairs={{0,4},{2,6},{4,0},{6,2},{1,5},{3,7},{5,1},{7,3},{8,12},{10,14},{12... | collective-permute-start | bytes 1843208 | tf_op jit(solution)/shard_map/ppermute | solution.py:170
  72.2 8.7 %collective-permute-done.1.refs_1_.refs_2_ = bf16[2,200,768]{2,1,0:T(8,128)(2,1)S(1)} collective-permute-done((bf16[2,200,768]{2,1,0:T(8,128)(2,1)S(1)}, bf16[2,200,768]{2,1,0:T(8,128)(2,1)S(1)}, u32[]{:S(2)}, u32[]{:S(2)}) %collective-permute-start.1) | collective-permute-done | bytes 614432 | tf_op jit(solution)/shard_map/ppermute | solution.py:170
  80.9 2.8 %collective-permute-done.2.refs_2_.refs_3_ = bf16[2,200,768]{2,1,0:T(8,128)(2,1)S(1)} collective-permute-done((bf16[2,200,768]{2,1,0:T(8,128)(2,1)S(1)}, bf16[2,200,768]{2,1,0:T(8,128)(2,1)S(1)}, u32[]{:S(2)}, u32[]{:S(2)}) %collective-permute-start.2) | collective-permute-done | bytes 614432 | tf_op jit(solution)/shard_map/ppermute | solution.py:170
  83.7 13.7 %collective-permute-done.3.refs_3_.refs_4_ = bf16[2,200,768]{2,1,0:T(8,128)(2,1)S(1)} collective-permute-done((bf16[2,200,768]{2,1,0:T(8,128)(2,1)S(1)}, bf16[2,200,768]{2,1,0:T(8,128)(2,1)S(1)}, u32[]{:S(2)}, u32[]{:S(2)}) %collective-permute-start.3) | collective-permute-done | bytes 614432 | tf_op jit(solution)/shard_map/ppermute | solution.py:170
  97.4 0.0 copy-start
  97.4 0.8 copy-done
  98.2 2.8 %shard_map.105 = (bf16[4,200,128]{2,1,0:T(8,128)(2,1)}, bf16[4,200,128]{2,1,0:T(8,128)(2,1)}) custom-call(bf16[2,200,768]{2,1,0:T(8,128)(2,1)S(1)} %pad_maximum_fusion.refs_0_.refs_1_, bf16[2,200,768]{2,1,0:T(8,128)(2,1)S(1)} %collective-permute-done.1.refs_1_.refs_2_, bf16[2,200,768]{2,1,0:T(8,128)(2,1)S(1)} %collective-permute-done.2.refs_2_.refs_3_, ...), custom_call_target="tpu_custom_call" | custom-call | flops 300000000 | bytes 1000000 | tf_op jit(solution)/shard_map/pallas_call | solution.py:166
  101.0 5.0 %shard_map.106 = (f32[4,200,128]{2,1,0:T(8,128)}, f32[4,200,128]{2,1,0:T(8,128)}) custom-call(bf16[512,1536]{1,0:T(8,128)(2,1)S(1)} %bitcast.13, bf16[2,200,768]{2,1,0:T(8,128)(2,1)S(1)} %pad_maximum_fusion.refs_0_.refs_1_, bf16[2,200,768]{2,1,0:T(8,128)(2,1)S(1)} %collective-permute-done.1.refs_1_.refs_2_, ...), custom_call_target="tpu_custom_call" | custom-call | flops 2000000000 | bytes 1000000 | tf_op jit(solution)/shard_map/pallas_call | solution.py:166
  106.0 0.0 collective-permute-done.refs_0_
  106.0 5.9 %shard_map.107 = bf16[8,2,128,128]{3,2,1,0:T(8,128)(2,1)} custom-call(bf16[512,1536]{1,0:T(8,128)(2,1)S(1)} %collective-permute-done.refs_0_, bf16[2,200,768]{2,1,0:T(8,128)(2,1)S(1)} %pad_maximum_fusion.refs_0_.refs_1_, bf16[2,200,768]{2,1,0:T(8,128)(2,1)S(1)} %collective-permute-done.1.refs_1_.refs_2_, ...), custom_call_target="tpu_custom_call" | custom-call | flops 2000000000 | bytes 1000000 | tf_op jit(solution)/shard_map/pallas_call | solution.py:166
  111.9 0.0 copy-start.3
  111.9 4.1 %all-to-all-start.1 = ((bf16[8,2,128,128]{3,2,1,0:T(8,128)(2,1)}), bf16[8,2,128,128]{3,2,1,0:T(8,128)(2,1)S(1)}, u32[]{:S(2)}, u32[]{:S(2)}) async-start(bf16[8,2,128,128]{3,2,1,0:T(8,128)(2,1)} %shard_map.107), calls=%async_computation.1 | async-start | bytes 1048576 | tf_op jit(solution)/shard_map/all_to_all | solution.py:208
  116.1 8.9 %all-to-all-done.1 = bf16[8,2,128,128]{3,2,1,0:T(8,128)(2,1)S(1)} async-done(((bf16[8,2,128,128]{3,2,1,0:T(8,128)(2,1)}), bf16[8,2,128,128]{3,2,1,0:T(8,128)(2,1)S(1)}, u32[]{:S(2)}, u32[]{:S(2)}) %all-to-all-start.1) | async-done | bytes 524320 | tf_op jit(solution)/shard_map/all_to_all | solution.py:208
  124.9 0.1 convert_reduce_fusion
  125.0 0.6 multiply_reduce_fusion
  126.4 14.1 %all_to_all.21 = f32[8,2,16,128]{3,2,1,0:T(8,128)S(1)} all-to-all(f32[8,2,16,128]{3,2,1,0:T(8,128)S(1)} %broadcast_in_dim.4), channel_id=1, replica_groups=mesh['dp_0'=8,'dp_1'=8,'x'=4,'core'=2] {'dp_0'}, dimensions={0} | all-to-all | bytes 262144 | tf_op jit(solution)/shard_map/all_to_all | solution.py:27
  140.5 13.1 %all_to_all.22 = f32[8,2,16,128]{3,2,1,0:T(8,128)S(1)} all-to-all(f32[8,2,16,128]{3,2,1,0:T(8,128)S(1)} %broadcast_in_dim.5), channel_id=1, replica_groups=mesh['dp_0'=8,'dp_1'=8,'x'=4,'core'=2] {'dp_1'}, dimensions={0} | all-to-all | bytes 262144 | tf_op jit(solution)/shard_map/all_to_all | solution.py:27
  153.6 0.0 copy-done.3
  153.6 0.6 add_multiply_fusion
  (5 shorter events, 0.1 us)
Async XLA Ops:
  2.8 59.4 %copy-start.1 = (bf16[1,1,197,768]{3,2,1,0:T(8,128)(2,1)S(1)}, bf16[1,1,197,768]{3,2,1,0:T(8,128)(2,1)}, u32[]{:S(2)}) copy-start(bf16[1,1,197,768]{3,2,1,0:T(8,128)(2,1)} %param.10) | copy-start | bytes 907780
  2.8 59.4 %copy-start.2 = (bf16[1,1,197,768]{3,2,1,0:T(8,128)(2,1)S(1)}, bf16[1,1,197,768]{3,2,1,0:T(8,128)(2,1)}, u32[]{:S(2)}) copy-start(bf16[1,1,197,768]{3,2,1,0:T(8,128)(2,1)} %param.9) | copy-start | bytes 907780
  60.2 45.8 %collective-permute-start = (bf16[512,1536]{1,0:T(8,128)(2,1)S(1)}, bf16[512,1536]{1,0:T(8,128)(2,1)S(1)}, u32[]{:S(2)}, u32[]{:S(2)}) collective-permute-start(bf16[512,1536]{1,0:T(8,128)(2,1)S(1)} %bitcast.12), channel_id=1, source_target_pairs={{0,1},{1,0},{2,3},{3,2},{4,5},{5,4},{6,7},{7,6},{8,9},{9,8},{10,11... | collective-permute-start | bytes 4718600 | tf_op jit(solution)/shard_map/ppermute | solution.py:194
  62.3 18.6 %collective-permute-start.1 = (bf16[2,200,768]{2,1,0:T(8,128)(2,1)S(1)}, bf16[2,200,768]{2,1,0:T(8,128)(2,1)S(1)}, u32[]{:S(2)}, u32[]{:S(2)}) collective-permute-start(bf16[2,200,768]{2,1,0:T(8,128)(2,1)S(1)} %pad_maximum_fusion.refs_0_.refs_1_), channel_id=1, source_target_pairs={{0,2},{2,4},{4,6},{6,0},{1,3},{3,5},{5,7},{7,1},{8,10},{10,12},{12... | collective-permute-start | bytes 1843208 | tf_op jit(solution)/shard_map/ppermute | solution.py:170
  65.7 18.0 %collective-permute-start.2 = (bf16[2,200,768]{2,1,0:T(8,128)(2,1)S(1)}, bf16[2,200,768]{2,1,0:T(8,128)(2,1)S(1)}, u32[]{:S(2)}, u32[]{:S(2)}) collective-permute-start(bf16[2,200,768]{2,1,0:T(8,128)(2,1)S(1)} %pad_maximum_fusion.refs_0_.refs_1_), channel_id=1, source_target_pairs={{0,6},{2,0},{4,2},{6,4},{1,7},{3,1},{5,3},{7,5},{8,14},{10,8},{12,... | collective-permute-start | bytes 1843208 | tf_op jit(solution)/shard_map/ppermute | solution.py:170
  68.2 29.2 %collective-permute-start.3 = (bf16[2,200,768]{2,1,0:T(8,128)(2,1)S(1)}, bf16[2,200,768]{2,1,0:T(8,128)(2,1)S(1)}, u32[]{:S(2)}, u32[]{:S(2)}) collective-permute-start(bf16[2,200,768]{2,1,0:T(8,128)(2,1)S(1)} %pad_maximum_fusion.refs_0_.refs_1_), channel_id=1, source_target_pairs={{0,4},{2,6},{4,0},{6,2},{1,5},{3,7},{5,1},{7,3},{8,12},{10,14},{12... | collective-permute-start | bytes 1843208 | tf_op jit(solution)/shard_map/ppermute | solution.py:170
  97.4 0.8 copy-start
  111.9 41.7 %copy-start.3 = (f32[2,16,128]{2,1,0:T(8,128)S(1)}, f32[2,16,128]{2,1,0:T(8,128)}, u32[]{:S(2)}) copy-start(f32[2,16,128]{2,1,0:T(8,128)} %param.17) | copy-start | bytes 49156
  111.9 13.0 %all-to-all-start.1 = ((bf16[8,2,128,128]{3,2,1,0:T(8,128)(2,1)}), bf16[8,2,128,128]{3,2,1,0:T(8,128)(2,1)S(1)}, u32[]{:S(2)}, u32[]{:S(2)}) async-start(bf16[8,2,128,128]{3,2,1,0:T(8,128)(2,1)} %shard_map.107), calls=%async_computation.1 | async-start | bytes 1048576 | tf_op jit(solution)/shard_map/all_to_all | solution.py:208

commit v3 on v2

--- a/solution.py
+++ b/solution.py
@@ -71,20 +71,22 @@
 def unpack_weights(gathered, senders, rank):
     height, twice = gathered.shape
     padded, width = height // senders, twice // 2
-    rows = width // rank
-    picked = (rows + 1) * senders
-    at = lax.broadcasted_iota(jnp.int32, (picked, height), 0)
-    of = lax.broadcasted_iota(jnp.int32, (picked, height), 1)
-    select = (of == (at % senders) * padded + at // senders).astype(f32).astype(bf16)
-    both = contract(select, gathered, ((1,), (0,))).astype(bf16)
-    units = rows * senders
-    up, down = both[:units, :width], both[:units, width:]
-    flat = both[units:]
-    left = jnp.concatenate([flat[:, r * rank : (r + 1) * rank] for r in range(rows)], axis=0)
-    right = jnp.concatenate(
-        [flat[:, width + r * rank : width + (r + 1) * rank] for r in range(rows)], axis=0
-    )
-    return up, down, left, right
+    rows, block = width // rank, min(senders, 32)
+    shape = ((rows + 1) * block, block * padded)
+    at = lax.broadcasted_iota(jnp.int32, shape, 0)
+    of = lax.broadcasted_iota(jnp.int32, shape, 1)
+    select = (of == (at % block) * padded + at // block).astype(f32).astype(bf16)
+    units = rows * block
+    up, down, left, right = [], [], [], []
+    for first in range(0, height, block * padded):
+        piece = gathered[first : first + block * padded]
+        both = contract(select, piece, ((1,), (0,))).astype(bf16)
+        up.append(both[:units, :width])
+        down.append(both[:units, width:])
+        flat = both[units:]
+        left += [flat[:, r * rank : (r + 1) * rank] for r in range(rows)]
+        right += [flat[:, width + r * rank : width + (r + 1) * rank] for r in range(rows)]
+    return tuple(jnp.concatenate(parts, axis=0) for parts in (up, down, left, right))
 
 
 def through_units(token_rows, grad_rows, weights):
@@ -97,33 +99,26 @@
     return v_up, u_down
 
 
-def project(near, late, fetches, results):
-    far, right_up, left_down = late
-    u_up, v_down = results
+def first_half(senders, rank, near, late, fetches, results):
+    right_up, left_down = late
+    v_up, u_up, u_down, v_down = results
+    unpacked = unpack_weights(near[0][...], senders, rank)
     for fetch in fetches:
         fetch.wait()
-    for k, group in enumerate((*near, far)):
+    for k, group in enumerate(near[1:]):
+        v_up[k], u_down[k] = through_units(group[0], group[1], unpacked)
         u_up[k] = contract(group[0], right_up[...], ((1,), (0,))).astype(bf16)
         v_down[k] = contract(group[1], left_down[...], ((1,), (0,))).astype(bf16)
 
 
-def first_half(senders, rank, near, late, fetches, results):
-    v_up, u_down = results
-    unpacked = unpack_weights(near[0][...], senders, rank)
-    for k, group in enumerate((*near[1:], late[0])):
-        if k == len(near) - 1:
-            fetches[0].wait()
-        v_up[k], u_down[k] = through_units(group[0], group[1], unpacked)
-
-
 def second_half(senders, rank, near, late, fetches, results):
-    far, u_up, v_down, v_up, u_down = late
+    v_up, u_up, u_down, v_down = late
     (terms,) = results
     unpacked = unpack_weights(near[0][...], senders, rank)
     for fetch in fetches:
         fetch.wait()
     first, second = 0.0, 0.0
-    for k, group in enumerate((*near[1:], far)):
+    for k, group in enumerate(near[1:]):
         v_up_rest, u_down_rest = through_units(group[0], group[1], unpacked)
         v_up_all = (v_up[k] + v_up_rest).astype(bf16)
         u_down_all = (u_down[k] + u_down_rest).astype(bf16)
@@ -137,7 +132,7 @@
     return [pltpu.with_memory_space_constraint(a, space) for a in arrays]
 
 
-def kernel(body, results, near, late=(), flops=0):
+def kernel(body, results, near, late=(), flops=0, space=pltpu.HBM):
     def run(*refs):
         at, parts = 0, []
         for size in (len(near), len(late), len(results), len(late)):
@@ -156,7 +151,7 @@
     scratch = [pltpu.VMEM(a.shape, a.dtype) for a in late]
     call = pl.pallas_call(
         run,
-        out_shape=tuple(pltpu.HBM(shape, dtype) for shape, dtype in results),
+        out_shape=tuple(space(shape, dtype) for shape, dtype in results),
         in_specs=[spec] * len(near) + [pl.BlockSpec(memory_space=pltpu.HBM)] * len(late),
         out_specs=(spec,) * len(results),
         scratch_shapes=scratch + [pltpu.SemaphoreType.DMA((max(1, len(late)),))],
@@ -183,25 +178,29 @@
     senders = lax.axis_size(DP)
     blocks = 2 * up_weight_t.shape[1] // rank
     shards = (up_weight_t, down_weight_t, left_up, right_down)
-    (copies,) = kernel(pack_weights, [((senders, blocks * 8, rank), bf16)], (), shards)
+    size = (senders, blocks * 8, rank)
+    (copies,) = kernel(pack_weights, [(size, bf16)], (), shards, space=jax.ShapeDtypeStruct)
     gathered = lax.all_to_all(copies, DP, 0, 0, tiled=True)
     gathered = gathered.reshape(senders, blocks, 8, rank).transpose(0, 2, 1, 3)
     gathered = gathered.reshape(senders * 8, blocks * rank)
     mine = jnp.stack([pad_rows(images), pad_rows(out_grads)])
-    below = neighbour(mine, 1)
-    above = neighbour(mine, -1)
-    far = neighbour(mine, 2)
+    far, below, above = (neighbour(mine, shift) for shift in (2, 1, -1))
     partners = lax.ppermute(gathered, "core", [(0, 1), (1, 0)])
-    groups = (mine, below, above)
-    size = (len(groups) + 1, mine.shape[1], rank)
-    kept = kernel(project, [(size, bf16)] * 2, groups, (far, right_up, left_down), flops=3 * 10**8)
+    groups = (mine, below, above, far)
+    size = (len(groups), mine.shape[1], rank)
     half = functools.partial(first_half, senders, rank)
-    sums = kernel(half, [(size, f32)] * 2, (gathered, *groups), (far,), flops=2 * 10**9)
+    sums = kernel(
+        half,
+        [(size, f32), (size, bf16)] * 2,
+        (gathered, *groups),
+        (right_up, left_down),
+        flops=2 * 10**9,
+    )
     all_augs = lax.axis_size(AUG)
     half = functools.partial(second_half, senders, rank)
     size = (all_augs, 2, rank, rank)
     (terms,) = kernel(
-        half, [(size, bf16)], (partners, *groups), (far, *kept, *sums), flops=2 * 10**9
+        half, [(size, bf16)], (partners, *groups), sums, flops=2 * 10**9
     )
     share_rows = rank // all_augs
     lower_row = lax.axis_index(AUG) * share_rows

time: 156 us -> 151 us (0.968)
  Pallas kernels: 15.8 us -> 11.8 us
    pallas_call x4 -> x3, Pallas kernels: 15.8 us -> 11.8 us  [kernel(): return call(*held(near, pltpu.VMEM), *held(late, pltpu.HBM))]
  transfers between devices with their start and end apart: 5 -> 5, of which waited for: 4 -> 4; matrix products, arithmetic and copies ran while one was open for 0% -> 0% of each run, Pallas kernels for 5% -> 4%
where the time goes in v3:
time: 151 us; the launch traced here: 150 us
  blocking collectives  84.4 us (56%)
  waiting for transfers between devices  34 us (23%)
  starting transfers between devices  15.9 us (11%)
  Pallas kernels  11.8 us (8%)
  between operations  2.6 us (2%)
    all_to_all x1, blocking collectives, local(): gathered = lax.all_to_all(copies, DP, 0, 0, tiled=True)  57.2 us
    all_to_all x2, blocking collectives, copy_for_each(): lax.all_to_all(jnp.broadcast_to(shard[None], (size, *shard.shape)), axis,...  27.2 us
    ppermute x3, waiting for transfers between devices, neighbour(): return lax.ppermute(array, 'x', [(i, (i + shift) % 4) for i in range(4)])  25.2 us
    pallas_call x3, Pallas kernels, kernel(): return call(*held(near, pltpu.VMEM), *held(late, pltpu.HBM))  11.8 us
    ppermute x3, starting transfers between devices, neighbour(): return lax.ppermute(array, 'x', [(i, (i + shift) % 4) for i in range(4)])  9.88 us
    all_to_all x1, waiting for transfers between devices, local(): lax.all_to_all(terms, AUG, 0, 0, tiled=True).astype(f32).sum(axis=0)  8.86 us
    all_to_all x1, starting transfers between devices, local(): lax.all_to_all(terms, AUG, 0, 0, tiled=True).astype(f32).sum(axis=0)  4.14 us
  transfers between devices with their start and end apart: 5, of which 4 were waited for; matrix products, arithmetic and copies ran while one was open for 0% of the time, Pallas kernels for 4%

profile of v3, /device:TPU:2, one launch (start us, length us, event | category | flops | bytes accessed | tf_op | source)
XLA Modules:
  0.0 150.3 jit_solution(9889671452393246728)
XLA Ops:
  0.6 1.0 shard_map.104
  1.6 0.0 copy-start
  1.6 0.0 copy-start.1
  1.6 57.2 %all_to_all.20 = bf16[64,96,128]{2,1,0:T(8,128)(2,1)S(1)} all-to-all(bf16[64,96,128]{2,1,0:T(8,128)(2,1)S(1)} %shard_map.104), channel_id=1, replica_groups=mesh['dp_0'=8,'dp_1'=8,'x'=4,'core'=2] {'dp_0','dp_1'}, dimensions={0} | all-to-all | bytes 3145728 | tf_op jit(solution)/shard_map/all_to_all | solution.py:183
  58.8 1.9 %collective-permute-start = (bf16[512,1536]{1,0:T(8,128)(2,1)S(1)}, bf16[512,1536]{1,0:T(8,128)(2,1)S(1)}, u32[]{:S(2)}, u32[]{:S(2)}) collective-permute-start(bf16[512,1536]{1,0:T(8,128)(2,1)S(1)} %bitcast.12), channel_id=1, source_target_pairs={{0,1},{1,0},{2,3},{3,2},{4,5},{5,4},{6,7},{7,6},{8,9},{9,8},{10,11... | collective-permute-start | bytes 4718600 | tf_op jit(solution)/shard_map/ppermute | solution.py:188
  60.8 0.0 copy-done
  60.8 0.0 copy-done.1
  60.8 0.1 pad_bitcast_fusion
  60.9 0.1 pad_maximum_fusion.refs_1_
  60.9 3.4 %collective-permute-start.1 = (bf16[2,200,768]{2,1,0:T(8,128)(2,1)S(1)}, bf16[2,200,768]{2,1,0:T(8,128)(2,1)S(1)}, u32[]{:S(2)}, u32[]{:S(2)}) collective-permute-start(bf16[2,200,768]{2,1,0:T(8,128)(2,1)S(1)} %pad_maximum_fusion.refs_1_), channel_id=1, source_target_pairs={{0,2},{2,4},{4,6},{6,0},{1,3},{3,5},{5,7},{7,1},{8,10},{10,12},{12... | collective-permute-start | bytes 1843208 | tf_op jit(solution)/shard_map/ppermute | solution.py:165
  64.3 2.4 %collective-permute-start.2 = (bf16[2,200,768]{2,1,0:T(8,128)(2,1)S(1)}, bf16[2,200,768]{2,1,0:T(8,128)(2,1)S(1)}, u32[]{:S(2)}, u32[]{:S(2)}) collective-permute-start(bf16[2,200,768]{2,1,0:T(8,128)(2,1)S(1)} %pad_maximum_fusion.refs_1_), channel_id=1, source_target_pairs={{0,6},{2,0},{4,2},{6,4},{1,7},{3,1},{5,3},{7,5},{8,14},{10,8},{12,... | collective-permute-start | bytes 1843208 | tf_op jit(solution)/shard_map/ppermute | solution.py:165
  66.8 4.0 %collective-permute-start.3 = (bf16[2,200,768]{2,1,0:T(8,128)(2,1)S(1)}, bf16[2,200,768]{2,1,0:T(8,128)(2,1)S(1)}, u32[]{:S(2)}, u32[]{:S(2)}) collective-permute-start(bf16[2,200,768]{2,1,0:T(8,128)(2,1)S(1)} %pad_maximum_fusion.refs_1_), channel_id=1, source_target_pairs={{0,4},{2,6},{4,0},{6,2},{1,5},{3,7},{5,1},{7,3},{8,12},{10,14},{12... | collective-permute-start | bytes 1843208 | tf_op jit(solution)/shard_map/ppermute | solution.py:165
  70.8 8.7 %collective-permute-done.1.refs_2_ = bf16[2,200,768]{2,1,0:T(8,128)(2,1)S(1)} collective-permute-done((bf16[2,200,768]{2,1,0:T(8,128)(2,1)S(1)}, bf16[2,200,768]{2,1,0:T(8,128)(2,1)S(1)}, u32[]{:S(2)}, u32[]{:S(2)}) %collective-permute-start.1) | collective-permute-done | bytes 614432 | tf_op jit(solution)/shard_map/ppermute | solution.py:165
  79.5 2.8 %collective-permute-done.2.refs_3_ = bf16[2,200,768]{2,1,0:T(8,128)(2,1)S(1)} collective-permute-done((bf16[2,200,768]{2,1,0:T(8,128)(2,1)S(1)}, bf16[2,200,768]{2,1,0:T(8,128)(2,1)S(1)}, u32[]{:S(2)}, u32[]{:S(2)}) %collective-permute-start.2) | collective-permute-done | bytes 614432 | tf_op jit(solution)/shard_map/ppermute | solution.py:165
  82.3 13.7 %collective-permute-done.3.refs_4_ = bf16[2,200,768]{2,1,0:T(8,128)(2,1)S(1)} collective-permute-done((bf16[2,200,768]{2,1,0:T(8,128)(2,1)S(1)}, bf16[2,200,768]{2,1,0:T(8,128)(2,1)S(1)}, u32[]{:S(2)}, u32[]{:S(2)}) %collective-permute-start.3) | collective-permute-done | bytes 614432 | tf_op jit(solution)/shard_map/ppermute | solution.py:165
  96.0 5.4 %shard_map.105 = (f32[4,200,128]{2,1,0:T(8,128)}, bf16[4,200,128]{2,1,0:T(8,128)(2,1)}, f32[4,200,128]{2,1,0:T(8,128)}, bf16[4,200,128]{2,1,0:T(8,128)(2,1)}) custom-call(bf16[512,1536]{1,0:T(8,128)(2,1)S(1)} %bitcast.13, bf16[2,200,768]{2,1,0:T(8,128)(2,1)S(1)} %pad_maximum_fusion.refs_1_, bf16[2,200,768]{2,1,0:T(8,128)(2,1)S(1)} %collective-permute-done.1.refs_2_, ...), custom_call_target="tpu_custom_call" | custom-call | flops 2000000000 | bytes 1000000 | tf_op jit(solution)/shard_map/pallas_call | solution.py:161
  101.4 0.0 collective-permute-done.refs_0_
  101.4 5.4 %shard_map.106 = bf16[8,2,128,128]{3,2,1,0:T(8,128)(2,1)} custom-call(bf16[512,1536]{1,0:T(8,128)(2,1)S(1)} %collective-permute-done.refs_0_, bf16[2,200,768]{2,1,0:T(8,128)(2,1)S(1)} %pad_maximum_fusion.refs_1_, bf16[2,200,768]{2,1,0:T(8,128)(2,1)S(1)} %collective-permute-done.1.refs_2_, bf16[2,200,768]{2,1,0:T(8,128)(2,1)S(1)} %collective-permute-done.2.refs_3_, ...), custom_call_target="tpu_custom_call" | custom-call | flops 2000000000 | bytes 1000000 | tf_op jit(solution)/shard_map/pallas_call | solution.py:161
  106.9 0.0 copy-start.2
  106.9 4.1 %all-to-all-start.1 = ((bf16[8,2,128,128]{3,2,1,0:T(8,128)(2,1)}), bf16[8,2,128,128]{3,2,1,0:T(8,128)(2,1)S(1)}, u32[]{:S(2)}, u32[]{:S(2)}) async-start(bf16[8,2,128,128]{3,2,1,0:T(8,128)(2,1)} %shard_map.106), calls=%async_computation.1 | async-start | bytes 1048576 | tf_op jit(solution)/shard_map/all_to_all | solution.py:207
  111.0 8.9 %all-to-all-done.1 = bf16[8,2,128,128]{3,2,1,0:T(8,128)(2,1)S(1)} async-done(((bf16[8,2,128,128]{3,2,1,0:T(8,128)(2,1)}), bf16[8,2,128,128]{3,2,1,0:T(8,128)(2,1)S(1)}, u32[]{:S(2)}, u32[]{:S(2)}) %all-to-all-start.1) | async-done | bytes 524320 | tf_op jit(solution)/shard_map/all_to_all | solution.py:207
  119.9 0.1 convert_reduce_fusion
  120.0 0.6 multiply_reduce_fusion
  121.3 14.2 %all_to_all.21 = f32[8,2,16,128]{3,2,1,0:T(8,128)S(1)} all-to-all(f32[8,2,16,128]{3,2,1,0:T(8,128)S(1)} %broadcast_in_dim.4), channel_id=1, replica_groups=mesh['dp_0'=8,'dp_1'=8,'x'=4,'core'=2] {'dp_0'}, dimensions={0} | all-to-all | bytes 262144 | tf_op jit(solution)/shard_map/all_to_all | solution.py:27
  135.5 13.0 %all_to_all.22 = f32[8,2,16,128]{3,2,1,0:T(8,128)S(1)} all-to-all(f32[8,2,16,128]{3,2,1,0:T(8,128)S(1)} %broadcast_in_dim.5), channel_id=1, replica_groups=mesh['dp_0'=8,'dp_1'=8,'x'=4,'core'=2] {'dp_1'}, dimensions={0} | all-to-all | bytes 262144 | tf_op jit(solution)/shard_map/all_to_all | solution.py:27
  148.6 0.0 copy-done.2
  148.6 0.6 add_multiply_fusion
  (5 shorter events, 0.1 us)
Async XLA Ops:
  1.6 59.2 %copy-start = (bf16[1,1,197,768]{3,2,1,0:T(8,128)(2,1)S(1)}, bf16[1,1,197,768]{3,2,1,0:T(8,128)(2,1)}, u32[]{:S(2)}) copy-start(bf16[1,1,197,768]{3,2,1,0:T(8,128)(2,1)} %param.10) | copy-start | bytes 907780
  1.6 59.2 %copy-start.1 = (bf16[1,1,197,768]{3,2,1,0:T(8,128)(2,1)S(1)}, bf16[1,1,197,768]{3,2,1,0:T(8,128)(2,1)}, u32[]{:S(2)}) copy-start(bf16[1,1,197,768]{3,2,1,0:T(8,128)(2,1)} %param.9) | copy-start | bytes 907780
  58.8 42.6 %collective-permute-start = (bf16[512,1536]{1,0:T(8,128)(2,1)S(1)}, bf16[512,1536]{1,0:T(8,128)(2,1)S(1)}, u32[]{:S(2)}, u32[]{:S(2)}) collective-permute-start(bf16[512,1536]{1,0:T(8,128)(2,1)S(1)} %bitcast.12), channel_id=1, source_target_pairs={{0,1},{1,0},{2,3},{3,2},{4,5},{5,4},{6,7},{7,6},{8,9},{9,8},{10,11... | collective-permute-start | bytes 4718600 | tf_op jit(solution)/shard_map/ppermute | solution.py:188
  60.9 18.6 %collective-permute-start.1 = (bf16[2,200,768]{2,1,0:T(8,128)(2,1)S(1)}, bf16[2,200,768]{2,1,0:T(8,128)(2,1)S(1)}, u32[]{:S(2)}, u32[]{:S(2)}) collective-permute-start(bf16[2,200,768]{2,1,0:T(8,128)(2,1)S(1)} %pad_maximum_fusion.refs_1_), channel_id=1, source_target_pairs={{0,2},{2,4},{4,6},{6,0},{1,3},{3,5},{5,7},{7,1},{8,10},{10,12},{12... | collective-permute-start | bytes 1843208 | tf_op jit(solution)/shard_map/ppermute | solution.py:165
  64.3 18.0 %collective-permute-start.2 = (bf16[2,200,768]{2,1,0:T(8,128)(2,1)S(1)}, bf16[2,200,768]{2,1,0:T(8,128)(2,1)S(1)}, u32[]{:S(2)}, u32[]{:S(2)}) collective-permute-start(bf16[2,200,768]{2,1,0:T(8,128)(2,1)S(1)} %pad_maximum_fusion.refs_1_), channel_id=1, source_target_pairs={{0,6},{2,0},{4,2},{6,4},{1,7},{3,1},{5,3},{7,5},{8,14},{10,8},{12,... | collective-permute-start | bytes 1843208 | tf_op jit(solution)/shard_map/ppermute | solution.py:165
  66.8 29.2 %collective-permute-start.3 = (bf16[2,200,768]{2,1,0:T(8,128)(2,1)S(1)}, bf16[2,200,768]{2,1,0:T(8,128)(2,1)S(1)}, u32[]{:S(2)}, u32[]{:S(2)}) collective-permute-start(bf16[2,200,768]{2,1,0:T(8,128)(2,1)S(1)} %pad_maximum_fusion.refs_1_), channel_id=1, source_target_pairs={{0,4},{2,6},{4,0},{6,2},{1,5},{3,7},{5,1},{7,3},{8,12},{10,14},{12... | collective-permute-start | bytes 1843208 | tf_op jit(solution)/shard_map/ppermute | solution.py:165
  106.9 41.7 %copy-start.2 = (f32[2,16,128]{2,1,0:T(8,128)S(1)}, f32[2,16,128]{2,1,0:T(8,128)}, u32[]{:S(2)}) copy-start(f32[2,16,128]{2,1,0:T(8,128)} %param.17) | copy-start | bytes 49156
  106.9 13.0 %all-to-all-start.1 = ((bf16[8,2,128,128]{3,2,1,0:T(8,128)(2,1)}), bf16[8,2,128,128]{3,2,1,0:T(8,128)(2,1)S(1)}, u32[]{:S(2)}, u32[]{:S(2)}) async-start(bf16[8,2,128,128]{3,2,1,0:T(8,128)(2,1)} %shard_map.106), calls=%async_computation.1 | async-start | bytes 1048576 | tf_op jit(solution)/shard_map/all_to_all | solution.py:207

commit v4 on v3

--- a/solution.py
+++ b/solution.py
@@ -20,6 +20,7 @@
 clip_frac = 0.3
 noise_mult = 0.05
 kernel_vmem = 24 * 2**20
+lane = 128
 
 
 def copy_for_each(shard, axis):
@@ -48,45 +49,46 @@
 
 
 def pack_weights(_, shards, fetches, results):
-    up, down, left, right = shards
     (copies,) = results
+    count, height, _ = copies.shape
     for fetch in fetches:
         fetch.wait()
-    count, rows, lane = copies.shape[0], up.shape[0], left.shape[1]
-    tiles = up.shape[1] // lane
-    for wide, narrow, first in ((up, left, 0), (down, right, tiles)):
-        for t in range(tiles):
-            tile = jnp.concatenate(
-                [
-                    wide[:, t * lane : (t + 1) * lane].astype(f32),
-                    narrow[t : t + 1, :].astype(f32),
-                    jnp.zeros((8 - rows - 1, lane), f32),
-                ],
-                axis=0,
-            ).astype(bf16)
-            at = (first + t) * 8
-            copies[:, at : at + 8, :] = jnp.broadcast_to(tile[None], (count, 8, lane))
-
-
-def unpack_weights(gathered, senders, rank):
-    height, twice = gathered.shape
-    padded, width = height // senders, twice // 2
-    rows, block = width // rank, min(senders, 32)
-    shape = ((rows + 1) * block, block * padded)
-    at = lax.broadcasted_iota(jnp.int32, shape, 0)
-    of = lax.broadcasted_iota(jnp.int32, shape, 1)
-    select = (of == (at % block) * padded + at // block).astype(f32).astype(bf16)
-    units = rows * block
-    up, down, left, right = [], [], [], []
-    for first in range(0, height, block * padded):
-        piece = gathered[first : first + block * padded]
-        both = contract(select, piece, ((1,), (0,))).astype(bf16)
-        up.append(both[:units, :width])
-        down.append(both[:units, width:])
-        flat = both[units:]
-        left += [flat[:, r * rank : (r + 1) * rank] for r in range(rows)]
-        right += [flat[:, width + r * rank : width + (r + 1) * rank] for r in range(rows)]
-    return tuple(jnp.concatenate(parts, axis=0) for parts in (up, down, left, right))
+    columns = [
+        shard[:, at : at + lane].astype(f32)
+        for shard in shards
+        for at in range(0, shard.shape[1], lane)
+    ]
+    spare = height - sum(column.shape[0] for column in columns)
+    columns.append(jnp.zeros((spare, lane), f32))
+    tall = jnp.concatenate(columns, axis=0).astype(bf16)
+    copies[...] = jnp.broadcast_to(tall[None], (count, height, lane))
+
+
+def unpack_weights(gathered, senders, rows, lane):
+    height, wide = gathered.shape
+    tile, block = height // senders, min(senders, 32)
+    columns = wide // lane * tile // rows
+    size = block * tile
+    at = lax.broadcasted_iota(jnp.int32, (size, size), 0)
+    of = lax.broadcasted_iota(jnp.int32, (size, size), 1)
+    select = (of == (at % block) * tile + at // block).astype(f32).astype(bf16)
+    parts = []
+    for first in range(0, height, size):
+        both = contract(select, gathered[first : first + size], ((1,), (0,))).astype(bf16)
+
+        def cell(row, column):
+            t, s = divmod(column * rows + row, tile)
+            return both[s * block : (s + 1) * block, t * lane : (t + 1) * lane]
+
+        for row in range(rows):
+            parts.append([cell(row, column) for column in range(columns)])
+    half = (columns - 2) // 2
+    wides = [
+        jnp.concatenate([jnp.concatenate(p[lo : lo + half], axis=1) for p in parts], axis=0)
+        for lo in (0, half)
+    ]
+    narrows = [jnp.concatenate([p[c] for p in parts], axis=0) for c in (columns - 2, columns - 1)]
+    return (*wides, *narrows)
 
 
 def through_units(token_rows, grad_rows, weights):
@@ -99,10 +101,10 @@
     return v_up, u_down
 
 
-def first_half(senders, rank, near, late, fetches, results):
+def first_half(senders, rows, near, late, fetches, results):
     right_up, left_down = late
     v_up, u_up, u_down, v_down = results
-    unpacked = unpack_weights(near[0][...], senders, rank)
+    unpacked = unpack_weights(near[0][...], senders, rows, lane)
     for fetch in fetches:
         fetch.wait()
     for k, group in enumerate(near[1:]):
@@ -111,10 +113,10 @@
         v_down[k] = contract(group[1], left_down[...], ((1,), (0,))).astype(bf16)
 
 
-def second_half(senders, rank, near, late, fetches, results):
+def second_half(senders, rows, near, late, fetches, results):
     v_up, u_up, u_down, v_down = late
     (terms,) = results
-    unpacked = unpack_weights(near[0][...], senders, rank)
+    unpacked = unpack_weights(near[0][...], senders, rows, lane)
     for fetch in fetches:
         fetch.wait()
     first, second = 0.0, 0.0
@@ -132,7 +134,7 @@
     return [pltpu.with_memory_space_constraint(a, space) for a in arrays]
 
 
-def kernel(body, results, near, late=(), flops=0, space=pltpu.HBM):
+def kernel(body, results, near, late=(), flops=0):
     def run(*refs):
         at, parts = 0, []
         for size in (len(near), len(late), len(results), len(late)):
@@ -151,7 +153,7 @@
     scratch = [pltpu.VMEM(a.shape, a.dtype) for a in late]
     call = pl.pallas_call(
         run,
-        out_shape=tuple(space(shape, dtype) for shape, dtype in results),
+        out_shape=tuple(pltpu.HBM(shape, dtype) for shape, dtype in results),
         in_specs=[spec] * len(near) + [pl.BlockSpec(memory_space=pltpu.HBM)] * len(late),
         out_specs=(spec,) * len(results),
         scratch_shapes=scratch + [pltpu.SemaphoreType.DMA((max(1, len(late)),))],
@@ -176,19 +178,20 @@
     tokens = images.shape[2]
     rank = right_up.shape[1]
     senders = lax.axis_size(DP)
-    blocks = 2 * up_weight_t.shape[1] // rank
     shards = (up_weight_t, down_weight_t, left_up, right_down)
-    size = (senders, blocks * 8, rank)
-    (copies,) = kernel(pack_weights, [(size, bf16)], (), shards, space=jax.ShapeDtypeStruct)
+    rows = up_weight_t.shape[0]
+    blocks = -(-rows * sum(shard.shape[1] for shard in shards) // (8 * lane))
+    size = (senders, blocks * 8, lane)
+    (copies,) = kernel(pack_weights, [(size, bf16)], (), shards)
     gathered = lax.all_to_all(copies, DP, 0, 0, tiled=True)
-    gathered = gathered.reshape(senders, blocks, 8, rank).transpose(0, 2, 1, 3)
-    gathered = gathered.reshape(senders * 8, blocks * rank)
+    gathered = gathered.reshape(senders, blocks, 8, lane).transpose(0, 2, 1, 3)
+    gathered = gathered.reshape(senders * 8, blocks * lane)
     mine = jnp.stack([pad_rows(images), pad_rows(out_grads)])
     far, below, above = (neighbour(mine, shift) for shift in (2, 1, -1))
     partners = lax.ppermute(gathered, "core", [(0, 1), (1, 0)])
     groups = (mine, below, above, far)
     size = (len(groups), mine.shape[1], rank)
-    half = functools.partial(first_half, senders, rank)
+    half = functools.partial(first_half, senders, rows)
     sums = kernel(
         half,
         [(size, f32), (size, bf16)] * 2,
@@ -197,7 +200,7 @@
         flops=2 * 10**9,
     )
     all_augs = lax.axis_size(AUG)
-    half = functools.partial(second_half, senders, rank)
+    half = functools.partial(second_half, senders, rows)
     size = (all_augs, 2, rank, rank)
     (terms,) = kernel(
         half, [(size, bf16)], (partners, *groups), sums, flops=2 * 10**9

time: 151 us -> 149 us (0.987)
  blocking collectives: 84.4 us -> 81.4 us
    all_to_all x1, blocking collectives: 57.2 us -> 54.7 us  [local(): gathered = lax.all_to_all(copies, DP, 0, 0, tiled=True)]
where the time goes in v4:
time: 149 us; the launch traced here: 148 us
  blocking collectives  81.4 us (55%)
  waiting for transfers between devices  34 us (23%)
  starting transfers between devices  15.9 us (11%)
  Pallas kernels  12.9 us (9%)
  between operations  2.6 us (2%)
    all_to_all x1, blocking collectives, local(): gathered = lax.all_to_all(copies, DP, 0, 0, tiled=True)  54.7 us
    all_to_all x2, blocking collectives, copy_for_each(): lax.all_to_all(jnp.broadcast_to(shard[None], (size, *shard.shape)), axis,...  26.7 us
    ppermute x3, waiting for transfers between devices, neighbour(): return lax.ppermute(array, 'x', [(i, (i + shift) % 4) for i in range(4)])  25.2 us
    pallas_call x3, Pallas kernels, kernel(): return call(*held(near, pltpu.VMEM), *held(late, pltpu.HBM))  12.9 us
    ppermute x3, starting transfers between devices, neighbour(): return lax.ppermute(array, 'x', [(i, (i + shift) % 4) for i in range(4)])  9.88 us
    all_to_all x1, waiting for transfers between devices, local(): lax.all_to_all(terms, AUG, 0, 0, tiled=True).astype(f32).sum(axis=0)  8.86 us
    all_to_all x1, starting transfers between devices, local(): lax.all_to_all(terms, AUG, 0, 0, tiled=True).astype(f32).sum(axis=0)  4.14 us
  transfers between devices with their start and end apart: 5, of which 4 were waited for; matrix products, arithmetic and copies ran while one was open for 0% of the time, Pallas kernels for 4%

profile of v4, /device:TPU:2, one launch (start us, length us, event | category | flops | bytes accessed | tf_op | source)
XLA Modules:
  0.0 148.4 jit_solution(12165156102626424064)
XLA Ops:
  0.6 2.0 %shard_map.104 = bf16[64,88,128]{2,1,0:T(8,128)(2,1)} custom-call(bf16[6,768]{1,0:T(8,128)(2,1)} %refs_0_.1, bf16[6,768]{1,0:T(8,128)(2,1)} %refs_1_.1, bf16[6,128]{1,0:T(8,128)(2,1)} %refs_2_.1, bf16[6,128]{1,0:T(8,128)(2,1)} %refs_3_.1), custom_call_target="tpu_custom_call" | custom-call | bytes 1000000 | tf_op jit(solution)/shard_map/pallas_call | solution.py:163
  2.6 0.0 copy-start
  2.6 0.0 copy-start.1
  2.6 54.7 %all_to_all.20 = bf16[64,88,128]{2,1,0:T(8,128)(2,1)S(1)} all-to-all(bf16[64,88,128]{2,1,0:T(8,128)(2,1)} %shard_map.104), channel_id=1, replica_groups=mesh['dp_0'=8,'dp_1'=8,'x'=4,'core'=2] {'dp_0','dp_1'}, dimensions={0} | all-to-all | bytes 2883584 | tf_op jit(solution)/shard_map/all_to_all | solution.py:186
  57.4 1.9 %collective-permute-start = (bf16[512,1408]{1,0:T(8,128)(2,1)S(1)}, bf16[512,1408]{1,0:T(8,128)(2,1)S(1)}, u32[]{:S(2)}, u32[]{:S(2)}) collective-permute-start(bf16[512,1408]{1,0:T(8,128)(2,1)S(1)} %bitcast.12), channel_id=1, source_target_pairs={{0,1},{1,0},{2,3},{3,2},{4,5},{5,4},{6,7},{7,6},{8,9},{9,8},{10,11... | collective-permute-start | bytes 4325384 | tf_op jit(solution)/shard_map/ppermute | solution.py:191
  59.3 0.0 copy-done
  59.3 0.0 copy-done.1
  59.3 0.1 pad_bitcast_fusion
  59.4 0.1 pad_maximum_fusion.refs_1_
  59.5 3.4 %collective-permute-start.1 = (bf16[2,200,768]{2,1,0:T(8,128)(2,1)S(1)}, bf16[2,200,768]{2,1,0:T(8,128)(2,1)S(1)}, u32[]{:S(2)}, u32[]{:S(2)}) collective-permute-start(bf16[2,200,768]{2,1,0:T(8,128)(2,1)S(1)} %pad_maximum_fusion.refs_1_), channel_id=1, source_target_pairs={{0,2},{2,4},{4,6},{6,0},{1,3},{3,5},{5,7},{7,1},{8,10},{10,12},{12... | collective-permute-start | bytes 1843208 | tf_op jit(solution)/shard_map/ppermute | solution.py:167
  62.9 2.4 %collective-permute-start.2 = (bf16[2,200,768]{2,1,0:T(8,128)(2,1)S(1)}, bf16[2,200,768]{2,1,0:T(8,128)(2,1)S(1)}, u32[]{:S(2)}, u32[]{:S(2)}) collective-permute-start(bf16[2,200,768]{2,1,0:T(8,128)(2,1)S(1)} %pad_maximum_fusion.refs_1_), channel_id=1, source_target_pairs={{0,6},{2,0},{4,2},{6,4},{1,7},{3,1},{5,3},{7,5},{8,14},{10,8},{12,... | collective-permute-start | bytes 1843208 | tf_op jit(solution)/shard_map/ppermute | solution.py:167
  65.3 4.0 %collective-permute-start.3 = (bf16[2,200,768]{2,1,0:T(8,128)(2,1)S(1)}, bf16[2,200,768]{2,1,0:T(8,128)(2,1)S(1)}, u32[]{:S(2)}, u32[]{:S(2)}) collective-permute-start(bf16[2,200,768]{2,1,0:T(8,128)(2,1)S(1)} %pad_maximum_fusion.refs_1_), channel_id=1, source_target_pairs={{0,4},{2,6},{4,0},{6,2},{1,5},{3,7},{5,1},{7,3},{8,12},{10,14},{12... | collective-permute-start | bytes 1843208 | tf_op jit(solution)/shard_map/ppermute | solution.py:167
  69.4 8.7 %collective-permute-done.1.refs_2_ = bf16[2,200,768]{2,1,0:T(8,128)(2,1)S(1)} collective-permute-done((bf16[2,200,768]{2,1,0:T(8,128)(2,1)S(1)}, bf16[2,200,768]{2,1,0:T(8,128)(2,1)S(1)}, u32[]{:S(2)}, u32[]{:S(2)}) %collective-permute-start.1) | collective-permute-done | bytes 614432 | tf_op jit(solution)/shard_map/ppermute | solution.py:167
  78.1 2.8 %collective-permute-done.2.refs_3_ = bf16[2,200,768]{2,1,0:T(8,128)(2,1)S(1)} collective-permute-done((bf16[2,200,768]{2,1,0:T(8,128)(2,1)S(1)}, bf16[2,200,768]{2,1,0:T(8,128)(2,1)S(1)}, u32[]{:S(2)}, u32[]{:S(2)}) %collective-permute-start.2) | collective-permute-done | bytes 614432 | tf_op jit(solution)/shard_map/ppermute | solution.py:167
  80.8 13.7 %collective-permute-done.3.refs_4_ = bf16[2,200,768]{2,1,0:T(8,128)(2,1)S(1)} collective-permute-done((bf16[2,200,768]{2,1,0:T(8,128)(2,1)S(1)}, bf16[2,200,768]{2,1,0:T(8,128)(2,1)S(1)}, u32[]{:S(2)}, u32[]{:S(2)}) %collective-permute-start.3) | collective-permute-done | bytes 614432 | tf_op jit(solution)/shard_map/ppermute | solution.py:167
  94.5 5.5 %shard_map.105 = (f32[4,200,128]{2,1,0:T(8,128)}, bf16[4,200,128]{2,1,0:T(8,128)(2,1)}, f32[4,200,128]{2,1,0:T(8,128)}, bf16[4,200,128]{2,1,0:T(8,128)(2,1)}) custom-call(bf16[512,1408]{1,0:T(8,128)(2,1)S(1)} %bitcast.13, bf16[2,200,768]{2,1,0:T(8,128)(2,1)S(1)} %pad_maximum_fusion.refs_1_, bf16[2,200,768]{2,1,0:T(8,128)(2,1)S(1)} %collective-permute-done.1.refs_2_, ...), custom_call_target="tpu_custom_call" | custom-call | flops 2000000000 | bytes 1000000 | tf_op jit(solution)/shard_map/pallas_call | solution.py:163
  100.0 0.0 collective-permute-done.refs_0_
  100.0 5.5 %shard_map.106 = bf16[8,2,128,128]{3,2,1,0:T(8,128)(2,1)} custom-call(bf16[512,1408]{1,0:T(8,128)(2,1)S(1)} %collective-permute-done.refs_0_, bf16[2,200,768]{2,1,0:T(8,128)(2,1)S(1)} %pad_maximum_fusion.refs_1_, bf16[2,200,768]{2,1,0:T(8,128)(2,1)S(1)} %collective-permute-done.1.refs_2_, bf16[2,200,768]{2,1,0:T(8,128)(2,1)S(1)} %collective-permute-done.2.refs_3_, ...), custom_call_target="tpu_custom_call" | custom-call | flops 2000000000 | bytes 1000000 | tf_op jit(solution)/shard_map/pallas_call | solution.py:163
  105.5 0.0 copy-start.2
  105.5 4.1 %all-to-all-start.1 = ((bf16[8,2,128,128]{3,2,1,0:T(8,128)(2,1)}), bf16[8,2,128,128]{3,2,1,0:T(8,128)(2,1)S(1)}, u32[]{:S(2)}, u32[]{:S(2)}) async-start(bf16[8,2,128,128]{3,2,1,0:T(8,128)(2,1)} %shard_map.106), calls=%async_computation.1 | async-start | bytes 1048576 | tf_op jit(solution)/shard_map/all_to_all | solution.py:210
  109.7 8.9 %all-to-all-done.1 = bf16[8,2,128,128]{3,2,1,0:T(8,128)(2,1)S(1)} async-done(((bf16[8,2,128,128]{3,2,1,0:T(8,128)(2,1)}), bf16[8,2,128,128]{3,2,1,0:T(8,128)(2,1)S(1)}, u32[]{:S(2)}, u32[]{:S(2)}) %all-to-all-start.1) | async-done | bytes 524320 | tf_op jit(solution)/shard_map/all_to_all | solution.py:210
  118.5 0.1 convert_reduce_fusion
  118.6 0.6 multiply_reduce_fusion
  120.0 13.7 %all_to_all.21 = f32[8,2,16,128]{3,2,1,0:T(8,128)S(1)} all-to-all(f32[8,2,16,128]{3,2,1,0:T(8,128)S(1)} %broadcast_in_dim.4), channel_id=1, replica_groups=mesh['dp_0'=8,'dp_1'=8,'x'=4,'core'=2] {'dp_0'}, dimensions={0} | all-to-all | bytes 262144 | tf_op jit(solution)/shard_map/all_to_all | solution.py:28
  133.6 13.0 %all_to_all.22 = f32[8,2,16,128]{3,2,1,0:T(8,128)S(1)} all-to-all(f32[8,2,16,128]{3,2,1,0:T(8,128)S(1)} %broadcast_in_dim.5), channel_id=1, replica_groups=mesh['dp_0'=8,'dp_1'=8,'x'=4,'core'=2] {'dp_1'}, dimensions={0} | all-to-all | bytes 262144 | tf_op jit(solution)/shard_map/all_to_all | solution.py:28
  146.7 0.0 copy-done.2
  146.7 0.6 add_multiply_fusion
  (5 shorter events, 0.1 us)
Async XLA Ops:
  2.6 56.7 %copy-start = (bf16[1,1,197,768]{3,2,1,0:T(8,128)(2,1)S(1)}, bf16[1,1,197,768]{3,2,1,0:T(8,128)(2,1)}, u32[]{:S(2)}) copy-start(bf16[1,1,197,768]{3,2,1,0:T(8,128)(2,1)} %param.10) | copy-start | bytes 907780
  2.6 56.7 %copy-start.1 = (bf16[1,1,197,768]{3,2,1,0:T(8,128)(2,1)S(1)}, bf16[1,1,197,768]{3,2,1,0:T(8,128)(2,1)}, u32[]{:S(2)}) copy-start(bf16[1,1,197,768]{3,2,1,0:T(8,128)(2,1)} %param.9) | copy-start | bytes 907780
  57.4 42.6 %collective-permute-start = (bf16[512,1408]{1,0:T(8,128)(2,1)S(1)}, bf16[512,1408]{1,0:T(8,128)(2,1)S(1)}, u32[]{:S(2)}, u32[]{:S(2)}) collective-permute-start(bf16[512,1408]{1,0:T(8,128)(2,1)S(1)} %bitcast.12), channel_id=1, source_target_pairs={{0,1},{1,0},{2,3},{3,2},{4,5},{5,4},{6,7},{7,6},{8,9},{9,8},{10,11... | collective-permute-start | bytes 4325384 | tf_op jit(solution)/shard_map/ppermute | solution.py:191
  59.5 18.6 %collective-permute-start.1 = (bf16[2,200,768]{2,1,0:T(8,128)(2,1)S(1)}, bf16[2,200,768]{2,1,0:T(8,128)(2,1)S(1)}, u32[]{:S(2)}, u32[]{:S(2)}) collective-permute-start(bf16[2,200,768]{2,1,0:T(8,128)(2,1)S(1)} %pad_maximum_fusion.refs_1_), channel_id=1, source_target_pairs={{0,2},{2,4},{4,6},{6,0},{1,3},{3,5},{5,7},{7,1},{8,10},{10,12},{12... | collective-permute-start | bytes 1843208 | tf_op jit(solution)/shard_map/ppermute | solution.py:167
  62.9 18.0 %collective-permute-start.2 = (bf16[2,200,768]{2,1,0:T(8,128)(2,1)S(1)}, bf16[2,200,768]{2,1,0:T(8,128)(2,1)S(1)}, u32[]{:S(2)}, u32[]{:S(2)}) collective-permute-start(bf16[2,200,768]{2,1,0:T(8,128)(2,1)S(1)} %pad_maximum_fusion.refs_1_), channel_id=1, source_target_pairs={{0,6},{2,0},{4,2},{6,4},{1,7},{3,1},{5,3},{7,5},{8,14},{10,8},{12,... | collective-permute-start | bytes 1843208 | tf_op jit(solution)/shard_map/ppermute | solution.py:167
  65.3 29.2 %collective-permute-start.3 = (bf16[2,200,768]{2,1,0:T(8,128)(2,1)S(1)}, bf16[2,200,768]{2,1,0:T(8,128)(2,1)S(1)}, u32[]{:S(2)}, u32[]{:S(2)}) collective-permute-start(bf16[2,200,768]{2,1,0:T(8,128)(2,1)S(1)} %pad_maximum_fusion.refs_1_), channel_id=1, source_target_pairs={{0,4},{2,6},{4,0},{6,2},{1,5},{3,7},{5,1},{7,3},{8,12},{10,14},{12... | collective-permute-start | bytes 1843208 | tf_op jit(solution)/shard_map/ppermute | solution.py:167
  105.5 41.2 %copy-start.2 = (f32[2,16,128]{2,1,0:T(8,128)S(1)}, f32[2,16,128]{2,1,0:T(8,128)}, u32[]{:S(2)}) copy-start(f32[2,16,128]{2,1,0:T(8,128)} %param.17) | copy-start | bytes 49156
  105.5 13.0 %all-to-all-start.1 = ((bf16[8,2,128,128]{3,2,1,0:T(8,128)(2,1)}), bf16[8,2,128,128]{3,2,1,0:T(8,128)(2,1)S(1)}, u32[]{:S(2)}, u32[]{:S(2)}) async-start(bf16[8,2,128,128]{3,2,1,0:T(8,128)(2,1)} %shard_map.106), calls=%async_computation.1 | async-start | bytes 1048576 | tf_op jit(solution)/shard_map/all_to_all | solution.py:210

commit v5 on v4

--- a/solution.py
+++ b/solution.py
@@ -101,31 +101,23 @@
     return v_up, u_down
 
 
-def first_half(senders, rows, near, late, fetches, results):
-    right_up, left_down = late
-    v_up, u_up, u_down, v_down = results
-    unpacked = unpack_weights(near[0][...], senders, rows, lane)
-    for fetch in fetches:
-        fetch.wait()
-    for k, group in enumerate(near[1:]):
-        v_up[k], u_down[k] = through_units(group[0], group[1], unpacked)
-        u_up[k] = contract(group[0], right_up[...], ((1,), (0,))).astype(bf16)
-        v_down[k] = contract(group[1], left_down[...], ((1,), (0,))).astype(bf16)
-
-
-def second_half(senders, rows, near, late, fetches, results):
-    v_up, u_up, u_down, v_down = late
+def all_units(senders, rows, near, late, fetches, results):
+    weights, *groups = near
+    right_up, left_down, *others = late
     (terms,) = results
-    unpacked = unpack_weights(near[0][...], senders, rows, lane)
-    for fetch in fetches:
+    unpacked = unpack_weights(weights[...], senders, rows, lane)
+    for fetch in fetches[:2]:
         fetch.wait()
     first, second = 0.0, 0.0
-    for k, group in enumerate(near[1:]):
-        v_up_rest, u_down_rest = through_units(group[0], group[1], unpacked)
-        v_up_all = (v_up[k] + v_up_rest).astype(bf16)
-        u_down_all = (u_down[k] + u_down_rest).astype(bf16)
-        first += contract(v_up_all, u_up[k], ((0,), (0,)))
-        second += contract(v_down[k], u_down_all, ((0,), (0,)))
+    for k, group in enumerate((*groups, *others)):
+        if k >= len(groups):
+            fetches[2 + k - len(groups)].wait()
+        token_rows, grad_rows = group[0], group[1]
+        v_up, u_down = through_units(token_rows, grad_rows, unpacked)
+        u_up = contract(token_rows, right_up[...], ((1,), (0,))).astype(bf16)
+        v_down = contract(grad_rows, left_down[...], ((1,), (0,))).astype(bf16)
+        first += contract(v_up.astype(bf16), u_up, ((0,), (0,)))
+        second += contract(v_down, u_down.astype(bf16), ((0,), (0,)))
     both = jnp.stack([first, second]).astype(bf16)
     terms[...] = jnp.broadcast_to(both[None], terms.shape)
 
@@ -188,23 +180,13 @@
     gathered = gathered.reshape(senders * 8, blocks * lane)
     mine = jnp.stack([pad_rows(images), pad_rows(out_grads)])
     far, below, above = (neighbour(mine, shift) for shift in (2, 1, -1))
-    partners = lax.ppermute(gathered, "core", [(0, 1), (1, 0)])
-    groups = (mine, below, above, far)
-    size = (len(groups), mine.shape[1], rank)
-    half = functools.partial(first_half, senders, rows)
-    sums = kernel(
-        half,
-        [(size, f32), (size, bf16)] * 2,
-        (gathered, *groups),
-        (right_up, left_down),
-        flops=2 * 10**9,
-    )
+    swapped = [lax.ppermute(g, "core", [(0, 1), (1, 0)]) for g in (mine, below, above, far)]
     all_augs = lax.axis_size(AUG)
-    half = functools.partial(second_half, senders, rows)
+    units = functools.partial(all_units, senders, rows)
     size = (all_augs, 2, rank, rank)
-    (terms,) = kernel(
-        half, [(size, bf16)], (partners, *groups), sums, flops=2 * 10**9
-    )
+    near = (gathered, mine, below, above)
+    late = (right_up, left_down, far, *swapped)
+    (terms,) = kernel(units, [(size, bf16)], near, late, flops=4 * 10**9)
     share_rows = rank // all_augs
     lower_row = lax.axis_index(AUG) * share_rows
     aug_mean = lax.all_to_all(terms, AUG, 0, 0, tiled=True).astype(f32).sum(axis=0) / all_augs

time: 149 us -> 118 us (0.79)
  blocking collectives: 81.4 us -> 31 us
  starting transfers between devices: 15.9 us -> 40.6 us
  waiting for transfers between devices: 34 us -> 27.6 us
  local copies, waits for them, and re-layouts: 0.11 us -> 1.94 us
    all_to_all x1 -> x0, blocking collectives: 54.7 us -> none  [local(): gathered = lax.all_to_all(copies, DP, 0, 0, tiled=True)]
    all_to_all x0 -> x1, starting transfers between devices: none -> 16.7 us  [local(): gathered = lax.all_to_all(copies, DP, 0, 0, tiled=True)]
    ppermute x3, waiting for transfers between devices: 25.2 us -> 18.5 us  [neighbour(): return lax.ppermute(array, 'x', [(i, (i + shift) % 4) for i in range(4)])]
    ppermute x1 -> x4, starting transfers between devices: 1.91 us -> 7.65 us  [local(): lax.ppermute(g, 'core', [(0, 1), (1, 0)])]
    all_to_all x2, blocking collectives: 26.7 us -> 31 us  [copy_for_each(): lax.all_to_all(jnp.broadcast_to(shard[None], (size, *shard.shape)), axis,...]
    all_to_all x1, starting transfers between devices: 4.14 us -> 6.32 us  [local(): lax.all_to_all(terms, AUG, 0, 0, tiled=True).astype(f32).sum(axis=0)]
    unnamed x6 -> x14, local copies, waits for them, and re-layouts: 0.02 us -> 1.85 us
    pallas_call x3 -> x2, Pallas kernels: 12.9 us -> 12.1 us  [kernel(): return call(*held(near, pltpu.VMEM), *held(late, pltpu.HBM))]
  transfers between devices with their start and end apart: 5 -> 9, of which waited for: 4 -> 5; matrix products, arithmetic and copies ran while one was open for 0% -> 0% of each run, Pallas kernels for 4% -> 0%
where the time goes in v5:
time: 118 us; the launch traced here: 117 us
  starting transfers between devices  40.6 us (34%)
  blocking collectives  31 us (26%)
  waiting for transfers between devices  27.6 us (23%)
  Pallas kernels  12.1 us (10%)
  between operations  2.67 us (2%)
  local copies, waits for them, and re-layouts  1.94 us (2%)
  other arithmetic  1.41 us (1%)
    all_to_all x2, blocking collectives, copy_for_each(): lax.all_to_all(jnp.broadcast_to(shard[None], (size, *shard.shape)), axis,...  31 us
    ppermute x3, waiting for transfers between devices, neighbour(): return lax.ppermute(array, 'x', [(i, (i + shift) % 4) for i in range(4)])  18.5 us
    all_to_all x1, starting transfers between devices, local(): gathered = lax.all_to_all(copies, DP, 0, 0, tiled=True)  16.7 us
    pallas_call x2, Pallas kernels, kernel(): return call(*held(near, pltpu.VMEM), *held(late, pltpu.HBM))  12.1 us
    ppermute x3, starting transfers between devices, neighbour(): return lax.ppermute(array, 'x', [(i, (i + shift) % 4) for i in range(4)])  9.88 us
    all_to_all x1, waiting for transfers between devices, local(): lax.all_to_all(terms, AUG, 0, 0, tiled=True).astype(f32).sum(axis=0)  8.86 us
    ppermute x4, starting transfers between devices, local(): lax.ppermute(g, 'core', [(0, 1), (1, 0)])  7.65 us
    all_to_all x1, starting transfers between devices, local(): lax.all_to_all(terms, AUG, 0, 0, tiled=True).astype(f32).sum(axis=0)  6.32 us
  transfers between devices with their start and end apart: 9, of which 5 were waited for; matrix products, arithmetic and copies ran while one was open for 0% of the time, Pallas kernels for 0%

profile of v5, /device:TPU:2, one launch (start us, length us, event | category | flops | bytes accessed | tf_op | source)
XLA Modules:
  0.0 117.3 jit_solution(5512615457321618146)
XLA Ops:
  0.6 2.0 %shard_map.104 = bf16[64,88,128]{2,1,0:T(8,128)(2,1)} custom-call(bf16[6,768]{1,0:T(8,128)(2,1)} %refs_0_.1, bf16[6,768]{1,0:T(8,128)(2,1)} %refs_1_.1, bf16[6,128]{1,0:T(8,128)(2,1)} %refs_2_.1, bf16[6,128]{1,0:T(8,128)(2,1)} %refs_3_.1), custom_call_target="tpu_custom_call" | custom-call | bytes 1000000 | tf_op jit(solution)/shard_map/pallas_call | solution.py:155
  2.6 0.0 copy-start
  2.6 0.0 copy-start.1
  2.6 16.7 %all-to-all-start = ((bf16[64,88,128]{2,1,0:T(8,128)(2,1)}), bf16[64,88,128]{2,1,0:T(8,128)(2,1)S(1)}, u32[]{:S(2)}, u32[]{:S(2)}) async-start(bf16[64,88,128]{2,1,0:T(8,128)(2,1)} %shard_map.104), calls=%async_computation | async-start | bytes 2883584 | tf_op jit(solution)/shard_map/all_to_all | solution.py:178
  19.4 0.1 pad_bitcast_fusion
  19.5 0.1 pad_maximum_fusion.refs_1_
  19.5 3.4 %collective-permute-start = (bf16[2,200,768]{2,1,0:T(8,128)(2,1)S(1)}, bf16[2,200,768]{2,1,0:T(8,128)(2,1)S(1)}, u32[]{:S(2)}, u32[]{:S(2)}) collective-permute-start(bf16[2,200,768]{2,1,0:T(8,128)(2,1)S(1)} %pad_maximum_fusion.refs_1_), channel_id=1, source_target_pairs={{0,2},{2,4},{4,6},{6,0},{1,3},{3,5},{5,7},{7,1},{8,10},{10,12},{12... | collective-permute-start | bytes 1843208 | tf_op jit(solution)/shard_map/ppermute | solution.py:159
  22.9 2.4 %collective-permute-start.1 = (bf16[2,200,768]{2,1,0:T(8,128)(2,1)S(1)}, bf16[2,200,768]{2,1,0:T(8,128)(2,1)S(1)}, u32[]{:S(2)}, u32[]{:S(2)}) collective-permute-start(bf16[2,200,768]{2,1,0:T(8,128)(2,1)S(1)} %pad_maximum_fusion.refs_1_), channel_id=1, source_target_pairs={{0,6},{2,0},{4,2},{6,4},{1,7},{3,1},{5,3},{7,5},{8,14},{10,8},{12,... | collective-permute-start | bytes 1843208 | tf_op jit(solution)/shard_map/ppermute | solution.py:159
  25.4 4.0 %collective-permute-start.2 = (bf16[2,200,768]{2,1,0:T(8,128)(2,1)S(1)}, bf16[2,200,768]{2,1,0:T(8,128)(2,1)S(1)}, u32[]{:S(2)}, u32[]{:S(2)}) collective-permute-start(bf16[2,200,768]{2,1,0:T(8,128)(2,1)S(1)} %pad_maximum_fusion.refs_1_), channel_id=1, source_target_pairs={{0,4},{2,6},{4,0},{6,2},{1,5},{3,7},{5,1},{7,3},{8,12},{10,14},{12... | collective-permute-start | bytes 1843208 | tf_op jit(solution)/shard_map/ppermute | solution.py:159
  29.4 1.9 %collective-permute-start.3 = (bf16[2,200,768]{2,1,0:T(8,128)(2,1)S(1)}, bf16[2,200,768]{2,1,0:T(8,128)(2,1)S(1)}, u32[]{:S(2)}, u32[]{:S(2)}) collective-permute-start(bf16[2,200,768]{2,1,0:T(8,128)(2,1)S(1)} %pad_maximum_fusion.refs_1_), channel_id=1, source_target_pairs={{0,1},{1,0},{2,3},{3,2},{4,5},{5,4},{6,7},{7,6},{8,9},{9,8},{10,11... | collective-permute-start | bytes 1843208 | tf_op jit(solution)/shard_map/ppermute | solution.py:183
  31.4 6.8 %collective-permute-done.refs_2_ = bf16[2,200,768]{2,1,0:T(8,128)(2,1)S(1)} collective-permute-done((bf16[2,200,768]{2,1,0:T(8,128)(2,1)S(1)}, bf16[2,200,768]{2,1,0:T(8,128)(2,1)S(1)}, u32[]{:S(2)}, u32[]{:S(2)}) %collective-permute-start) | collective-permute-done | bytes 614432 | tf_op jit(solution)/shard_map/ppermute | solution.py:159
  38.1 1.9 %collective-permute-start.4 = (bf16[2,200,768]{2,1,0:T(8,128)(2,1)S(1)}, bf16[2,200,768]{2,1,0:T(8,128)(2,1)S(1)}, u32[]{:S(2)}, u32[]{:S(2)}) collective-permute-start(bf16[2,200,768]{2,1,0:T(8,128)(2,1)S(1)} %collective-permute-done.refs_2_), channel_id=1, source_target_pairs={{0,1},{1,0},{2,3},{3,2},{4,5},{5,4},{6,7},{7,6},{8,9},{9,8},{10,11... | collective-permute-start | bytes 1843208 | tf_op jit(solution)/shard_map/ppermute | solution.py:183
  40.1 0.9 collective-permute-done.1.refs_3_
  40.9 1.9 %collective-permute-start.5 = (bf16[2,200,768]{2,1,0:T(8,128)(2,1)S(1)}, bf16[2,200,768]{2,1,0:T(8,128)(2,1)S(1)}, u32[]{:S(2)}, u32[]{:S(2)}) collective-permute-start(bf16[2,200,768]{2,1,0:T(8,128)(2,1)S(1)} %collective-permute-done.1.refs_3_), channel_id=1, source_target_pairs={{0,1},{1,0},{2,3},{3,2},{4,5},{5,4},{6,7},{7,6},{8,9},{9,8},{10,11... | collective-permute-start | bytes 1843208 | tf_op jit(solution)/shard_map/ppermute | solution.py:183
  42.8 10.8 %collective-permute-done.2.refs_6_ = bf16[2,200,768]{2,1,0:T(8,128)(2,1)S(1)} collective-permute-done((bf16[2,200,768]{2,1,0:T(8,128)(2,1)S(1)}, bf16[2,200,768]{2,1,0:T(8,128)(2,1)S(1)}, u32[]{:S(2)}, u32[]{:S(2)}) %collective-permute-start.2) | collective-permute-done | bytes 614432 | tf_op jit(solution)/shard_map/ppermute | solution.py:159
  53.7 1.9 %collective-permute-start.6 = (bf16[2,200,768]{2,1,0:T(8,128)(2,1)S(1)}, bf16[2,200,768]{2,1,0:T(8,128)(2,1)}, u32[]{:S(2)}, u32[]{:S(2)}) collective-permute-start(bf16[2,200,768]{2,1,0:T(8,128)(2,1)S(1)} %collective-permute-done.2.refs_6_), channel_id=1, source_target_pairs={{0,1},{1,0},{2,3},{3,2},{4,5},{5,4},{6,7},{7,6},{8,9},{9,8},{10,11... | collective-permute-start | bytes 1843208 | tf_op jit(solution)/shard_map/ppermute | solution.py:183
  55.6 0.0 collective-permute-done.3.refs_7_
  55.6 0.0 collective-permute-done.4.refs_8_
  55.6 0.0 collective-permute-done.5.refs_9_
  55.6 0.8 copy-done.4
  56.4 0.2 copy-done.5
  56.6 0.8 copy-done.6
  57.5 0.2 collective-permute-done.6.refs_10_
  57.7 10.1 %shard_map.105 = bf16[8,2,128,128]{3,2,1,0:T(8,128)(2,1)} custom-call(bf16[512,1408]{1,0:T(8,128)(2,1)S(1)} %bitcast.12, bf16[2,200,768]{2,1,0:T(8,128)(2,1)S(1)} %pad_maximum_fusion.refs_1_, bf16[2,200,768]{2,1,0:T(8,128)(2,1)S(1)} %collective-permute-done.refs_2_, bf16[2,200,768]{2,1,0:T(8,128)(2,1)S(1)} %collective-permute-done.1.refs_3_, ...), custom_call_target="tpu_custom_call" | custom-call | flops 4000000000 | bytes 1000000 | tf_op jit(solution)/shard_map/pallas_call | solution.py:155
  67.9 0.0 copy-start.2
  67.9 6.3 %all-to-all-start.1 = ((bf16[8,2,128,128]{3,2,1,0:T(8,128)(2,1)}), bf16[8,2,128,128]{3,2,1,0:T(8,128)(2,1)S(1)}, u32[]{:S(2)}, u32[]{:S(2)}) async-start(bf16[8,2,128,128]{3,2,1,0:T(8,128)(2,1)} %shard_map.105), calls=%async_computation.1 | async-start | bytes 1048576 | tf_op jit(solution)/shard_map/all_to_all | solution.py:192
  74.2 8.9 %all-to-all-done.1 = bf16[8,2,128,128]{3,2,1,0:T(8,128)(2,1)S(1)} async-done(((bf16[8,2,128,128]{3,2,1,0:T(8,128)(2,1)}), bf16[8,2,128,128]{3,2,1,0:T(8,128)(2,1)S(1)}, u32[]{:S(2)}, u32[]{:S(2)}) %all-to-all-start.1) | async-done | bytes 524320 | tf_op jit(solution)/shard_map/all_to_all | solution.py:192
  83.1 0.1 convert_reduce_fusion
  83.1 0.6 multiply_reduce_fusion
  84.5 15.5 %all_to_all.20 = f32[8,2,16,128]{3,2,1,0:T(8,128)S(1)} all-to-all(f32[8,2,16,128]{3,2,1,0:T(8,128)S(1)} %broadcast_in_dim.4), channel_id=1, replica_groups=mesh['dp_0'=8,'dp_1'=8,'x'=4,'core'=2] {'dp_0'}, dimensions={0} | all-to-all | bytes 262144 | tf_op jit(solution)/shard_map/all_to_all | solution.py:28
  100.0 15.5 %all_to_all.21 = f32[8,2,16,128]{3,2,1,0:T(8,128)S(1)} all-to-all(f32[8,2,16,128]{3,2,1,0:T(8,128)S(1)} %broadcast_in_dim.5), channel_id=1, replica_groups=mesh['dp_0'=8,'dp_1'=8,'x'=4,'core'=2] {'dp_1'}, dimensions={0} | all-to-all | bytes 262144 | tf_op jit(solution)/shard_map/all_to_all | solution.py:28
  115.5 0.6 add_multiply_fusion
  (14 shorter events, 0.1 us)
Async XLA Ops:
  2.6 16.8 %copy-start = (bf16[1,1,197,768]{3,2,1,0:T(8,128)(2,1)S(1)}, bf16[1,1,197,768]{3,2,1,0:T(8,128)(2,1)}, u32[]{:S(2)}) copy-start(bf16[1,1,197,768]{3,2,1,0:T(8,128)(2,1)} %param.10) | copy-start | bytes 907780
  2.6 16.8 %copy-start.1 = (bf16[1,1,197,768]{3,2,1,0:T(8,128)(2,1)S(1)}, bf16[1,1,197,768]{3,2,1,0:T(8,128)(2,1)}, u32[]{:S(2)}) copy-start(bf16[1,1,197,768]{3,2,1,0:T(8,128)(2,1)} %param.9) | copy-start | bytes 907780
  2.6 55.1 %all-to-all-start = ((bf16[64,88,128]{2,1,0:T(8,128)(2,1)}), bf16[64,88,128]{2,1,0:T(8,128)(2,1)S(1)}, u32[]{:S(2)}, u32[]{:S(2)}) async-start(bf16[64,88,128]{2,1,0:T(8,128)(2,1)} %shard_map.104), calls=%async_computation | async-start | bytes 2883584 | tf_op jit(solution)/shard_map/all_to_all | solution.py:178
  19.5 18.6 %collective-permute-start = (bf16[2,200,768]{2,1,0:T(8,128)(2,1)S(1)}, bf16[2,200,768]{2,1,0:T(8,128)(2,1)S(1)}, u32[]{:S(2)}, u32[]{:S(2)}) collective-permute-start(bf16[2,200,768]{2,1,0:T(8,128)(2,1)S(1)} %pad_maximum_fusion.refs_1_), channel_id=1, source_target_pairs={{0,2},{2,4},{4,6},{6,0},{1,3},{3,5},{5,7},{7,1},{8,10},{10,12},{12... | collective-permute-start | bytes 1843208 | tf_op jit(solution)/shard_map/ppermute | solution.py:159
  22.9 18.0 %collective-permute-start.1 = (bf16[2,200,768]{2,1,0:T(8,128)(2,1)S(1)}, bf16[2,200,768]{2,1,0:T(8,128)(2,1)S(1)}, u32[]{:S(2)}, u32[]{:S(2)}) collective-permute-start(bf16[2,200,768]{2,1,0:T(8,128)(2,1)S(1)} %pad_maximum_fusion.refs_1_), channel_id=1, source_target_pairs={{0,6},{2,0},{4,2},{6,4},{1,7},{3,1},{5,3},{7,5},{8,14},{10,8},{12,... | collective-permute-start | bytes 1843208 | tf_op jit(solution)/shard_map/ppermute | solution.py:159
  25.4 28.3 %collective-permute-start.2 = (bf16[2,200,768]{2,1,0:T(8,128)(2,1)S(1)}, bf16[2,200,768]{2,1,0:T(8,128)(2,1)S(1)}, u32[]{:S(2)}, u32[]{:S(2)}) collective-permute-start(bf16[2,200,768]{2,1,0:T(8,128)(2,1)S(1)} %pad_maximum_fusion.refs_1_), channel_id=1, source_target_pairs={{0,4},{2,6},{4,0},{6,2},{1,5},{3,7},{5,1},{7,3},{8,12},{10,14},{12... | collective-permute-start | bytes 1843208 | tf_op jit(solution)/shard_map/ppermute | solution.py:159
  29.4 26.2 %collective-permute-start.3 = (bf16[2,200,768]{2,1,0:T(8,128)(2,1)S(1)}, bf16[2,200,768]{2,1,0:T(8,128)(2,1)S(1)}, u32[]{:S(2)}, u32[]{:S(2)}) collective-permute-start(bf16[2,200,768]{2,1,0:T(8,128)(2,1)S(1)} %pad_maximum_fusion.refs_1_), channel_id=1, source_target_pairs={{0,1},{1,0},{2,3},{3,2},{4,5},{5,4},{6,7},{7,6},{8,9},{9,8},{10,11... | collective-permute-start | bytes 1843208 | tf_op jit(solution)/shard_map/ppermute | solution.py:183
  38.1 17.5 %collective-permute-start.4 = (bf16[2,200,768]{2,1,0:T(8,128)(2,1)S(1)}, bf16[2,200,768]{2,1,0:T(8,128)(2,1)S(1)}, u32[]{:S(2)}, u32[]{:S(2)}) collective-permute-start(bf16[2,200,768]{2,1,0:T(8,128)(2,1)S(1)} %collective-permute-done.refs_2_), channel_id=1, source_target_pairs={{0,1},{1,0},{2,3},{3,2},{4,5},{5,4},{6,7},{7,6},{8,9},{9,8},{10,11... | collective-permute-start | bytes 1843208 | tf_op jit(solution)/shard_map/ppermute | solution.py:183
  40.9 14.7 %collective-permute-start.5 = (bf16[2,200,768]{2,1,0:T(8,128)(2,1)S(1)}, bf16[2,200,768]{2,1,0:T(8,128)(2,1)S(1)}, u32[]{:S(2)}, u32[]{:S(2)}) collective-permute-start(bf16[2,200,768]{2,1,0:T(8,128)(2,1)S(1)} %collective-permute-done.1.refs_3_), channel_id=1, source_target_pairs={{0,1},{1,0},{2,3},{3,2},{4,5},{5,4},{6,7},{7,6},{8,9},{9,8},{10,11... | collective-permute-start | bytes 1843208 | tf_op jit(solution)/shard_map/ppermute | solution.py:183
  53.7 2.0 %copy-start.3 = (bf16[2,200,768]{2,1,0:T(8,128)(2,1)}, bf16[2,200,768]{2,1,0:T(8,128)(2,1)S(1)}, u32[]{:S(2)}) copy-start(bf16[2,200,768]{2,1,0:T(8,128)(2,1)S(1)} %collective-permute-done.2.refs_6_) | copy-start | bytes 1843204
  53.7 4.1 %collective-permute-start.6 = (bf16[2,200,768]{2,1,0:T(8,128)(2,1)S(1)}, bf16[2,200,768]{2,1,0:T(8,128)(2,1)}, u32[]{:S(2)}, u32[]{:S(2)}) collective-permute-start(bf16[2,200,768]{2,1,0:T(8,128)(2,1)S(1)} %collective-permute-done.2.refs_6_), channel_id=1, source_target_pairs={{0,1},{1,0},{2,3},{3,2},{4,5},{5,4},{6,7},{7,6},{8,9},{9,8},{10,11... | collective-permute-start | bytes 1843208 | tf_op jit(solution)/shard_map/ppermute | solution.py:183
  55.6 0.8 copy-start.4
  55.6 1.0 copy-start.5
  56.6 0.8 copy-start.6
  67.9 47.7 %copy-start.2 = (f32[2,16,128]{2,1,0:T(8,128)S(1)}, f32[2,16,128]{2,1,0:T(8,128)}, u32[]{:S(2)}) copy-start(f32[2,16,128]{2,1,0:T(8,128)} %param.17) | copy-start | bytes 49156
  67.9 15.2 %all-to-all-start.1 = ((bf16[8,2,128,128]{3,2,1,0:T(8,128)(2,1)}), bf16[8,2,128,128]{3,2,1,0:T(8,128)(2,1)S(1)}, u32[]{:S(2)}, u32[]{:S(2)}) async-start(bf16[8,2,128,128]{3,2,1,0:T(8,128)(2,1)} %shard_map.105), calls=%async_computation.1 | async-start | bytes 1048576 | tf_op jit(solution)/shard_map/all_to_all | solution.py:192

commit v6 on v5

--- a/solution.py
+++ b/solution.py
@@ -179,8 +179,11 @@
     gathered = gathered.reshape(senders, blocks, 8, lane).transpose(0, 2, 1, 3)
     gathered = gathered.reshape(senders * 8, blocks * lane)
     mine = jnp.stack([pad_rows(images), pad_rows(out_grads)])
-    far, below, above = (neighbour(mine, shift) for shift in (2, 1, -1))
-    swapped = [lax.ppermute(g, "core", [(0, 1), (1, 0)]) for g in (mine, below, above, far)]
+    far = neighbour(mine, 2)
+    below, above = (neighbour(mine, shift) for shift in (1, -1))
+    swapped = []
+    for group in (mine, far, below, above):
+        swapped.append(lax.ppermute(group, "core", [(0, 1), (1, 0)]))
     all_augs = lax.axis_size(AUG)
     units = functools.partial(all_units, senders, rows)
     size = (all_augs, 2, rank, rank)

time: 118 us -> 116 us (0.983)
    all_to_all x1, starting transfers between devices: 6.32 us -> 4.77 us  [local(): lax.all_to_all(terms, AUG, 0, 0, tiled=True).astype(f32).sum(axis=0)]
  transfers between devices with their start and end apart: 9 -> 9, of which waited for: 5 -> 3; matrix products, arithmetic and copies ran while one was open for 0% -> 0% of each run, Pallas kernels for 0% -> 0%
where the time goes in v6:
time: 116 us
  starting transfers between devices  39.5 us (34%)
  blocking collectives  31 us (27%)
  waiting for transfers between devices  27.1 us (23%)
  Pallas kernels  12.1 us (10%)
  between operations  2.67 us (2%)
  local copies, waits for them, and re-layouts  1.94 us (2%)
  other arithmetic  1.41 us (1%)
    all_to_all x2, blocking collectives, copy_for_each(): lax.all_to_all(jnp.broadcast_to(shard[None], (size, *shard.shape)), axis,...  31 us
    ppermute x3, waiting for transfers between devices, neighbour(): return lax.ppermute(array, 'x', [(i, (i + shift) % 4) for i in range(4)])  18.2 us
    all_to_all x1, starting transfers between devices, local(): gathered = lax.all_to_all(copies, DP, 0, 0, tiled=True)  16.7 us
    pallas_call x2, Pallas kernels, kernel(): return call(*held(near, pltpu.VMEM), *held(late, pltpu.HBM))  12.1 us
    ppermute x3, starting transfers between devices, neighbour(): return lax.ppermute(array, 'x', [(i, (i + shift) % 4) for i in range(4)])  9.88 us
    all_to_all x1, waiting for transfers between devices, local(): lax.all_to_all(terms, AUG, 0, 0, tiled=True).astype(f32).sum(axis=0)  8.86 us
    ppermute x4, starting transfers between devices, local(): swapped.append(lax.ppermute(group, 'core', [(0, 1), (1, 0)]))  8.15 us
    all_to_all x1, starting transfers between devices, local(): lax.all_to_all(terms, AUG, 0, 0, tiled=True).astype(f32).sum(axis=0)  4.77 us
  transfers between devices with their start and end apart: 9, of which 3 were waited for; matrix products, arithmetic and copies ran while one was open for 0% of the time, Pallas kernels for 0%

profile of v6, /device:TPU:2, one launch (start us, length us, event | category | flops | bytes accessed | tf_op | source)
XLA Modules:
  0.0 115.7 jit_solution(4054779715699156764)
XLA Ops:
  0.6 2.0 %shard_map.104 = bf16[64,88,128]{2,1,0:T(8,128)(2,1)} custom-call(bf16[6,768]{1,0:T(8,128)(2,1)} %refs_0_.1, bf16[6,768]{1,0:T(8,128)(2,1)} %refs_1_.1, bf16[6,128]{1,0:T(8,128)(2,1)} %refs_2_.1, bf16[6,128]{1,0:T(8,128)(2,1)} %refs_3_.1), custom_call_target="tpu_custom_call" | custom-call | bytes 1000000 | tf_op jit(solution)/shard_map/pallas_call | solution.py:155
  2.6 0.0 copy-start
  2.6 0.0 copy-start.1
  2.6 16.7 %all-to-all-start = ((bf16[64,88,128]{2,1,0:T(8,128)(2,1)}), bf16[64,88,128]{2,1,0:T(8,128)(2,1)S(1)}, u32[]{:S(2)}, u32[]{:S(2)}) async-start(bf16[64,88,128]{2,1,0:T(8,128)(2,1)} %shard_map.104), calls=%async_computation | async-start | bytes 2883584 | tf_op jit(solution)/shard_map/all_to_all | solution.py:178
  19.4 0.1 pad_bitcast_fusion
  19.5 0.1 pad_maximum_fusion.refs_1_
  19.5 4.0 %collective-permute-start.2 = (bf16[2,200,768]{2,1,0:T(8,128)(2,1)S(1)}, bf16[2,200,768]{2,1,0:T(8,128)(2,1)S(1)}, u32[]{:S(2)}, u32[]{:S(2)}) collective-permute-start(bf16[2,200,768]{2,1,0:T(8,128)(2,1)S(1)} %pad_maximum_fusion.refs_1_), channel_id=1, source_target_pairs={{0,4},{2,6},{4,0},{6,2},{1,5},{3,7},{5,1},{7,3},{8,12},{10,14},{12... | collective-permute-start | bytes 1843208 | tf_op jit(solution)/shard_map/ppermute | solution.py:159
  23.6 1.9 %collective-permute-start = (bf16[2,200,768]{2,1,0:T(8,128)(2,1)S(1)}, bf16[2,200,768]{2,1,0:T(8,128)(2,1)S(1)}, u32[]{:S(2)}, u32[]{:S(2)}) collective-permute-start(bf16[2,200,768]{2,1,0:T(8,128)(2,1)S(1)} %pad_maximum_fusion.refs_1_), channel_id=1, source_target_pairs={{0,2},{2,4},{4,6},{6,0},{1,3},{3,5},{5,7},{7,1},{8,10},{10,12},{12... | collective-permute-start | bytes 1843208 | tf_op jit(solution)/shard_map/ppermute | solution.py:159
  25.5 3.9 %collective-permute-start.1 = (bf16[2,200,768]{2,1,0:T(8,128)(2,1)S(1)}, bf16[2,200,768]{2,1,0:T(8,128)(2,1)S(1)}, u32[]{:S(2)}, u32[]{:S(2)}) collective-permute-start(bf16[2,200,768]{2,1,0:T(8,128)(2,1)S(1)} %pad_maximum_fusion.refs_1_), channel_id=1, source_target_pairs={{0,6},{2,0},{4,2},{6,4},{1,7},{3,1},{5,3},{7,5},{8,14},{10,8},{12,... | collective-permute-start | bytes 1843208 | tf_op jit(solution)/shard_map/ppermute | solution.py:159
  29.4 1.9 %collective-permute-start.3 = (bf16[2,200,768]{2,1,0:T(8,128)(2,1)S(1)}, bf16[2,200,768]{2,1,0:T(8,128)(2,1)S(1)}, u32[]{:S(2)}, u32[]{:S(2)}) collective-permute-start(bf16[2,200,768]{2,1,0:T(8,128)(2,1)S(1)} %pad_maximum_fusion.refs_1_), channel_id=1, source_target_pairs={{0,1},{1,0},{2,3},{3,2},{4,5},{5,4},{6,7},{7,6},{8,9},{9,8},{10,11... | collective-permute-start | bytes 1843208 | tf_op jit(solution)/shard_map/ppermute | solution.py:186
  31.4 8.3 %collective-permute-done.2.refs_6_ = bf16[2,200,768]{2,1,0:T(8,128)(2,1)S(1)} collective-permute-done((bf16[2,200,768]{2,1,0:T(8,128)(2,1)S(1)}, bf16[2,200,768]{2,1,0:T(8,128)(2,1)S(1)}, u32[]{:S(2)}, u32[]{:S(2)}) %collective-permute-start.2) | collective-permute-done | bytes 614432 | tf_op jit(solution)/shard_map/ppermute | solution.py:159
  39.7 1.9 %collective-permute-start.4 = (bf16[2,200,768]{2,1,0:T(8,128)(2,1)S(1)}, bf16[2,200,768]{2,1,0:T(8,128)(2,1)S(1)}, u32[]{:S(2)}, u32[]{:S(2)}) collective-permute-start(bf16[2,200,768]{2,1,0:T(8,128)(2,1)S(1)} %collective-permute-done.2.refs_6_), channel_id=1, source_target_pairs={{0,1},{1,0},{2,3},{3,2},{4,5},{5,4},{6,7},{7,6},{8,9},{9,8},{10,11... | collective-permute-start | bytes 1843208 | tf_op jit(solution)/shard_map/ppermute | solution.py:186
  41.6 9.9 %collective-permute-done.refs_2_ = bf16[2,200,768]{2,1,0:T(8,128)(2,1)S(1)} collective-permute-done((bf16[2,200,768]{2,1,0:T(8,128)(2,1)S(1)}, bf16[2,200,768]{2,1,0:T(8,128)(2,1)S(1)}, u32[]{:S(2)}, u32[]{:S(2)}) %collective-permute-start) | collective-permute-done | bytes 614432 | tf_op jit(solution)/shard_map/ppermute | solution.py:159
  51.5 1.9 %collective-permute-start.5 = (bf16[2,200,768]{2,1,0:T(8,128)(2,1)S(1)}, bf16[2,200,768]{2,1,0:T(8,128)(2,1)S(1)}, u32[]{:S(2)}, u32[]{:S(2)}) collective-permute-start(bf16[2,200,768]{2,1,0:T(8,128)(2,1)S(1)} %collective-permute-done.refs_2_), channel_id=1, source_target_pairs={{0,1},{1,0},{2,3},{3,2},{4,5},{5,4},{6,7},{7,6},{8,9},{9,8},{10,11... | collective-permute-start | bytes 1843208 | tf_op jit(solution)/shard_map/ppermute | solution.py:186
  53.4 0.0 collective-permute-done.1.refs_3_
  53.4 2.4 %collective-permute-start.6 = (bf16[2,200,768]{2,1,0:T(8,128)(2,1)S(1)}, bf16[2,200,768]{2,1,0:T(8,128)(2,1)}, u32[]{:S(2)}, u32[]{:S(2)}) collective-permute-start(bf16[2,200,768]{2,1,0:T(8,128)(2,1)S(1)} %collective-permute-done.1.refs_3_), channel_id=1, source_target_pairs={{0,1},{1,0},{2,3},{3,2},{4,5},{5,4},{6,7},{7,6},{8,9},{9,8},{10,11... | collective-permute-start | bytes 1843208 | tf_op jit(solution)/shard_map/ppermute | solution.py:186
  55.8 0.0 collective-permute-done.3.refs_7_
  55.8 0.0 collective-permute-done.4.refs_8_
  55.9 0.0 collective-permute-done.5.refs_9_
  55.9 0.8 copy-done.4
  56.7 0.2 copy-done.5
  56.9 0.8 copy-done.6
  57.7 0.0 collective-permute-done.6.refs_10_
  57.7 10.1 %shard_map.105 = bf16[8,2,128,128]{3,2,1,0:T(8,128)(2,1)} custom-call(bf16[512,1408]{1,0:T(8,128)(2,1)S(1)} %bitcast.12, bf16[2,200,768]{2,1,0:T(8,128)(2,1)S(1)} %pad_maximum_fusion.refs_1_, bf16[2,200,768]{2,1,0:T(8,128)(2,1)S(1)} %collective-permute-done.refs_2_, bf16[2,200,768]{2,1,0:T(8,128)(2,1)S(1)} %collective-permute-done.1.refs_3_, ...), custom_call_target="tpu_custom_call" | custom-call | flops 4000000000 | bytes 1000000 | tf_op jit(solution)/shard_map/pallas_call | solution.py:155
  67.9 0.0 copy-start.2
  67.9 4.8 %all-to-all-start.1 = ((bf16[8,2,128,128]{3,2,1,0:T(8,128)(2,1)}), bf16[8,2,128,128]{3,2,1,0:T(8,128)(2,1)S(1)}, u32[]{:S(2)}, u32[]{:S(2)}) async-start(bf16[8,2,128,128]{3,2,1,0:T(8,128)(2,1)} %shard_map.105), calls=%async_computation.1 | async-start | bytes 1048576 | tf_op jit(solution)/shard_map/all_to_all | solution.py:195
  72.6 8.9 %all-to-all-done.1 = bf16[8,2,128,128]{3,2,1,0:T(8,128)(2,1)S(1)} async-done(((bf16[8,2,128,128]{3,2,1,0:T(8,128)(2,1)}), bf16[8,2,128,128]{3,2,1,0:T(8,128)(2,1)S(1)}, u32[]{:S(2)}, u32[]{:S(2)}) %all-to-all-start.1) | async-done | bytes 524320 | tf_op jit(solution)/shard_map/all_to_all | solution.py:195
  81.5 0.1 convert_reduce_fusion
  81.6 0.6 multiply_reduce_fusion
  82.9 15.5 %all_to_all.20 = f32[8,2,16,128]{3,2,1,0:T(8,128)S(1)} all-to-all(f32[8,2,16,128]{3,2,1,0:T(8,128)S(1)} %broadcast_in_dim.4), channel_id=1, replica_groups=mesh['dp_0'=8,'dp_1'=8,'x'=4,'core'=2] {'dp_0'}, dimensions={0} | all-to-all | bytes 262144 | tf_op jit(solution)/shard_map/all_to_all | solution.py:28
  98.4 15.5 %all_to_all.21 = f32[8,2,16,128]{3,2,1,0:T(8,128)S(1)} all-to-all(f32[8,2,16,128]{3,2,1,0:T(8,128)S(1)} %broadcast_in_dim.5), channel_id=1, replica_groups=mesh['dp_0'=8,'dp_1'=8,'x'=4,'core'=2] {'dp_1'}, dimensions={0} | all-to-all | bytes 262144 | tf_op jit(solution)/shard_map/all_to_all | solution.py:28
  114.0 0.6 add_multiply_fusion
  (14 shorter events, 0.1 us)
Async XLA Ops:
  2.6 16.8 %copy-start = (bf16[1,1,197,768]{3,2,1,0:T(8,128)(2,1)S(1)}, bf16[1,1,197,768]{3,2,1,0:T(8,128)(2,1)}, u32[]{:S(2)}) copy-start(bf16[1,1,197,768]{3,2,1,0:T(8,128)(2,1)} %param.10) | copy-start | bytes 907780
  2.6 16.8 %copy-start.1 = (bf16[1,1,197,768]{3,2,1,0:T(8,128)(2,1)S(1)}, bf16[1,1,197,768]{3,2,1,0:T(8,128)(2,1)}, u32[]{:S(2)}) copy-start(bf16[1,1,197,768]{3,2,1,0:T(8,128)(2,1)} %param.9) | copy-start | bytes 907780
  2.6 55.1 %all-to-all-start = ((bf16[64,88,128]{2,1,0:T(8,128)(2,1)}), bf16[64,88,128]{2,1,0:T(8,128)(2,1)S(1)}, u32[]{:S(2)}, u32[]{:S(2)}) async-start(bf16[64,88,128]{2,1,0:T(8,128)(2,1)} %shard_map.104), calls=%async_computation | async-start | bytes 2883584 | tf_op jit(solution)/shard_map/all_to_all | solution.py:178
  19.5 20.2 %collective-permute-start.2 = (bf16[2,200,768]{2,1,0:T(8,128)(2,1)S(1)}, bf16[2,200,768]{2,1,0:T(8,128)(2,1)S(1)}, u32[]{:S(2)}, u32[]{:S(2)}) collective-permute-start(bf16[2,200,768]{2,1,0:T(8,128)(2,1)S(1)} %pad_maximum_fusion.refs_1_), channel_id=1, source_target_pairs={{0,4},{2,6},{4,0},{6,2},{1,5},{3,7},{5,1},{7,3},{8,12},{10,14},{12... | collective-permute-start | bytes 1843208 | tf_op jit(solution)/shard_map/ppermute | solution.py:159
  23.6 27.9 %collective-permute-start = (bf16[2,200,768]{2,1,0:T(8,128)(2,1)S(1)}, bf16[2,200,768]{2,1,0:T(8,128)(2,1)S(1)}, u32[]{:S(2)}, u32[]{:S(2)}) collective-permute-start(bf16[2,200,768]{2,1,0:T(8,128)(2,1)S(1)} %pad_maximum_fusion.refs_1_), channel_id=1, source_target_pairs={{0,2},{2,4},{4,6},{6,0},{1,3},{3,5},{5,7},{7,1},{8,10},{10,12},{12... | collective-permute-start | bytes 1843208 | tf_op jit(solution)/shard_map/ppermute | solution.py:159
  25.5 27.9 %collective-permute-start.1 = (bf16[2,200,768]{2,1,0:T(8,128)(2,1)S(1)}, bf16[2,200,768]{2,1,0:T(8,128)(2,1)S(1)}, u32[]{:S(2)}, u32[]{:S(2)}) collective-permute-start(bf16[2,200,768]{2,1,0:T(8,128)(2,1)S(1)} %pad_maximum_fusion.refs_1_), channel_id=1, source_target_pairs={{0,6},{2,0},{4,2},{6,4},{1,7},{3,1},{5,3},{7,5},{8,14},{10,8},{12,... | collective-permute-start | bytes 1843208 | tf_op jit(solution)/shard_map/ppermute | solution.py:159
  29.4 26.4 %collective-permute-start.3 = (bf16[2,200,768]{2,1,0:T(8,128)(2,1)S(1)}, bf16[2,200,768]{2,1,0:T(8,128)(2,1)S(1)}, u32[]{:S(2)}, u32[]{:S(2)}) collective-permute-start(bf16[2,200,768]{2,1,0:T(8,128)(2,1)S(1)} %pad_maximum_fusion.refs_1_), channel_id=1, source_target_pairs={{0,1},{1,0},{2,3},{3,2},{4,5},{5,4},{6,7},{7,6},{8,9},{9,8},{10,11... | collective-permute-start | bytes 1843208 | tf_op jit(solution)/shard_map/ppermute | solution.py:186
  39.7 16.2 %copy-start.3 = (bf16[2,200,768]{2,1,0:T(8,128)(2,1)}, bf16[2,200,768]{2,1,0:T(8,128)(2,1)S(1)}, u32[]{:S(2)}) copy-start(bf16[2,200,768]{2,1,0:T(8,128)(2,1)S(1)} %collective-permute-done.2.refs_6_) | copy-start | bytes 1843204
  39.7 16.1 %collective-permute-start.4 = (bf16[2,200,768]{2,1,0:T(8,128)(2,1)S(1)}, bf16[2,200,768]{2,1,0:T(8,128)(2,1)S(1)}, u32[]{:S(2)}, u32[]{:S(2)}) collective-permute-start(bf16[2,200,768]{2,1,0:T(8,128)(2,1)S(1)} %collective-permute-done.2.refs_6_), channel_id=1, source_target_pairs={{0,1},{1,0},{2,3},{3,2},{4,5},{5,4},{6,7},{7,6},{8,9},{9,8},{10,11... | collective-permute-start | bytes 1843208 | tf_op jit(solution)/shard_map/ppermute | solution.py:186
  51.5 4.4 %collective-permute-start.5 = (bf16[2,200,768]{2,1,0:T(8,128)(2,1)S(1)}, bf16[2,200,768]{2,1,0:T(8,128)(2,1)S(1)}, u32[]{:S(2)}, u32[]{:S(2)}) collective-permute-start(bf16[2,200,768]{2,1,0:T(8,128)(2,1)S(1)} %collective-permute-done.refs_2_), channel_id=1, source_target_pairs={{0,1},{1,0},{2,3},{3,2},{4,5},{5,4},{6,7},{7,6},{8,9},{9,8},{10,11... | collective-permute-start | bytes 1843208 | tf_op jit(solution)/shard_map/ppermute | solution.py:186
  53.4 4.3 %collective-permute-start.6 = (bf16[2,200,768]{2,1,0:T(8,128)(2,1)S(1)}, bf16[2,200,768]{2,1,0:T(8,128)(2,1)}, u32[]{:S(2)}, u32[]{:S(2)}) collective-permute-start(bf16[2,200,768]{2,1,0:T(8,128)(2,1)S(1)} %collective-permute-done.1.refs_3_), channel_id=1, source_target_pairs={{0,1},{1,0},{2,3},{3,2},{4,5},{5,4},{6,7},{7,6},{8,9},{9,8},{10,11... | collective-permute-start | bytes 1843208 | tf_op jit(solution)/shard_map/ppermute | solution.py:186
  55.8 0.8 copy-start.4
  55.9 1.0 copy-start.5
  56.9 0.8 copy-start.6
  67.9 46.1 %copy-start.2 = (f32[2,16,128]{2,1,0:T(8,128)S(1)}, f32[2,16,128]{2,1,0:T(8,128)}, u32[]{:S(2)}) copy-start(f32[2,16,128]{2,1,0:T(8,128)} %param.17) | copy-start | bytes 49156
  67.9 13.6 %all-to-all-start.1 = ((bf16[8,2,128,128]{3,2,1,0:T(8,128)(2,1)}), bf16[8,2,128,128]{3,2,1,0:T(8,128)(2,1)S(1)}, u32[]{:S(2)}, u32[]{:S(2)}) async-start(bf16[8,2,128,128]{3,2,1,0:T(8,128)(2,1)} %shard_map.105), calls=%async_computation.1 | async-start | bytes 1048576 | tf_op jit(solution)/shard_map/all_to_all | solution.py:195

commit v7 on v6

--- a/solution.py
+++ b/solution.py
@@ -109,10 +109,11 @@
     for fetch in fetches[:2]:
         fetch.wait()
     first, second = 0.0, 0.0
-    for k, group in enumerate((*groups, *others)):
-        if k >= len(groups):
-            fetches[2 + k - len(groups)].wait()
-        token_rows, grad_rows = group[0], group[1]
+    for batch in (groups + others[:1], others[1:]):
+        for fetch in fetches[2:3] if batch[0] is groups[0] else fetches[3:]:
+            fetch.wait()
+        token_rows = jnp.concatenate([group[0] for group in batch], axis=0)
+        grad_rows = jnp.concatenate([group[1] for group in batch], axis=0)
         v_up, u_down = through_units(token_rows, grad_rows, unpacked)
         u_up = contract(token_rows, right_up[...], ((1,), (0,))).astype(bf16)
         v_down = contract(grad_rows, left_down[...], ((1,), (0,))).astype(bf16)

time: 116 us -> 114 us (0.983)
  Pallas kernels: 12.1 us -> 9.72 us
    pallas_call x2, Pallas kernels: 12.1 us -> 9.72 us  [kernel(): return call(*held(near, pltpu.VMEM), *held(late, pltpu.HBM))]
where the time goes in v7:
time: 114 us; the launch traced here: 113 us
  starting transfers between devices  39.5 us (35%)
  blocking collectives  31 us (27%)
  waiting for transfers between devices  27.1 us (24%)
  Pallas kernels  9.72 us (9%)
  between operations  2.67 us (2%)
  local copies, waits for them, and re-layouts  1.94 us (2%)
  other arithmetic  1.41 us (1%)
    all_to_all x2, blocking collectives, copy_for_each(): lax.all_to_all(jnp.broadcast_to(shard[None], (size, *shard.shape)), axis,...  31 us
    ppermute x3, waiting for transfers between devices, neighbour(): return lax.ppermute(array, 'x', [(i, (i + shift) % 4) for i in range(4)])  18.2 us
    all_to_all x1, starting transfers between devices, local(): gathered = lax.all_to_all(copies, DP, 0, 0, tiled=True)  16.7 us
    ppermute x3, starting transfers between devices, neighbour(): return lax.ppermute(array, 'x', [(i, (i + shift) % 4) for i in range(4)])  9.88 us
    pallas_call x2, Pallas kernels, kernel(): return call(*held(near, pltpu.VMEM), *held(late, pltpu.HBM))  9.72 us
    all_to_all x1, waiting for transfers between devices, local(): lax.all_to_all(terms, AUG, 0, 0, tiled=True).astype(f32).sum(axis=0)  8.86 us
    ppermute x4, starting transfers between devices, local(): swapped.append(lax.ppermute(group, 'core', [(0, 1), (1, 0)]))  8.15 us
    all_to_all x1, starting transfers between devices, local(): lax.all_to_all(terms, AUG, 0, 0, tiled=True).astype(f32).sum(axis=0)  4.76 us
  transfers between devices with their start and end apart: 9, of which 3 were waited for; matrix products, arithmetic and copies ran while one was open for 0% of the time, Pallas kernels for 0%

profile of v7, /device:TPU:2, one launch (start us, length us, event | category | flops | bytes accessed | tf_op | source)
XLA Modules:
  0.0 113.3 jit_solution(7632849730556200651)
XLA Ops:
  0.6 2.0 %shard_map.104 = bf16[64,88,128]{2,1,0:T(8,128)(2,1)} custom-call(bf16[6,768]{1,0:T(8,128)(2,1)} %refs_0_.1, bf16[6,768]{1,0:T(8,128)(2,1)} %refs_1_.1, bf16[6,128]{1,0:T(8,128)(2,1)} %refs_2_.1, bf16[6,128]{1,0:T(8,128)(2,1)} %refs_3_.1), custom_call_target="tpu_custom_call" | custom-call | bytes 1000000 | tf_op jit(solution)/shard_map/pallas_call | solution.py:156
  2.6 0.0 copy-start
  2.6 0.0 copy-start.1
  2.6 16.7 %all-to-all-start = ((bf16[64,88,128]{2,1,0:T(8,128)(2,1)}), bf16[64,88,128]{2,1,0:T(8,128)(2,1)S(1)}, u32[]{:S(2)}, u32[]{:S(2)}) async-start(bf16[64,88,128]{2,1,0:T(8,128)(2,1)} %shard_map.104), calls=%async_computation | async-start | bytes 2883584 | tf_op jit(solution)/shard_map/all_to_all | solution.py:179
  19.4 0.1 pad_bitcast_fusion
  19.5 0.1 pad_maximum_fusion.refs_1_
  19.5 4.0 %collective-permute-start.2 = (bf16[2,200,768]{2,1,0:T(8,128)(2,1)S(1)}, bf16[2,200,768]{2,1,0:T(8,128)(2,1)S(1)}, u32[]{:S(2)}, u32[]{:S(2)}) collective-permute-start(bf16[2,200,768]{2,1,0:T(8,128)(2,1)S(1)} %pad_maximum_fusion.refs_1_), channel_id=1, source_target_pairs={{0,4},{2,6},{4,0},{6,2},{1,5},{3,7},{5,1},{7,3},{8,12},{10,14},{12... | collective-permute-start | bytes 1843208 | tf_op jit(solution)/shard_map/ppermute | solution.py:160
  23.6 1.9 %collective-permute-start = (bf16[2,200,768]{2,1,0:T(8,128)(2,1)S(1)}, bf16[2,200,768]{2,1,0:T(8,128)(2,1)S(1)}, u32[]{:S(2)}, u32[]{:S(2)}) collective-permute-start(bf16[2,200,768]{2,1,0:T(8,128)(2,1)S(1)} %pad_maximum_fusion.refs_1_), channel_id=1, source_target_pairs={{0,2},{2,4},{4,6},{6,0},{1,3},{3,5},{5,7},{7,1},{8,10},{10,12},{12... | collective-permute-start | bytes 1843208 | tf_op jit(solution)/shard_map/ppermute | solution.py:160
  25.5 3.9 %collective-permute-start.1 = (bf16[2,200,768]{2,1,0:T(8,128)(2,1)S(1)}, bf16[2,200,768]{2,1,0:T(8,128)(2,1)S(1)}, u32[]{:S(2)}, u32[]{:S(2)}) collective-permute-start(bf16[2,200,768]{2,1,0:T(8,128)(2,1)S(1)} %pad_maximum_fusion.refs_1_), channel_id=1, source_target_pairs={{0,6},{2,0},{4,2},{6,4},{1,7},{3,1},{5,3},{7,5},{8,14},{10,8},{12,... | collective-permute-start | bytes 1843208 | tf_op jit(solution)/shard_map/ppermute | solution.py:160
  29.4 1.9 %collective-permute-start.3 = (bf16[2,200,768]{2,1,0:T(8,128)(2,1)S(1)}, bf16[2,200,768]{2,1,0:T(8,128)(2,1)S(1)}, u32[]{:S(2)}, u32[]{:S(2)}) collective-permute-start(bf16[2,200,768]{2,1,0:T(8,128)(2,1)S(1)} %pad_maximum_fusion.refs_1_), channel_id=1, source_target_pairs={{0,1},{1,0},{2,3},{3,2},{4,5},{5,4},{6,7},{7,6},{8,9},{9,8},{10,11... | collective-permute-start | bytes 1843208 | tf_op jit(solution)/shard_map/ppermute | solution.py:187
  31.4 8.3 %collective-permute-done.2.refs_6_ = bf16[2,200,768]{2,1,0:T(8,128)(2,1)S(1)} collective-permute-done((bf16[2,200,768]{2,1,0:T(8,128)(2,1)S(1)}, bf16[2,200,768]{2,1,0:T(8,128)(2,1)S(1)}, u32[]{:S(2)}, u32[]{:S(2)}) %collective-permute-start.2) | collective-permute-done | bytes 614432 | tf_op jit(solution)/shard_map/ppermute | solution.py:160
  39.7 1.9 %collective-permute-start.4 = (bf16[2,200,768]{2,1,0:T(8,128)(2,1)S(1)}, bf16[2,200,768]{2,1,0:T(8,128)(2,1)S(1)}, u32[]{:S(2)}, u32[]{:S(2)}) collective-permute-start(bf16[2,200,768]{2,1,0:T(8,128)(2,1)S(1)} %collective-permute-done.2.refs_6_), channel_id=1, source_target_pairs={{0,1},{1,0},{2,3},{3,2},{4,5},{5,4},{6,7},{7,6},{8,9},{9,8},{10,11... | collective-permute-start | bytes 1843208 | tf_op jit(solution)/shard_map/ppermute | solution.py:187
  41.6 9.9 %collective-permute-done.refs_2_ = bf16[2,200,768]{2,1,0:T(8,128)(2,1)S(1)} collective-permute-done((bf16[2,200,768]{2,1,0:T(8,128)(2,1)S(1)}, bf16[2,200,768]{2,1,0:T(8,128)(2,1)S(1)}, u32[]{:S(2)}, u32[]{:S(2)}) %collective-permute-start) | collective-permute-done | bytes 614432 | tf_op jit(solution)/shard_map/ppermute | solution.py:160
  51.5 1.9 %collective-permute-start.5 = (bf16[2,200,768]{2,1,0:T(8,128)(2,1)S(1)}, bf16[2,200,768]{2,1,0:T(8,128)(2,1)S(1)}, u32[]{:S(2)}, u32[]{:S(2)}) collective-permute-start(bf16[2,200,768]{2,1,0:T(8,128)(2,1)S(1)} %collective-permute-done.refs_2_), channel_id=1, source_target_pairs={{0,1},{1,0},{2,3},{3,2},{4,5},{5,4},{6,7},{7,6},{8,9},{9,8},{10,11... | collective-permute-start | bytes 1843208 | tf_op jit(solution)/shard_map/ppermute | solution.py:187
  53.4 0.0 collective-permute-done.1.refs_3_
  53.4 2.4 %collective-permute-start.6 = (bf16[2,200,768]{2,1,0:T(8,128)(2,1)S(1)}, bf16[2,200,768]{2,1,0:T(8,128)(2,1)}, u32[]{:S(2)}, u32[]{:S(2)}) collective-permute-start(bf16[2,200,768]{2,1,0:T(8,128)(2,1)S(1)} %collective-permute-done.1.refs_3_), channel_id=1, source_target_pairs={{0,1},{1,0},{2,3},{3,2},{4,5},{5,4},{6,7},{7,6},{8,9},{9,8},{10,11... | collective-permute-start | bytes 1843208 | tf_op jit(solution)/shard_map/ppermute | solution.py:187
  55.8 0.0 collective-permute-done.3.refs_7_
  55.8 0.0 collective-permute-done.4.refs_8_
  55.9 0.0 collective-permute-done.5.refs_9_
  55.9 0.8 copy-done.4
  56.7 0.2 copy-done.5
  56.9 0.8 copy-done.6
  57.7 0.0 collective-permute-done.6.refs_10_
  57.7 7.7 %shard_map.105 = bf16[8,2,128,128]{3,2,1,0:T(8,128)(2,1)} custom-call(bf16[512,1408]{1,0:T(8,128)(2,1)S(1)} %bitcast.12, bf16[2,200,768]{2,1,0:T(8,128)(2,1)S(1)} %pad_maximum_fusion.refs_1_, bf16[2,200,768]{2,1,0:T(8,128)(2,1)S(1)} %collective-permute-done.refs_2_, bf16[2,200,768]{2,1,0:T(8,128)(2,1)S(1)} %collective-permute-done.1.refs_3_, ...), custom_call_target="tpu_custom_call" | custom-call | flops 4000000000 | bytes 1000000 | tf_op jit(solution)/shard_map/pallas_call | solution.py:156
  65.5 0.0 copy-start.2
  65.5 4.8 %all-to-all-start.1 = ((bf16[8,2,128,128]{3,2,1,0:T(8,128)(2,1)}), bf16[8,2,128,128]{3,2,1,0:T(8,128)(2,1)S(1)}, u32[]{:S(2)}, u32[]{:S(2)}) async-start(bf16[8,2,128,128]{3,2,1,0:T(8,128)(2,1)} %shard_map.105), calls=%async_computation.1 | async-start | bytes 1048576 | tf_op jit(solution)/shard_map/all_to_all | solution.py:196
  70.2 8.9 %all-to-all-done.1 = bf16[8,2,128,128]{3,2,1,0:T(8,128)(2,1)S(1)} async-done(((bf16[8,2,128,128]{3,2,1,0:T(8,128)(2,1)}), bf16[8,2,128,128]{3,2,1,0:T(8,128)(2,1)S(1)}, u32[]{:S(2)}, u32[]{:S(2)}) %all-to-all-start.1) | async-done | bytes 524320 | tf_op jit(solution)/shard_map/all_to_all | solution.py:196
  79.1 0.1 convert_reduce_fusion
  79.2 0.6 multiply_reduce_fusion
  80.5 15.5 %all_to_all.20 = f32[8,2,16,128]{3,2,1,0:T(8,128)S(1)} all-to-all(f32[8,2,16,128]{3,2,1,0:T(8,128)S(1)} %broadcast_in_dim.4), channel_id=1, replica_groups=mesh['dp_0'=8,'dp_1'=8,'x'=4,'core'=2] {'dp_0'}, dimensions={0} | all-to-all | bytes 262144 | tf_op jit(solution)/shard_map/all_to_all | solution.py:28
  96.0 15.6 %all_to_all.21 = f32[8,2,16,128]{3,2,1,0:T(8,128)S(1)} all-to-all(f32[8,2,16,128]{3,2,1,0:T(8,128)S(1)} %broadcast_in_dim.5), channel_id=1, replica_groups=mesh['dp_0'=8,'dp_1'=8,'x'=4,'core'=2] {'dp_1'}, dimensions={0} | all-to-all | bytes 262144 | tf_op jit(solution)/shard_map/all_to_all | solution.py:28
  111.6 0.6 add_multiply_fusion
  (14 shorter events, 0.1 us)
Async XLA Ops:
  2.6 16.8 %copy-start = (bf16[1,1,197,768]{3,2,1,0:T(8,128)(2,1)S(1)}, bf16[1,1,197,768]{3,2,1,0:T(8,128)(2,1)}, u32[]{:S(2)}) copy-start(bf16[1,1,197,768]{3,2,1,0:T(8,128)(2,1)} %param.10) | copy-start | bytes 907780
  2.6 16.8 %copy-start.1 = (bf16[1,1,197,768]{3,2,1,0:T(8,128)(2,1)S(1)}, bf16[1,1,197,768]{3,2,1,0:T(8,128)(2,1)}, u32[]{:S(2)}) copy-start(bf16[1,1,197,768]{3,2,1,0:T(8,128)(2,1)} %param.9) | copy-start | bytes 907780
  2.6 55.1 %all-to-all-start = ((bf16[64,88,128]{2,1,0:T(8,128)(2,1)}), bf16[64,88,128]{2,1,0:T(8,128)(2,1)S(1)}, u32[]{:S(2)}, u32[]{:S(2)}) async-start(bf16[64,88,128]{2,1,0:T(8,128)(2,1)} %shard_map.104), calls=%async_computation | async-start | bytes 2883584 | tf_op jit(solution)/shard_map/all_to_all | solution.py:179
  19.5 20.2 %collective-permute-start.2 = (bf16[2,200,768]{2,1,0:T(8,128)(2,1)S(1)}, bf16[2,200,768]{2,1,0:T(8,128)(2,1)S(1)}, u32[]{:S(2)}, u32[]{:S(2)}) collective-permute-start(bf16[2,200,768]{2,1,0:T(8,128)(2,1)S(1)} %pad_maximum_fusion.refs_1_), channel_id=1, source_target_pairs={{0,4},{2,6},{4,0},{6,2},{1,5},{3,7},{5,1},{7,3},{8,12},{10,14},{12... | collective-permute-start | bytes 1843208 | tf_op jit(solution)/shard_map/ppermute | solution.py:160
  23.6 27.9 %collective-permute-start = (bf16[2,200,768]{2,1,0:T(8,128)(2,1)S(1)}, bf16[2,200,768]{2,1,0:T(8,128)(2,1)S(1)}, u32[]{:S(2)}, u32[]{:S(2)}) collective-permute-start(bf16[2,200,768]{2,1,0:T(8,128)(2,1)S(1)} %pad_maximum_fusion.refs_1_), channel_id=1, source_target_pairs={{0,2},{2,4},{4,6},{6,0},{1,3},{3,5},{5,7},{7,1},{8,10},{10,12},{12... | collective-permute-start | bytes 1843208 | tf_op jit(solution)/shard_map/ppermute | solution.py:160
  25.5 27.9 %collective-permute-start.1 = (bf16[2,200,768]{2,1,0:T(8,128)(2,1)S(1)}, bf16[2,200,768]{2,1,0:T(8,128)(2,1)S(1)}, u32[]{:S(2)}, u32[]{:S(2)}) collective-permute-start(bf16[2,200,768]{2,1,0:T(8,128)(2,1)S(1)} %pad_maximum_fusion.refs_1_), channel_id=1, source_target_pairs={{0,6},{2,0},{4,2},{6,4},{1,7},{3,1},{5,3},{7,5},{8,14},{10,8},{12,... | collective-permute-start | bytes 1843208 | tf_op jit(solution)/shard_map/ppermute | solution.py:160
  29.4 26.4 %collective-permute-start.3 = (bf16[2,200,768]{2,1,0:T(8,128)(2,1)S(1)}, bf16[2,200,768]{2,1,0:T(8,128)(2,1)S(1)}, u32[]{:S(2)}, u32[]{:S(2)}) collective-permute-start(bf16[2,200,768]{2,1,0:T(8,128)(2,1)S(1)} %pad_maximum_fusion.refs_1_), channel_id=1, source_target_pairs={{0,1},{1,0},{2,3},{3,2},{4,5},{5,4},{6,7},{7,6},{8,9},{9,8},{10,11... | collective-permute-start | bytes 1843208 | tf_op jit(solution)/shard_map/ppermute | solution.py:187
  39.7 16.2 %copy-start.3 = (bf16[2,200,768]{2,1,0:T(8,128)(2,1)}, bf16[2,200,768]{2,1,0:T(8,128)(2,1)S(1)}, u32[]{:S(2)}) copy-start(bf16[2,200,768]{2,1,0:T(8,128)(2,1)S(1)} %collective-permute-done.2.refs_6_) | copy-start | bytes 1843204
  39.7 16.1 %collective-permute-start.4 = (bf16[2,200,768]{2,1,0:T(8,128)(2,1)S(1)}, bf16[2,200,768]{2,1,0:T(8,128)(2,1)S(1)}, u32[]{:S(2)}, u32[]{:S(2)}) collective-permute-start(bf16[2,200,768]{2,1,0:T(8,128)(2,1)S(1)} %collective-permute-done.2.refs_6_), channel_id=1, source_target_pairs={{0,1},{1,0},{2,3},{3,2},{4,5},{5,4},{6,7},{7,6},{8,9},{9,8},{10,11... | collective-permute-start | bytes 1843208 | tf_op jit(solution)/shard_map/ppermute | solution.py:187
  51.5 4.4 %collective-permute-start.5 = (bf16[2,200,768]{2,1,0:T(8,128)(2,1)S(1)}, bf16[2,200,768]{2,1,0:T(8,128)(2,1)S(1)}, u32[]{:S(2)}, u32[]{:S(2)}) collective-permute-start(bf16[2,200,768]{2,1,0:T(8,128)(2,1)S(1)} %collective-permute-done.refs_2_), channel_id=1, source_target_pairs={{0,1},{1,0},{2,3},{3,2},{4,5},{5,4},{6,7},{7,6},{8,9},{9,8},{10,11... | collective-permute-start | bytes 1843208 | tf_op jit(solution)/shard_map/ppermute | solution.py:187
  53.4 4.3 %collective-permute-start.6 = (bf16[2,200,768]{2,1,0:T(8,128)(2,1)S(1)}, bf16[2,200,768]{2,1,0:T(8,128)(2,1)}, u32[]{:S(2)}, u32[]{:S(2)}) collective-permute-start(bf16[2,200,768]{2,1,0:T(8,128)(2,1)S(1)} %collective-permute-done.1.refs_3_), channel_id=1, source_target_pairs={{0,1},{1,0},{2,3},{3,2},{4,5},{5,4},{6,7},{7,6},{8,9},{9,8},{10,11... | collective-permute-start | bytes 1843208 | tf_op jit(solution)/shard_map/ppermute | solution.py:187
  55.8 0.8 copy-start.4
  55.9 1.0 copy-start.5
  56.9 0.8 copy-start.6
  65.5 46.1 %copy-start.2 = (f32[2,16,128]{2,1,0:T(8,128)S(1)}, f32[2,16,128]{2,1,0:T(8,128)}, u32[]{:S(2)}) copy-start(f32[2,16,128]{2,1,0:T(8,128)} %param.17) | copy-start | bytes 49156
  65.5 13.6 %all-to-all-start.1 = ((bf16[8,2,128,128]{3,2,1,0:T(8,128)(2,1)}), bf16[8,2,128,128]{3,2,1,0:T(8,128)(2,1)S(1)}, u32[]{:S(2)}, u32[]{:S(2)}) async-start(bf16[8,2,128,128]{3,2,1,0:T(8,128)(2,1)} %shard_map.105), calls=%async_computation.1 | async-start | bytes 1048576 | tf_op jit(solution)/shard_map/all_to_all | solution.py:196

commit v8 on v6

--- a/solution.py
+++ b/solution.py
@@ -101,23 +101,34 @@
     return v_up, u_down
 
 
+def batches(groups, others, fetches):
+    for batch, waits in ((groups + others[:1], fetches[:1]), (others[1:], fetches[1:])):
+        for fetch in waits:
+            fetch.wait()
+        yield tuple(jnp.concatenate([group[i] for group in batch], axis=0) for i in (0, 1))
+
+
+def project(near, late, fetches, results):
+    right_up, left_down, *others = late
+    for fetch in fetches[:2]:
+        fetch.wait()
+    for k, (token_rows, grad_rows) in enumerate(batches(list(near), others, fetches[2:])):
+        results[0][k] = contract(token_rows, right_up[...], ((1,), (0,))).astype(bf16)
+        results[1][k] = contract(grad_rows, left_down[...], ((1,), (0,))).astype(bf16)
+
+
 def all_units(senders, rows, near, late, fetches, results):
     weights, *groups = near
-    right_up, left_down, *others = late
+    u_up, v_down, *others = late
     (terms,) = results
     unpacked = unpack_weights(weights[...], senders, rows, lane)
     for fetch in fetches[:2]:
         fetch.wait()
     first, second = 0.0, 0.0
-    for k, group in enumerate((*groups, *others)):
-        if k >= len(groups):
-            fetches[2 + k - len(groups)].wait()
-        token_rows, grad_rows = group[0], group[1]
+    for k, (token_rows, grad_rows) in enumerate(batches(groups, others, fetches[2:])):
         v_up, u_down = through_units(token_rows, grad_rows, unpacked)
-        u_up = contract(token_rows, right_up[...], ((1,), (0,))).astype(bf16)
-        v_down = contract(grad_rows, left_down[...], ((1,), (0,))).astype(bf16)
-        first += contract(v_up.astype(bf16), u_up, ((0,), (0,)))
-        second += contract(v_down, u_down.astype(bf16), ((0,), (0,)))
+        first += contract(v_up.astype(bf16), u_up[k], ((0,), (0,)))
+        second += contract(v_down[k], u_down.astype(bf16), ((0,), (0,)))
     both = jnp.stack([first, second]).astype(bf16)
     terms[...] = jnp.broadcast_to(both[None], terms.shape)
 
@@ -187,9 +198,10 @@
     all_augs = lax.axis_size(AUG)
     units = functools.partial(all_units, senders, rows)
     size = (all_augs, 2, rank, rank)
-    near = (gathered, mine, below, above)
-    late = (right_up, left_down, far, *swapped)
-    (terms,) = kernel(units, [(size, bf16)], near, late, flops=4 * 10**9)
+    near, others = (mine, below, above), (far, *swapped)
+    half = (2, (len(near) + len(others)) // 2 * mine.shape[1], rank)
+    kept = kernel(project, [(half, bf16)] * 2, near, (right_up, left_down, *others), 10**9)
+    (terms,) = kernel(units, [(size, bf16)], (gathered, *near), (*kept, *others), 4 * 10**9)
     share_rows = rank // all_augs
     lower_row = lax.axis_index(AUG) * share_rows
     aug_mean = lax.all_to_all(terms, AUG, 0, 0, tiled=True).astype(f32).sum(axis=0) / all_augs

time: 116 us -> 117 us (level)
  waiting for transfers between devices: 27.1 us -> 28.7 us
    ppermute x4, waiting for transfers between devices: 0.01 us -> 1.59 us  [local(): swapped.append(lax.ppermute(group, 'core', [(0, 1), (1, 0)]))]
    pallas_call x2 -> x3, Pallas kernels: 12.1 us -> 12.3 us  [kernel(): return call(*held(near, pltpu.VMEM), *held(late, pltpu.HBM))]
  transfers between devices with their start and end apart: 9 -> 9, of which waited for: 3 -> 4; matrix products, arithmetic and copies ran while one was open for 0% -> 0% of each run, Pallas kernels for 0% -> 3%
where the time goes in v8:
time: 117 us
  starting transfers between devices  39.5 us (34%)
  blocking collectives  31 us (26%)
  waiting for transfers between devices  28.7 us (25%)
  Pallas kernels  12.3 us (11%)
  between operations  2.7 us (2%)
  other arithmetic  1.41 us (1%)
    all_to_all x2, blocking collectives, copy_for_each(): lax.all_to_all(jnp.broadcast_to(shard[None], (size, *shard.shape)), axis,...  31 us
    ppermute x3, waiting for transfers between devices, neighbour(): return lax.ppermute(array, 'x', [(i, (i + shift) % 4) for i in range(4)])  18.2 us
    all_to_all x1, starting transfers between devices, local(): gathered = lax.all_to_all(copies, DP, 0, 0, tiled=True)  16.7 us
    pallas_call x3, Pallas kernels, kernel(): return call(*held(near, pltpu.VMEM), *held(late, pltpu.HBM))  12.3 us
    ppermute x3, starting transfers between devices, neighbour(): return lax.ppermute(array, 'x', [(i, (i + shift) % 4) for i in range(4)])  9.88 us
    all_to_all x1, waiting for transfers between devices, local(): lax.all_to_all(terms, AUG, 0, 0, tiled=True).astype(f32).sum(axis=0)  8.86 us
    ppermute x4, starting transfers between devices, local(): swapped.append(lax.ppermute(group, 'core', [(0, 1), (1, 0)]))  8.14 us
    all_to_all x1, starting transfers between devices, local(): lax.all_to_all(terms, AUG, 0, 0, tiled=True).astype(f32).sum(axis=0)  4.77 us
  transfers between devices with their start and end apart: 9, of which 4 were waited for; matrix products, arithmetic and copies ran while one was open for 0% of the time, Pallas kernels for 3%

profile of v8, /device:TPU:2, one launch (start us, length us, event | category | flops | bytes accessed | tf_op | source)
XLA Modules:
  0.0 116.5 jit_solution(11799640540560211401)
XLA Ops:
  0.6 2.0 %shard_map.104 = bf16[64,88,128]{2,1,0:T(8,128)(2,1)} custom-call(bf16[6,768]{1,0:T(8,128)(2,1)} %refs_0_.1, bf16[6,768]{1,0:T(8,128)(2,1)} %refs_1_.1, bf16[6,128]{1,0:T(8,128)(2,1)} %refs_2_.1, bf16[6,128]{1,0:T(8,128)(2,1)} %refs_3_.2), custom_call_target="tpu_custom_call" | custom-call | bytes 1000000 | tf_op jit(solution)/shard_map/pallas_call | solution.py:166
  2.6 0.0 copy-start.5
  2.6 0.0 copy-start.6
  2.7 16.7 %all-to-all-start = ((bf16[64,88,128]{2,1,0:T(8,128)(2,1)}), bf16[64,88,128]{2,1,0:T(8,128)(2,1)S(1)}, u32[]{:S(2)}, u32[]{:S(2)}) async-start(bf16[64,88,128]{2,1,0:T(8,128)(2,1)} %shard_map.104), calls=%async_computation | async-start | bytes 2883584 | tf_op jit(solution)/shard_map/all_to_all | solution.py:189
  19.4 0.1 pad_bitcast_fusion
  19.5 0.1 pad_maximum_fusion.refs_0_.refs_1_
  19.5 4.0 %collective-permute-start.2 = (bf16[2,200,768]{2,1,0:T(8,128)(2,1)S(1)}, bf16[2,200,768]{2,1,0:T(8,128)(2,1)S(1)}, u32[]{:S(2)}, u32[]{:S(2)}) collective-permute-start(bf16[2,200,768]{2,1,0:T(8,128)(2,1)S(1)} %pad_maximum_fusion.refs_0_.refs_1_), channel_id=1, source_target_pairs={{0,4},{2,6},{4,0},{6,2},{1,5},{3,7},{5,1},{7,3},{8,12},{10,14},{12... | collective-permute-start | bytes 1843208 | tf_op jit(solution)/shard_map/ppermute | solution.py:170
  23.6 1.9 %collective-permute-start = (bf16[2,200,768]{2,1,0:T(8,128)(2,1)S(1)}, bf16[2,200,768]{2,1,0:T(8,128)(2,1)S(1)}, u32[]{:S(2)}, u32[]{:S(2)}) collective-permute-start(bf16[2,200,768]{2,1,0:T(8,128)(2,1)S(1)} %pad_maximum_fusion.refs_0_.refs_1_), channel_id=1, source_target_pairs={{0,2},{2,4},{4,6},{6,0},{1,3},{3,5},{5,7},{7,1},{8,10},{10,12},{12... | collective-permute-start | bytes 1843208 | tf_op jit(solution)/shard_map/ppermute | solution.py:170
  25.5 3.9 %collective-permute-start.1 = (bf16[2,200,768]{2,1,0:T(8,128)(2,1)S(1)}, bf16[2,200,768]{2,1,0:T(8,128)(2,1)S(1)}, u32[]{:S(2)}, u32[]{:S(2)}) collective-permute-start(bf16[2,200,768]{2,1,0:T(8,128)(2,1)S(1)} %pad_maximum_fusion.refs_0_.refs_1_), channel_id=1, source_target_pairs={{0,6},{2,0},{4,2},{6,4},{1,7},{3,1},{5,3},{7,5},{8,14},{10,8},{12,... | collective-permute-start | bytes 1843208 | tf_op jit(solution)/shard_map/ppermute | solution.py:170
  29.4 1.9 %collective-permute-start.3 = (bf16[2,200,768]{2,1,0:T(8,128)(2,1)S(1)}, bf16[2,200,768]{2,1,0:T(8,128)(2,1)S(1)}, u32[]{:S(2)}, u32[]{:S(2)}) collective-permute-start(bf16[2,200,768]{2,1,0:T(8,128)(2,1)S(1)} %pad_maximum_fusion.refs_0_.refs_1_), channel_id=1, source_target_pairs={{0,1},{1,0},{2,3},{3,2},{4,5},{5,4},{6,7},{7,6},{8,9},{9,8},{10,11... | collective-permute-start | bytes 1843208 | tf_op jit(solution)/shard_map/ppermute | solution.py:197
  31.4 8.3 %collective-permute-done.2.refs_5_.refs_6_ = bf16[2,200,768]{2,1,0:T(8,128)(2,1)S(1)} collective-permute-done((bf16[2,200,768]{2,1,0:T(8,128)(2,1)S(1)}, bf16[2,200,768]{2,1,0:T(8,128)(2,1)S(1)}, u32[]{:S(2)}, u32[]{:S(2)}) %collective-permute-start.2) | collective-permute-done | bytes 614432 | tf_op jit(solution)/shard_map/ppermute | solution.py:170
  39.7 1.9 %collective-permute-start.4 = (bf16[2,200,768]{2,1,0:T(8,128)(2,1)S(1)}, bf16[2,200,768]{2,1,0:T(8,128)(2,1)S(1)}, u32[]{:S(2)}, u32[]{:S(2)}) collective-permute-start(bf16[2,200,768]{2,1,0:T(8,128)(2,1)S(1)} %collective-permute-done.2.refs_5_.refs_6_), channel_id=1, source_target_pairs={{0,1},{1,0},{2,3},{3,2},{4,5},{5,4},{6,7},{7,6},{8,9},{9,8},{10,11... | collective-permute-start | bytes 1843208 | tf_op jit(solution)/shard_map/ppermute | solution.py:197
  41.6 9.9 %collective-permute-done.refs_1_.refs_2_ = bf16[2,200,768]{2,1,0:T(8,128)(2,1)S(1)} collective-permute-done((bf16[2,200,768]{2,1,0:T(8,128)(2,1)S(1)}, bf16[2,200,768]{2,1,0:T(8,128)(2,1)S(1)}, u32[]{:S(2)}, u32[]{:S(2)}) %collective-permute-start) | collective-permute-done | bytes 614432 | tf_op jit(solution)/shard_map/ppermute | solution.py:170
  51.5 1.9 %collective-permute-start.5 = (bf16[2,200,768]{2,1,0:T(8,128)(2,1)S(1)}, bf16[2,200,768]{2,1,0:T(8,128)(2,1)S(1)}, u32[]{:S(2)}, u32[]{:S(2)}) collective-permute-start(bf16[2,200,768]{2,1,0:T(8,128)(2,1)S(1)} %collective-permute-done.refs_1_.refs_2_), channel_id=1, source_target_pairs={{0,1},{1,0},{2,3},{3,2},{4,5},{5,4},{6,7},{7,6},{8,9},{9,8},{10,11... | collective-permute-start | bytes 1843208 | tf_op jit(solution)/shard_map/ppermute | solution.py:197
  53.4 0.0 collective-permute-done.1.refs_2_.refs_3_
  53.4 2.4 %collective-permute-start.6 = (bf16[2,200,768]{2,1,0:T(8,128)(2,1)S(1)}, bf16[2,200,768]{2,1,0:T(8,128)(2,1)S(1)}, u32[]{:S(2)}, u32[]{:S(2)}) collective-permute-start(bf16[2,200,768]{2,1,0:T(8,128)(2,1)S(1)} %collective-permute-done.1.refs_2_.refs_3_), channel_id=1, source_target_pairs={{0,1},{1,0},{2,3},{3,2},{4,5},{5,4},{6,7},{7,6},{8,9},{9,8},{10,11... | collective-permute-start | bytes 1843208 | tf_op jit(solution)/shard_map/ppermute | solution.py:197
  55.8 0.0 collective-permute-done.3.refs_6_.refs_7_
  55.9 0.0 collective-permute-done.4.refs_7_.refs_8_
  55.9 0.0 collective-permute-done.5.refs_8_.refs_9_
  55.9 1.6 %collective-permute-done.6.refs_9_.refs_10_ = bf16[2,200,768]{2,1,0:T(8,128)(2,1)S(1)} collective-permute-done((bf16[2,200,768]{2,1,0:T(8,128)(2,1)S(1)}, bf16[2,200,768]{2,1,0:T(8,128)(2,1)S(1)}, u32[]{:S(2)}, u32[]{:S(2)}) %collective-permute-start.6) | collective-permute-done | bytes 614432 | tf_op jit(solution)/shard_map/ppermute | solution.py:197
  57.5 0.8 copy-done.4
  58.3 3.9 %shard_map.105 = (bf16[2,800,128]{2,1,0:T(8,128)(2,1)}, bf16[2,800,128]{2,1,0:T(8,128)(2,1)}) custom-call(bf16[2,200,768]{2,1,0:T(8,128)(2,1)S(1)} %pad_maximum_fusion.refs_0_.refs_1_, bf16[2,200,768]{2,1,0:T(8,128)(2,1)S(1)} %collective-permute-done.refs_1_.refs_2_, bf16[2,200,768]{2,1,0:T(8,128)(2,1)S(1)} %collective-permute-done.1.refs_2_.refs_3_, ...), custom_call_target="tpu_custom_call" | custom-call | flops 1000000000 | bytes 1000000 | tf_op jit(solution)/shard_map/pallas_call | solution.py:166
  62.2 0.0 all-to-all-done
  62.2 6.5 %shard_map.106 = bf16[8,2,128,128]{3,2,1,0:T(8,128)(2,1)} custom-call(bf16[512,1408]{1,0:T(8,128)(2,1)S(1)} %bitcast.12, bf16[2,200,768]{2,1,0:T(8,128)(2,1)S(1)} %pad_maximum_fusion.refs_0_.refs_1_, bf16[2,200,768]{2,1,0:T(8,128)(2,1)S(1)} %collective-permute-done.refs_1_.refs_2_, bf16[2,200,768]{2,1,0:T(8,128)(2,1)S(1)} %collective-permute-done.1.refs_2_.refs_3_, ...), custom_call_target="tpu_custom_call" | custom-call | flops 4000000000 | bytes 1000000 | tf_op jit(solution)/shard_map/pallas_call | solution.py:166
  68.7 0.0 copy-start.7
  68.7 4.8 %all-to-all-start.1 = ((bf16[8,2,128,128]{3,2,1,0:T(8,128)(2,1)}), bf16[8,2,128,128]{3,2,1,0:T(8,128)(2,1)S(1)}, u32[]{:S(2)}, u32[]{:S(2)}) async-start(bf16[8,2,128,128]{3,2,1,0:T(8,128)(2,1)} %shard_map.106), calls=%async_computation.1 | async-start | bytes 1048576 | tf_op jit(solution)/shard_map/all_to_all | solution.py:207
  73.4 8.9 %all-to-all-done.1 = bf16[8,2,128,128]{3,2,1,0:T(8,128)(2,1)S(1)} async-done(((bf16[8,2,128,128]{3,2,1,0:T(8,128)(2,1)}), bf16[8,2,128,128]{3,2,1,0:T(8,128)(2,1)S(1)}, u32[]{:S(2)}, u32[]{:S(2)}) %all-to-all-start.1) | async-done | bytes 524320 | tf_op jit(solution)/shard_map/all_to_all | solution.py:207
  82.3 0.1 convert_reduce_fusion
  82.4 0.6 multiply_reduce_fusion
  83.7 15.4 %all_to_all.20 = f32[8,2,16,128]{3,2,1,0:T(8,128)S(1)} all-to-all(f32[8,2,16,128]{3,2,1,0:T(8,128)S(1)} %broadcast_in_dim.4), channel_id=1, replica_groups=mesh['dp_0'=8,'dp_1'=8,'x'=4,'core'=2] {'dp_0'}, dimensions={0} | all-to-all | bytes 262144 | tf_op jit(solution)/shard_map/all_to_all | solution.py:28
  99.2 15.5 %all_to_all.21 = f32[8,2,16,128]{3,2,1,0:T(8,128)S(1)} all-to-all(f32[8,2,16,128]{3,2,1,0:T(8,128)S(1)} %broadcast_in_dim.5), channel_id=1, replica_groups=mesh['dp_0'=8,'dp_1'=8,'x'=4,'core'=2] {'dp_1'}, dimensions={0} | all-to-all | bytes 262144 | tf_op jit(solution)/shard_map/all_to_all | solution.py:28
  114.8 0.6 add_multiply_fusion
  (17 shorter events, 0.1 us)
Async XLA Ops:
  2.6 16.8 %copy-start.5 = (bf16[1,1,197,768]{3,2,1,0:T(8,128)(2,1)S(1)}, bf16[1,1,197,768]{3,2,1,0:T(8,128)(2,1)}, u32[]{:S(2)}) copy-start(bf16[1,1,197,768]{3,2,1,0:T(8,128)(2,1)} %param.10) | copy-start | bytes 907780
  2.6 16.8 %copy-start.6 = (bf16[1,1,197,768]{3,2,1,0:T(8,128)(2,1)S(1)}, bf16[1,1,197,768]{3,2,1,0:T(8,128)(2,1)}, u32[]{:S(2)}) copy-start(bf16[1,1,197,768]{3,2,1,0:T(8,128)(2,1)} %param.9) | copy-start | bytes 907780
  2.7 59.5 %all-to-all-start = ((bf16[64,88,128]{2,1,0:T(8,128)(2,1)}), bf16[64,88,128]{2,1,0:T(8,128)(2,1)S(1)}, u32[]{:S(2)}, u32[]{:S(2)}) async-start(bf16[64,88,128]{2,1,0:T(8,128)(2,1)} %shard_map.104), calls=%async_computation | async-start | bytes 2883584 | tf_op jit(solution)/shard_map/all_to_all | solution.py:189
  19.5 20.2 %collective-permute-start.2 = (bf16[2,200,768]{2,1,0:T(8,128)(2,1)S(1)}, bf16[2,200,768]{2,1,0:T(8,128)(2,1)S(1)}, u32[]{:S(2)}, u32[]{:S(2)}) collective-permute-start(bf16[2,200,768]{2,1,0:T(8,128)(2,1)S(1)} %pad_maximum_fusion.refs_0_.refs_1_), channel_id=1, source_target_pairs={{0,4},{2,6},{4,0},{6,2},{1,5},{3,7},{5,1},{7,3},{8,12},{10,14},{12... | collective-permute-start | bytes 1843208 | tf_op jit(solution)/shard_map/ppermute | solution.py:170
  23.6 27.9 %collective-permute-start = (bf16[2,200,768]{2,1,0:T(8,128)(2,1)S(1)}, bf16[2,200,768]{2,1,0:T(8,128)(2,1)S(1)}, u32[]{:S(2)}, u32[]{:S(2)}) collective-permute-start(bf16[2,200,768]{2,1,0:T(8,128)(2,1)S(1)} %pad_maximum_fusion.refs_0_.refs_1_), channel_id=1, source_target_pairs={{0,2},{2,4},{4,6},{6,0},{1,3},{3,5},{5,7},{7,1},{8,10},{10,12},{12... | collective-permute-start | bytes 1843208 | tf_op jit(solution)/shard_map/ppermute | solution.py:170
  25.5 27.9 %collective-permute-start.1 = (bf16[2,200,768]{2,1,0:T(8,128)(2,1)S(1)}, bf16[2,200,768]{2,1,0:T(8,128)(2,1)S(1)}, u32[]{:S(2)}, u32[]{:S(2)}) collective-permute-start(bf16[2,200,768]{2,1,0:T(8,128)(2,1)S(1)} %pad_maximum_fusion.refs_0_.refs_1_), channel_id=1, source_target_pairs={{0,6},{2,0},{4,2},{6,4},{1,7},{3,1},{5,3},{7,5},{8,14},{10,8},{12,... | collective-permute-start | bytes 1843208 | tf_op jit(solution)/shard_map/ppermute | solution.py:170
  29.4 26.4 %collective-permute-start.3 = (bf16[2,200,768]{2,1,0:T(8,128)(2,1)S(1)}, bf16[2,200,768]{2,1,0:T(8,128)(2,1)S(1)}, u32[]{:S(2)}, u32[]{:S(2)}) collective-permute-start(bf16[2,200,768]{2,1,0:T(8,128)(2,1)S(1)} %pad_maximum_fusion.refs_0_.refs_1_), channel_id=1, source_target_pairs={{0,1},{1,0},{2,3},{3,2},{4,5},{5,4},{6,7},{7,6},{8,9},{9,8},{10,11... | collective-permute-start | bytes 1843208 | tf_op jit(solution)/shard_map/ppermute | solution.py:197
  39.7 17.8 %copy-start = (bf16[2,200,768]{2,1,0:T(8,128)(2,1)}, bf16[2,200,768]{2,1,0:T(8,128)(2,1)S(1)}, u32[]{:S(2)}) copy-start(bf16[2,200,768]{2,1,0:T(8,128)(2,1)S(1)} %collective-permute-done.2.refs_5_.refs_6_) | copy-start | bytes 1843204
  39.7 16.1 %collective-permute-start.4 = (bf16[2,200,768]{2,1,0:T(8,128)(2,1)S(1)}, bf16[2,200,768]{2,1,0:T(8,128)(2,1)S(1)}, u32[]{:S(2)}, u32[]{:S(2)}) collective-permute-start(bf16[2,200,768]{2,1,0:T(8,128)(2,1)S(1)} %collective-permute-done.2.refs_5_.refs_6_), channel_id=1, source_target_pairs={{0,1},{1,0},{2,3},{3,2},{4,5},{5,4},{6,7},{7,6},{8,9},{9,8},{10,11... | collective-permute-start | bytes 1843208 | tf_op jit(solution)/shard_map/ppermute | solution.py:197
  51.5 4.4 %collective-permute-start.5 = (bf16[2,200,768]{2,1,0:T(8,128)(2,1)S(1)}, bf16[2,200,768]{2,1,0:T(8,128)(2,1)S(1)}, u32[]{:S(2)}, u32[]{:S(2)}) collective-permute-start(bf16[2,200,768]{2,1,0:T(8,128)(2,1)S(1)} %collective-permute-done.refs_1_.refs_2_), channel_id=1, source_target_pairs={{0,1},{1,0},{2,3},{3,2},{4,5},{5,4},{6,7},{7,6},{8,9},{9,8},{10,11... | collective-permute-start | bytes 1843208 | tf_op jit(solution)/shard_map/ppermute | solution.py:197
  53.4 4.1 %collective-permute-start.6 = (bf16[2,200,768]{2,1,0:T(8,128)(2,1)S(1)}, bf16[2,200,768]{2,1,0:T(8,128)(2,1)S(1)}, u32[]{:S(2)}, u32[]{:S(2)}) collective-permute-start(bf16[2,200,768]{2,1,0:T(8,128)(2,1)S(1)} %collective-permute-done.1.refs_2_.refs_3_), channel_id=1, source_target_pairs={{0,1},{1,0},{2,3},{3,2},{4,5},{5,4},{6,7},{7,6},{8,9},{9,8},{10,11... | collective-permute-start | bytes 1843208 | tf_op jit(solution)/shard_map/ppermute | solution.py:197
  55.9 1.6 %copy-start.1 = (bf16[2,200,768]{2,1,0:T(8,128)(2,1)}, bf16[2,200,768]{2,1,0:T(8,128)(2,1)S(1)}, u32[]{:S(2)}) copy-start(bf16[2,200,768]{2,1,0:T(8,128)(2,1)S(1)} %collective-permute-done.3.refs_6_.refs_7_) | copy-start | bytes 1843204
  55.9 1.6 %copy-start.2 = (bf16[2,200,768]{2,1,0:T(8,128)(2,1)}, bf16[2,200,768]{2,1,0:T(8,128)(2,1)S(1)}, u32[]{:S(2)}) copy-start(bf16[2,200,768]{2,1,0:T(8,128)(2,1)S(1)} %collective-permute-done.4.refs_7_.refs_8_) | copy-start | bytes 1843204
  55.9 1.6 %copy-start.3 = (bf16[2,200,768]{2,1,0:T(8,128)(2,1)}, bf16[2,200,768]{2,1,0:T(8,128)(2,1)S(1)}, u32[]{:S(2)}) copy-start(bf16[2,200,768]{2,1,0:T(8,128)(2,1)S(1)} %collective-permute-done.5.refs_8_.refs_9_) | copy-start | bytes 1843204
  57.5 0.8 copy-start.4
  68.7 46.1 %copy-start.7 = (f32[2,16,128]{2,1,0:T(8,128)S(1)}, f32[2,16,128]{2,1,0:T(8,128)}, u32[]{:S(2)}) copy-start(f32[2,16,128]{2,1,0:T(8,128)} %param.17) | copy-start | bytes 49156
  68.7 13.6 %all-to-all-start.1 = ((bf16[8,2,128,128]{3,2,1,0:T(8,128)(2,1)}), bf16[8,2,128,128]{3,2,1,0:T(8,128)(2,1)S(1)}, u32[]{:S(2)}, u32[]{:S(2)}) async-start(bf16[8,2,128,128]{3,2,1,0:T(8,128)(2,1)} %shard_map.106), calls=%async_computation.1 | async-start | bytes 1048576 | tf_op jit(solution)/shard_map/all_to_all | solution.py:207
